TPU v7x, 8 devices: a whole 2x2x1 slice. The times are simulated.
8 devices in a mesh: dp: 1 (over z), emb: 2 (over y), head: 4 (over x, core).
Axes of the slice: x: 2, y: 2, z: 1, core: 2. Of those that a mesh axis runs over, the one named last changes fastest.
Arguments:
- hidden: bfloat16 [16, 512, 7168], P('dp', None, 'emb')
- g_in: bfloat16 [7168], P('emb')
- w_dq: bfloat16 [7168, 1536], P('emb', 'head')
- g_q: bfloat16 [1536], P('head')
- w_dkv: bfloat16 [7168, 512], P('emb', 'head')
- g_kv: bfloat16 [512], P('head')
- w_kr: bfloat16 [7168, 64], P('emb')
- w_uq: bfloat16 [1536, 64, 192], P(None, 'head')
- w_uk: bfloat16 [512, 64, 128], P(None, 'head')
- w_uv: bfloat16 [512, 64, 128], P(None, 'head')
- w_o: bfloat16 [64, 128, 7168], P('head', None, 'emb')
Outputs:
- output 1: bfloat16 [16, 512, 7168], P('dp', None, 'emb')
- output 2: bfloat16 [16, 512, 512], P('dp', None, 'head')
- output 3: bfloat16 [16, 512, 64], P('dp')
All inputs are finite; a program needn't handle non-finite values.
Results may differ from a plain program's by a relative error of at most 0.0181088.
Values are sent between devices in bfloat16 or wider.
A program may use at most 1 GiB of HBM per device.

v0:
```python
import math
import jax
import jax.numpy as jnp
from jax import lax
from jax.sharding import PartitionSpec as P

ROPE_BASE = 10000.0
NORM_EPS = 1.0e-6
MSCALE = 0.1 * math.log(40.0) + 1.0


def split_norm(latent, gain_vec, full_width, axis_name):
    wide_vals = latent.astype(jnp.float32)
    sq_sum = lax.psum(jnp.sum(wide_vals * wide_vals, axis=-1, keepdims=True), axis_name)
    return (wide_vals * lax.rsqrt(sq_sum / full_width + NORM_EPS) * gain_vec.astype(jnp.float32)).astype(jnp.bfloat16)


def rope_tables(seq_len, rope_dim):
    half_dim = rope_dim // 2
    inv_freq = ROPE_BASE ** (-2.0 * jnp.arange(half_dim, dtype=jnp.float32) / rope_dim)
    angles = jnp.arange(seq_len, dtype=jnp.float32)[:, None] * inv_freq[None, :]
    return jnp.cos(angles), jnp.sin(angles)


def rotate(values, cos_t, sin_t):
    half_dim = values.shape[-1] // 2
    front_half = values[..., :half_dim]
    back_half = values[..., half_dim:]
    return jnp.concatenate([front_half * cos_t - back_half * sin_t, front_half * sin_t + back_half * cos_t], axis=-1)


def causal_attention(q_nope, q_pe, k_nope, k_pe, v_heads, soft_scale):
    seq_len = q_nope.shape[1]
    q_block = min(seq_len, 128)
    key_pos = jnp.arange(seq_len)

    def attend_block(blk_idx):
        q_start = blk_idx * q_block
        qn_blk = lax.dynamic_slice_in_dim(q_nope, q_start, q_block, axis=1)
        qp_blk = lax.dynamic_slice_in_dim(q_pe, q_start, q_block, axis=1)
        scores = jnp.einsum("hqd,hkd->hqk", qn_blk, k_nope, preferred_element_type=jnp.float32)
        scores = scores + jnp.einsum("hqr,kr->hqk", qp_blk, k_pe, preferred_element_type=jnp.float32)
        q_pos = q_start + jnp.arange(q_block)
        allowed = key_pos[None, :] <= q_pos[:, None]
        scores = jnp.where(allowed, scores * soft_scale, -jnp.inf)
        attn_prob = jax.nn.softmax(scores, axis=-1).astype(jnp.bfloat16)
        return jnp.einsum("irl,ilw->irw", attn_prob, v_heads, preferred_element_type=jnp.float32).astype(jnp.bfloat16)

    return lax.map(attend_block, jnp.arange(seq_len // q_block))


def solution(mesh):
    emb_count = mesh.shape["emb"]
    in_specs = (P("dp", None, "emb"), P("emb"), P("emb", "head"), P("head"), P("emb", "head"), P("head"), P("emb", None), P(None, "head", None), P(None, "head", None), P(None, "head", None), P("head", None, "emb"))
    out_specs = (P("dp", None, "emb"), P("dp", None, "head"), P("dp", None, None))

    def local_block(hidden, g_in, w_dq, g_q, w_dkv, g_kv, w_kr, w_uq, w_uk, w_uv, w_o):
        seq_len = hidden.shape[1]
        nope_dim = w_uk.shape[2]
        soft_scale = MSCALE * MSCALE / math.sqrt(w_uq.shape[2])
        h_norm = split_norm(hidden, g_in, hidden.shape[2] * emb_count, "emb")
        cq_part = jnp.einsum("btd,dc->btc", h_norm, w_dq, preferred_element_type=jnp.float32).astype(jnp.bfloat16)
        ckv_part = jnp.einsum("btd,dc->btc", h_norm, w_dkv, preferred_element_type=jnp.float32).astype(jnp.bfloat16)
        kr_part = jnp.einsum("btd,dc->btc", h_norm, w_kr, preferred_element_type=jnp.float32).astype(jnp.bfloat16)
        c_q, c_kv, k_raw = lax.psum((cq_part, ckv_part, kr_part), "emb")
        cq_loc = split_norm(c_q, g_q, w_uq.shape[0], "head")
        ckv_loc = split_norm(c_kv, g_kv, w_uk.shape[0], "head")
        cq_full = lax.all_gather(cq_loc, "head", axis=2, tiled=True)
        ckv_full = lax.all_gather(ckv_loc, "head", axis=2, tiled=True)
        cos_t, sin_t = rope_tables(seq_len, w_kr.shape[1])
        k_pe = rotate(k_raw.astype(jnp.float32), cos_t, sin_t).astype(jnp.bfloat16)
        wq_nope = w_uq[:, :, :nope_dim]
        wq_rope = w_uq[:, :, nope_dim:]

        def one_seq(seq_in):
            cq_s, ckv_s, kpe_s = seq_in
            q_nope = jnp.einsum("tc,chk->htk", cq_s, wq_nope, preferred_element_type=jnp.float32).astype(jnp.bfloat16)
            q_raw = jnp.einsum("tc,chk->htk", cq_s, wq_rope, preferred_element_type=jnp.float32).astype(jnp.bfloat16)
            q_pe = rotate(q_raw.astype(jnp.float32), cos_t, sin_t).astype(jnp.bfloat16)
            k_nope = jnp.einsum("tc,chk->htk", ckv_s, w_uk, preferred_element_type=jnp.float32).astype(jnp.bfloat16)
            v_heads = jnp.einsum("tc,chk->htk", ckv_s, w_uv, preferred_element_type=jnp.float32).astype(jnp.bfloat16)
            ctx_blocks = causal_attention(q_nope, q_pe, k_nope, kpe_s, v_heads, soft_scale)
            attn_part = jnp.einsum("nhqv,hvd->nqd", ctx_blocks, w_o, preferred_element_type=jnp.float32).astype(jnp.bfloat16)
            return attn_part.reshape(seq_len, w_o.shape[2])

        attn_part = lax.map(one_seq, (cq_full, ckv_full, k_pe))
        attn_sum = lax.psum(attn_part, "head")
        result = (hidden.astype(jnp.float32) + attn_sum.astype(jnp.float32)).astype(jnp.bfloat16)
        return result, ckv_loc, k_pe

    return jax.shard_map(local_block, mesh=mesh, in_specs=in_specs, out_specs=out_specs, check_vma=False)
```

profile of v0, /device:TPU:0, one launch (start us, length us, event | category | flops | bytes accessed | tf_op | source)
XLA Modules:
  0.0 3272.5 jit_solution(11070494726012166662)
XLA Ops:
  7.2 19.1 fusion.49
  26.3 10.3 psum.49
  36.8 37.9 %fusion.65 = bf16[16,512,384]{2,1,0:T(8,128)(2,1)} fusion(bf16[16,512,3584]{2,1,0:T(8,128)(2,1)} %param.15, f32[3584]{0:T(1024)S(1)} %convert_element_type.86, f32[16,512]{1,0:T(8,128)S(1)} %rsqrt_bitcast_fusion.2, bf16[3584,384]{1,0:T(8,128)(2,1)S(1)} %copy-done), kind=kOutput, calls=%fused_computation.74 | convolution fusion | flops 22669164544 | bytes 67811328 | tf_op jit(solution)/shard_map/btd,dc->btc/dot_general | solution.py:62
  74.7 24.6 fusion.69
  99.3 25.2 fusion.72
  124.6 214.8 %all-reduce.10.cloned.1.call-done = (bf16[16,512,384]{2,1,0:T(8,128)(2,1)}, bf16[16,512,128]{2,1,0:T(8,128)(2,1)}, bf16[16,512,64]{1,2,0:T(8,128)(2,1)}) async-done(((bf16[16,512,384]{2,1,0:T(8,128)(2,1)}, bf16[16,512,128]{2,1,0:T(8,128)(2,1)}, bf16[16,512,64]{1,2,0:T(8,128)(2,1)}), (bf16[16,512,384]{2,1,0:T(8,128)(2,1)}, bf16[16,512,128]{2,1,0:T(8,128)(2,1)}, ...) | async-done | bytes 9437200 | tf_op jit(solution)/shard_map/psum | solution.py:65
  346.1 26.1 all-reduce.8.cloned.1.call-done
  392.4 9.0 copy.19
  404.6 27.6 all-gather.5.cloned.1.call-done
  432.2 153.9 %all-gather.3.cloned.1.call-done = bf16[16,512,1536]{2,1,0:T(8,128)(2,1)} async-done(((bf16[16,512,384]{2,1,0:T(8,128)(2,1)}), bf16[16,512,1536]{2,1,0:T(8,128)(2,1)}) %all-gather.3.cloned.1.call-update) | async-done | bytes 25165840 | tf_op jit(solution)/shard_map/all_gather | solution.py:68
  586.1 1665.3 %while.28 = (s32[]{:T(128)}, bf16[16,512,3584]{2,1,0:T(8,128)(2,1)}, bf16[16,512,1536]{2,1,0:T(8,128)(2,1)}, bf16[1536,16,128]{2,1,0:T(8,128)(2,1)}, bf16[1536,1...) while((s32[]{:T(128)}, ...), condition=%wide.region_14.15_spmd.clone.clone.clone, body=%wide.region_9.14_spmd.clone.clone.clone.sunk | while | flops 15185562624 | bytes 147149520 | solution.py:86
  607.4 68.8 %while.29 = (s32[]{:T(128)}, bf16[4,16,128,128]{3,2,1,0:T(8,128)(2,1)}, s32[4]{0:T(128)S(1)}, bf16[16,512,128]{2,1,0:T(8,128)(2,1)}, bf16[16,512,128]{2,1,0:T(8,...) while((s32[]{:T(128)}, ...), condition=%wide.region_13.13_spmd.clone, body=%wide.region_10.12_spmd.clone.sunk | while | flops 679808128 | bytes 47662808 | solution.py:49
  676.2 12.1 bitcast_convert_fusion.2
  711.5 68.8 %while.29 = (s32[]{:T(128)}, bf16[4,16,128,128]{3,2,1,0:T(8,128)(2,1)}, s32[4]{0:T(128)S(1)}, bf16[16,512,128]{2,1,0:T(8,128)(2,1)}, bf16[16,512,128]{2,1,0:T(8,...) while((s32[]{:T(128)}, ...), condition=%wide.region_13.13_spmd.clone, body=%wide.region_10.12_spmd.clone.sunk | while | flops 679808128 | bytes 47662808 | solution.py:49
  754.5 8.6 fusion.129
  780.3 12.1 bitcast_convert_fusion.2
  815.5 68.8 %while.29 = (s32[]{:T(128)}, bf16[4,16,128,128]{3,2,1,0:T(8,128)(2,1)}, s32[4]{0:T(128)S(1)}, bf16[16,512,128]{2,1,0:T(8,128)(2,1)}, bf16[16,512,128]{2,1,0:T(8,...) while((s32[]{:T(128)}, ...), condition=%wide.region_13.13_spmd.clone, body=%wide.region_10.12_spmd.clone.sunk | while | flops 679808128 | bytes 47662808 | solution.py:49
  884.3 12.1 bitcast_convert_fusion.2
  919.6 68.8 %while.29 = (s32[]{:T(128)}, bf16[4,16,128,128]{3,2,1,0:T(8,128)(2,1)}, s32[4]{0:T(128)S(1)}, bf16[16,512,128]{2,1,0:T(8,128)(2,1)}, bf16[16,512,128]{2,1,0:T(8,...) while((s32[]{:T(128)}, ...), condition=%wide.region_13.13_spmd.clone, body=%wide.region_10.12_spmd.clone.sunk | while | flops 679808128 | bytes 47662808 | solution.py:49
  962.6 8.6 fusion.129
  988.4 12.1 bitcast_convert_fusion.2
  1023.7 68.8 %while.29 = (s32[]{:T(128)}, bf16[4,16,128,128]{3,2,1,0:T(8,128)(2,1)}, s32[4]{0:T(128)S(1)}, bf16[16,512,128]{2,1,0:T(8,128)(2,1)}, bf16[16,512,128]{2,1,0:T(8,...) while((s32[]{:T(128)}, ...), condition=%wide.region_13.13_spmd.clone, body=%wide.region_10.12_spmd.clone.sunk | while | flops 679808128 | bytes 47662808 | solution.py:49
  1092.5 12.1 bitcast_convert_fusion.2
  1127.8 68.8 %while.29 = (s32[]{:T(128)}, bf16[4,16,128,128]{3,2,1,0:T(8,128)(2,1)}, s32[4]{0:T(128)S(1)}, bf16[16,512,128]{2,1,0:T(8,128)(2,1)}, bf16[16,512,128]{2,1,0:T(8,...) while((s32[]{:T(128)}, ...), condition=%wide.region_13.13_spmd.clone, body=%wide.region_10.12_spmd.clone.sunk | while | flops 679808128 | bytes 47662808 | solution.py:49
  1170.8 8.6 fusion.129
  1196.6 12.1 bitcast_convert_fusion.2
  1231.8 68.8 %while.29 = (s32[]{:T(128)}, bf16[4,16,128,128]{3,2,1,0:T(8,128)(2,1)}, s32[4]{0:T(128)S(1)}, bf16[16,512,128]{2,1,0:T(8,128)(2,1)}, bf16[16,512,128]{2,1,0:T(8,...) while((s32[]{:T(128)}, ...), condition=%wide.region_13.13_spmd.clone, body=%wide.region_10.12_spmd.clone.sunk | while | flops 679808128 | bytes 47662808 | solution.py:49
  1300.6 12.1 bitcast_convert_fusion.2
  1335.9 68.8 %while.29 = (s32[]{:T(128)}, bf16[4,16,128,128]{3,2,1,0:T(8,128)(2,1)}, s32[4]{0:T(128)S(1)}, bf16[16,512,128]{2,1,0:T(8,128)(2,1)}, bf16[16,512,128]{2,1,0:T(8,...) while((s32[]{:T(128)}, ...), condition=%wide.region_13.13_spmd.clone, body=%wide.region_10.12_spmd.clone.sunk | while | flops 679808128 | bytes 47662808 | solution.py:49
  1404.7 12.1 bitcast_convert_fusion.2
  1440.0 68.8 %while.29 = (s32[]{:T(128)}, bf16[4,16,128,128]{3,2,1,0:T(8,128)(2,1)}, s32[4]{0:T(128)S(1)}, bf16[16,512,128]{2,1,0:T(8,128)(2,1)}, bf16[16,512,128]{2,1,0:T(8,...) while((s32[]{:T(128)}, ...), condition=%wide.region_13.13_spmd.clone, body=%wide.region_10.12_spmd.clone.sunk | while | flops 679808128 | bytes 47662808 | solution.py:49
  1508.8 12.1 bitcast_convert_fusion.2
  1544.0 68.8 %while.29 = (s32[]{:T(128)}, bf16[4,16,128,128]{3,2,1,0:T(8,128)(2,1)}, s32[4]{0:T(128)S(1)}, bf16[16,512,128]{2,1,0:T(8,128)(2,1)}, bf16[16,512,128]{2,1,0:T(8,...) while((s32[]{:T(128)}, ...), condition=%wide.region_13.13_spmd.clone, body=%wide.region_10.12_spmd.clone.sunk | while | flops 679808128 | bytes 47662808 | solution.py:49
  1612.8 12.1 bitcast_convert_fusion.2
  1648.1 68.8 %while.29 = (s32[]{:T(128)}, bf16[4,16,128,128]{3,2,1,0:T(8,128)(2,1)}, s32[4]{0:T(128)S(1)}, bf16[16,512,128]{2,1,0:T(8,128)(2,1)}, bf16[16,512,128]{2,1,0:T(8,...) while((s32[]{:T(128)}, ...), condition=%wide.region_13.13_spmd.clone, body=%wide.region_10.12_spmd.clone.sunk | while | flops 679808128 | bytes 47662808 | solution.py:49
  1716.9 12.1 bitcast_convert_fusion.2
  1752.2 68.8 %while.29 = (s32[]{:T(128)}, bf16[4,16,128,128]{3,2,1,0:T(8,128)(2,1)}, s32[4]{0:T(128)S(1)}, bf16[16,512,128]{2,1,0:T(8,128)(2,1)}, bf16[16,512,128]{2,1,0:T(8,...) while((s32[]{:T(128)}, ...), condition=%wide.region_13.13_spmd.clone, body=%wide.region_10.12_spmd.clone.sunk | while | flops 679808128 | bytes 47662808 | solution.py:49
  1821.0 12.1 bitcast_convert_fusion.2
  1856.2 68.8 %while.29 = (s32[]{:T(128)}, bf16[4,16,128,128]{3,2,1,0:T(8,128)(2,1)}, s32[4]{0:T(128)S(1)}, bf16[16,512,128]{2,1,0:T(8,128)(2,1)}, bf16[16,512,128]{2,1,0:T(8,...) while((s32[]{:T(128)}, ...), condition=%wide.region_13.13_spmd.clone, body=%wide.region_10.12_spmd.clone.sunk | while | flops 679808128 | bytes 47662808 | solution.py:49
  1925.0 12.1 bitcast_convert_fusion.2
  1960.3 68.8 %while.29 = (s32[]{:T(128)}, bf16[4,16,128,128]{3,2,1,0:T(8,128)(2,1)}, s32[4]{0:T(128)S(1)}, bf16[16,512,128]{2,1,0:T(8,128)(2,1)}, bf16[16,512,128]{2,1,0:T(8,...) while((s32[]{:T(128)}, ...), condition=%wide.region_13.13_spmd.clone, body=%wide.region_10.12_spmd.clone.sunk | while | flops 679808128 | bytes 47662808 | solution.py:49
  2029.1 12.1 bitcast_convert_fusion.2
  2064.4 68.8 %while.29 = (s32[]{:T(128)}, bf16[4,16,128,128]{3,2,1,0:T(8,128)(2,1)}, s32[4]{0:T(128)S(1)}, bf16[16,512,128]{2,1,0:T(8,128)(2,1)}, bf16[16,512,128]{2,1,0:T(8,...) while((s32[]{:T(128)}, ...), condition=%wide.region_13.13_spmd.clone, body=%wide.region_10.12_spmd.clone.sunk | while | flops 679808128 | bytes 47662808 | solution.py:49
  2133.2 12.1 bitcast_convert_fusion.2
  2168.4 68.8 %while.29 = (s32[]{:T(128)}, bf16[4,16,128,128]{3,2,1,0:T(8,128)(2,1)}, s32[4]{0:T(128)S(1)}, bf16[16,512,128]{2,1,0:T(8,128)(2,1)}, bf16[16,512,128]{2,1,0:T(8,...) while((s32[]{:T(128)}, ...), condition=%wide.region_13.13_spmd.clone, body=%wide.region_10.12_spmd.clone.sunk | while | flops 679808128 | bytes 47662808 | solution.py:49
  2237.2 12.1 bitcast_convert_fusion.2
  2251.4 956.8 %all-reduce.6.cloned.1.call-done = bf16[16,512,3584]{2,1,0:T(8,128)(2,1)} async-done(((bf16[16,512,3584]{2,1,0:T(8,128)(2,1)}), bf16[16,512,3584]{2,1,0:T(8,128)(2,1)}) %all-reduce.6.cloned.1.call-update) | async-done | bytes 58720272 | tf_op jit(solution)/shard_map/psum | solution.py:87
  3208.2 57.3 %fusion.52 = bf16[16,512,3584]{2,1,0:T(8,128)(2,1)} fusion(bf16[16,512,3584]{2,1,0:T(8,128)(2,1)} %param.15, bf16[16,512,3584]{2,1,0:T(8,128)(2,1)} %all-reduce.6.cloned.1.call-done), kind=kLoop, calls=%fused_computation.60 | loop fusion | flops 117440512 | bytes 176160768 | tf_op jit(solution)/shard_map/convert_element_type | solution.py:88
  (953 shorter events, 1432.0 us)
Async XLA Ops:
  7.2 29.6 copy-start
  7.2 29.5 copy-start.5
  7.2 332.2 %all-reduce.10.cloned.1.call-start = ((), (), s32[]{:S(2)}) async-start(), calls=%async_computation.4 | async-start | bytes 18874368 | tf_op jit(solution)/shard_map/psum | solution.py:65
  74.7 24.6 copy-start.9
  124.5 247.7 %all-reduce.8.cloned.1.call-start = ((), (), s32[]{:S(2)}) async-start(), calls=%async_computation.3 | async-start | bytes 131072 | tf_op jit(solution)/shard_map/psum | solution.py:14
  339.4 6.7 copy-start.10
  344.3 31.0 copy-start.6
  346.1 86.2 %all-gather.5.cloned.1.call-start = ((), (), s32[]{:S(2)}) async-start(), calls=%async_computation.1 | async-start | bytes 10485760 | tf_op jit(solution)/shard_map/all_gather | solution.py:69
  375.2 210.9 %all-gather.3.cloned.1.call-start = ((), (), s32[]{:S(2)}) async-start(), calls=%async_computation | async-start | bytes 31457280 | tf_op jit(solution)/shard_map/all_gather | solution.py:68
  382.5 2825.7 %all-reduce.6.cloned.1.call-start = ((), (), s32[]{:S(2)}) async-start(), calls=%async_computation.2 | async-start | bytes 117440512 | tf_op jit(solution)/shard_map/psum | solution.py:87
  590.5 6.4 slice-start
  596.9 7.3 copy-start.7
  694.6 6.4 slice-start
  695.4 5.5 slice-start.1
  701.0 7.3 copy-start.7
  798.6 6.4 slice-start
  805.0 7.3 copy-start.7
  902.7 6.4 slice-start
  909.1 7.3 copy-start.7
  1006.8 6.4 slice-start
  1013.2 7.3 copy-start.7
  1110.9 6.4 slice-start
  1111.7 5.5 slice-start.1
  1117.3 7.3 copy-start.7
  1214.9 6.4 slice-start
  1221.3 7.3 copy-start.7
  1319.0 6.4 slice-start
  1319.9 5.5 slice-start.1
  1325.4 7.3 copy-start.7
  1423.1 6.4 slice-start
  1429.5 7.3 copy-start.7
  1527.1 6.4 slice-start
  1528.0 5.5 slice-start.1
  1533.5 7.3 copy-start.7
  1631.2 6.4 slice-start
  1637.6 7.3 copy-start.7
  1735.3 6.4 slice-start
  1741.7 7.3 copy-start.7
  1839.3 6.4 slice-start
  1845.7 7.3 copy-start.7
  1943.4 6.4 slice-start
  1949.8 7.3 copy-start.7
  2047.5 6.4 slice-start
  2048.3 5.5 slice-start.1
  2053.9 7.3 copy-start.7
  2151.5 6.4 slice-start
  2157.9 7.3 copy-start.7
  3208.2 57.3 %copy-start.1 = (bf16[3584,384]{1,0:T(8,128)(2,1)S(1)}, bf16[3584,384]{1,0:T(8,128)(2,1)}, u32[]{:S(2)}) copy-start(bf16[3584,384]{1,0:T(8,128)(2,1)} %param.17) | copy-start | bytes 8257540
  (93 other events, 228.3 us)
Sparse Core Ops, SparseCore 0:
  124.7 214.6 all-reduce.9
  346.2 25.9 all-reduce.7
  375.3 56.8 all-gather.4
  433.6 152.4 all-gather.2
  2251.6 956.6 all-reduce.5
where the time goes:
time: 3290 us; the launch traced here: 3270 us
  waiting for transfers between devices  1380 us (42%)
  matrix products  1350 us (41%)
  other arithmetic  245 us (7%)
  local copies, waits for them, and re-layouts  233 us (7%)
  loops' own time  43.9 us (1%)
    psum x1, waiting for transfers between devices, local_block(): attn_sum = lax.psum(attn_part, 'head')  957 us
    dot_general x64, matrix products, attend_block(): jnp.einsum('irl,ilw->irw', attn_prob, v_heads, preferred_element_type=jnp...  549 us
    psum x1, waiting for transfers between devices, local_block(): c_q, c_kv, k_raw = lax.psum((cq_part, ckv_part, kr_part), 'emb')  215 us
    dot_general x16, matrix products, one_seq(): jnp.einsum('nhqv,hvd->nqd', ctx_blocks, w_o, preferred_element_type=jnp.f...  194 us
    all_gather x1, waiting for transfers between devices, local_block(): cq_full = lax.all_gather(cq_loc, 'head', axis=2, tiled=True)  154 us
    while x256, local copies, waits for them, and re-layouts  128 us
    dot_general x16, matrix products, one_seq(): jnp.einsum('tc,chk->htk', cq_s, wq_nope, preferred_element_type=jnp.float32)  117 us
    dot_general x64, matrix products, attend_block(): jnp.einsum('hqd,hkd->hqk', qn_blk, k_nope, preferred_element_type=jnp.flo...  113 us
  transfers between devices with their start and end apart: 5, of which 5 were waited for; matrix products, arithmetic and copies ran while one was open for 1% of the time, Pallas kernels for 0%

commit v1 on v0

v1 whole, which is shorter than its diff:
```python
import math
import jax
import jax.numpy as jnp
from jax import lax
from jax.experimental import pallas as pl
from jax.experimental.pallas import tpu as pltpu
from jax.sharding import PartitionSpec as P

ROPE_BASE = 10000.0
NORM_EPS = 1.0e-6
MSCALE = 0.1 * math.log(40.0) + 1.0
BF16 = jnp.bfloat16
F32 = jnp.float32


SIBLING = [(0, 1), (1, 0), (2, 3), (3, 2)]
ACROSS = [(0, 2), (2, 0), (1, 3), (3, 1)]
EMB_SWAP = [(0, 1), (1, 0)]

FIRST = 2
DOWNS = {0: ((2, 2),), 2: ((4, 4),)}
PIECES = {7: ((0, 256), (256, 512))}
ROWS = 256


def after(value, *deps):
    return lax.optimization_barrier((value,) + deps)[0]


def rope_tables(seq_len, rope_dim):
    half_dim = rope_dim // 2
    inv_freq = ROPE_BASE ** (-2.0 * jnp.arange(half_dim, dtype=F32) / rope_dim)
    angles = jnp.arange(seq_len, dtype=F32)[:, None] * inv_freq[None, :]
    cos_t, sin_t = jnp.cos(angles), jnp.sin(angles)
    return jnp.concatenate([cos_t] * 4, axis=1), jnp.concatenate([-sin_t, -sin_t, sin_t, sin_t], axis=1)


def down_kernel(offs_ref, h_ref, rstd_ref, g_ref, *rest):
    pieces, out_ref, w_all = rest[:-2], rest[-2], rest[-1]

    @pl.when(pl.program_id(0) == 0)
    def _():
        for k, ref in enumerate(pieces):
            off = pl.multiple_of(offs_ref[k + 1], 128)
            w_all[:, pl.ds(off, ref.shape[1])] = ref[...]

    hn = (h_ref[0].astype(F32) * rstd_ref[0] * g_ref[...]).astype(BF16)
    out_ref[...] = jnp.dot(hn, w_all[...], preferred_element_type=F32).astype(BF16)


def down(hidden, rstd, g_in, first, n, core_base, pieces, offsets):
    seq, width = hidden.shape[1:]
    tiles = seq // ROWS
    total = sum(p.shape[1] for p in pieces)
    offs = jnp.stack([core_base + first] + [jnp.asarray(o, jnp.int32) for o in offsets]).astype(jnp.int32)
    whole = lambda p: pl.BlockSpec(p.shape, lambda t, o: (0, 0), pipeline_mode=pl.Buffered(1))
    return pl.pallas_call(
        down_kernel,
        grid_spec=pltpu.PrefetchScalarGridSpec(
            num_scalar_prefetch=1,
            grid=(n * tiles,),
            in_specs=[
                pl.BlockSpec((1, ROWS, width), lambda t, o: (o[0] + t // tiles, t % tiles, 0)),
                pl.BlockSpec((1, ROWS, 1), lambda t, o: (first + t // tiles, t % tiles, 0)),
                whole(g_in),
            ] + [whole(p) for p in pieces],
            out_specs=pl.BlockSpec((ROWS, total), lambda t, o: (t, 0)),
            scratch_shapes=[pltpu.VMEM((width, total), BF16)],
        ),
        out_shape=jax.ShapeDtypeStruct((n * seq, total), BF16),
        compiler_params=pltpu.CompilerParams(dimension_semantics=("arbitrary",)),
        cost_estimate=pl.CostEstimate(flops=2 * n * seq * width * total, bytes_accessed=2 * n * seq * width + 2 * width * total, transcendentals=0),
        name="down",
    )(offs, hidden, rstd, g_in, *pieces)


def block_kernel(scale, split, side_ref, *refs):
    n_in = 3 if split else 2
    ins = refs[:n_in]
    gq_ref, gkv_ref, cos_ref, sin_ref, wq_ref, wk_ref, wv_ref, wo_a_ref, wo_b_ref = refs[n_in:n_in + 9]
    part_ref, ckv_ref, kk_ref, cq_ref, kpe_ref, ctx_ref = refs[n_in + 9:]
    step = pl.program_id(0)
    seq, q_lora = cq_ref.shape
    kv_lora = ckv_ref.shape[1]
    heads = wq_ref.shape[0]
    wide = heads * 128
    steps = ctx_ref.shape[1] // wide
    blk = 256

    def norm(vals, gain):
        mean_sq = jnp.mean(vals * vals, axis=-1, keepdims=True)
        return (vals * lax.rsqrt(mean_sq + NORM_EPS) * gain).astype(BF16)

    @pl.when(step == 0)
    def _():
        @pl.loop(0, seq // 128)
        def _(c):
            rows = pl.ds(pl.multiple_of(c * 128, 128), 128)

            def summed(a_ref, b_ref, lo, hi):
                return (a_ref[rows, lo:hi].astype(F32) + b_ref[rows, lo:hi].astype(F32)).astype(BF16).astype(F32)

            if split:
                first = side_ref[0] == 0
                qh, kh = q_lora // 2, kv_lora // 2

                def both(lo, hi):
                    own, far = ins[0][rows, lo:hi].astype(F32), ins[1][rows, lo:hi].astype(F32)
                    return jnp.concatenate([jnp.where(first, own, far), jnp.where(first, far, own)], axis=1)

                cq, ckv, kr = both(0, qh), both(qh, qh + kh), ins[2][rows].astype(F32)
            else:
                cq, ckv = summed(ins[0], ins[1], 0, q_lora), summed(ins[0], ins[1], q_lora, q_lora + kv_lora)
                kr = summed(ins[0], ins[1], q_lora + kv_lora, q_lora + kv_lora + 128)
            cq_ref[rows] = norm(cq, gq_ref[...])
            ckv_ref[rows] = norm(ckv, gkv_ref[...])
            kk = kr * cos_ref[rows] + pltpu.roll(kr, 64, 1) * sin_ref[rows]
            odd = (lax.broadcasted_iota(jnp.int32, kk.shape, 1) // 32) % 2 == 1
            kk_ref[rows] = kk.astype(BF16)
            kpe_ref[0, rows] = jnp.where(odd, 0.0, kk).astype(BF16)
            kpe_ref[1, rows] = jnp.where(odd, kk, 0.0).astype(BF16)

    def nt(a, b):
        return lax.dot_general(a, b, (((1,), (1,)), ((), ())), preferred_element_type=F32)

    @pl.when(step < steps)
    def _():
        cq, ckv = cq_ref[...], ckv_ref[...]
        qn = nt(cq, wq_ref[:, :128].reshape(wide, q_lora)).astype(BF16)
        qps = []
        for pair in range(heads // 2):
            a, b = 2 * pair, 2 * pair + 1
            wr = jnp.concatenate([wq_ref[a, 128:160], wq_ref[b, 128:160], wq_ref[a, 160:192], wq_ref[b, 160:192]], axis=0)
            qr = nt(cq, wr).astype(BF16).astype(F32)
            qps.append((qr * cos_ref[...] + pltpu.roll(qr, 64, 1) * sin_ref[...]).astype(BF16))
        kn = jnp.dot(ckv, wk_ref[...], preferred_element_type=F32).astype(BF16)
        val = jnp.dot(ckv, wv_ref[...], preferred_element_type=F32).astype(BF16)
        row = lax.broadcasted_iota(jnp.int32, (blk, blk), 0)
        col = lax.broadcasted_iota(jnp.int32, (blk, blk), 1)
        allowed = col <= row
        items = [(hh, qb) for hh in range(heads) for qb in range(seq // blk)]

        def score(hh, qb):
            cols, rows, end = slice(hh * 128, hh * 128 + 128), slice(qb * blk, (qb + 1) * blk), (qb + 1) * blk
            key = jnp.concatenate([kn[:end, cols], kpe_ref[hh % 2, :end]], axis=1)
            q = jnp.concatenate([qn[rows, cols], qps[hh // 2][rows]], axis=1)
            s = nt(q, key)
            diag = jnp.where(allowed, s[:, end - blk:], -jnp.inf)
            return diag if qb == 0 else jnp.concatenate([s[:, :end - blk], diag], axis=1)

        def softmax(s):
            top = jnp.max(s, axis=1, keepdims=True)
            e = jnp.exp2((s - top) * (scale * math.log2(math.e)))
            return (e * (1.0 / jnp.sum(e, axis=1, keepdims=True))).astype(BF16)

        scores = [score(*it) for it in items]
        probs = [softmax(s) for s in scores]
        for p, (hh, qb) in zip(probs, items):
            rows, end = slice(qb * blk, (qb + 1) * blk), (qb + 1) * blk
            o = jnp.dot(p, val[:end, hh * 128:hh * 128 + 128], preferred_element_type=F32).astype(BF16)
            ctx_ref[rows, pl.ds(pl.multiple_of(step * wide + hh * 128, 128), 128)] = o

    @pl.when(step >= steps)
    def _():
        depth = wo_a_ref.shape[0]
        out = jnp.dot(ctx_ref[:, :depth], wo_a_ref[...], preferred_element_type=F32)
        out += jnp.dot(ctx_ref[:, depth:], wo_b_ref[...], preferred_element_type=F32)
        part_ref[...] = out.astype(BF16)


def head_block(ins, at, side, gq, gkv, cos_p, sin_p, wq, wkv, wo_a, wo_b, scale):
    seq = cos_p.shape[0]
    n_heads, qk, q_lora = wq.shape
    kv_lora, depth, width = wkv.shape[0], wo_a.shape[0], wo_a.shape[1]
    heads, wide = 4, 512
    steps, out_steps = n_heads // heads, width // wide
    once = pl.Buffered(1)
    hd = lambda j: jnp.minimum(j, steps - 1)
    oc = lambda j: jnp.maximum(j - steps, 0)
    const = lambda shape: pl.BlockSpec(shape, lambda j, o: (0,) * len(shape), pipeline_mode=once)
    return pl.pallas_call(
        lambda *refs: block_kernel(scale, len(ins) == 3, *refs),
        grid_spec=pltpu.PrefetchScalarGridSpec(
            num_scalar_prefetch=1,
            grid=(steps + out_steps,),
            in_specs=[pl.BlockSpec((seq, a.shape[1]), lambda j, o, r=r: (r, 0), pipeline_mode=once) for a, r in zip(ins, at)] + [
                const((1, q_lora)), const((1, kv_lora)), const((seq, 128)), const((seq, 128)),
                pl.BlockSpec((heads, qk, q_lora), lambda j, o: (hd(j), 0, 0)),
                pl.BlockSpec((kv_lora, wide), lambda j, o: (0, hd(j))),
                pl.BlockSpec((kv_lora, wide), lambda j, o: (0, steps + hd(j))),
                pl.BlockSpec((depth, wide), lambda j, o: (0, oc(j))),
                pl.BlockSpec((depth, wide), lambda j, o: (0, oc(j))),
            ],
            out_specs=[
                pl.BlockSpec((seq, wide), lambda j, o: (0, oc(j))),
                pl.BlockSpec((seq, kv_lora), lambda j, o: (0, 0)),
                pl.BlockSpec((seq, 128), lambda j, o: (0, 0)),
            ],
            scratch_shapes=[pltpu.VMEM((seq, q_lora), BF16), pltpu.VMEM((2, seq, 128), BF16), pltpu.VMEM((seq, n_heads * 128), BF16)],
        ),
        out_shape=[jax.ShapeDtypeStruct((seq, width), BF16), jax.ShapeDtypeStruct((seq, kv_lora), BF16), jax.ShapeDtypeStruct((seq, 128), BF16)],
        compiler_params=pltpu.CompilerParams(dimension_semantics=("arbitrary",), vmem_limit_bytes=60 * 2**20),
        cost_estimate=pl.CostEstimate(flops=45 * 10**9, bytes_accessed=64 * 10**6, transcendentals=n_heads * seq * seq),
        name="block",
    )(side, *ins, gq, gkv, cos_p, sin_p, wq, wkv, wkv, wo_a, wo_b)


def blank(shape, dtype):
    return pl.pallas_call(lambda o_ref: None, out_shape=jax.ShapeDtypeStruct(shape, dtype), out_specs=pl.BlockSpec(memory_space=pl.ANY), name="blank")()


def solution(mesh):
    emb_count = mesh.shape["emb"]
    in_specs = (P("dp", None, "emb"), P("emb"), P("emb", "head"), P("head"), P("emb", "head"), P("head"), P("emb", None), P(None, "head", None), P(None, "head", None), P(None, "head", None), P("head", None, "emb"))
    out_specs = (P("dp", None, "emb"), P("dp", None, "head"), P("dp", None, None))

    def swap(v):
        return lax.ppermute(v, "head", SIBLING)

    def cross(v):
        return lax.ppermute(v, "head", ACROSS)

    def emb_swap(v):
        return lax.ppermute(v, "emb", EMB_SWAP)

    def block(hidden, g_in, w_dq, g_q, w_dkv, g_kv, w_kr, w_uq, w_uk, w_uv, w_o):
        n_seq, seq, width = hidden.shape
        half = n_seq // 2
        own_heads = w_uk.shape[1]
        q_lora, kv_lora = w_uq.shape[0], w_uk.shape[0]
        q_blk, kv_blk = w_dq.shape[1], w_dkv.shape[1]
        rope = w_kr.shape[1]
        hr = rope // 2
        scale = MSCALE * MSCALE / math.sqrt(w_uq.shape[2])
        pos = lax.axis_index("head")
        core = lax.rem(pos, 2)
        side = lax.div(pos, 2)
        base = core * half

        far_q = cross(w_dq)
        near_q, near_kv = swap(w_dq), swap(w_dkv)
        sib_uq, sib_uk, sib_uv = swap(w_uq), swap(w_uk), swap(w_uv)
        sib_o = swap(w_o)

        cos_p, sin_p = rope_tables(seq, rope)
        w_kr2 = jnp.concatenate([w_kr[:, :hr], w_kr[:, :hr], w_kr[:, hr:], w_kr[:, hr:]], axis=1)
        gain = jnp.concatenate([g_q, g_kv])[None]
        far_gain = cross(gain)
        g_row = g_in.astype(F32)[None]

        h_wide = lax.dynamic_slice_in_dim(hidden, base, half, 0).astype(F32)
        sq = jnp.sum(h_wide * h_wide, axis=-1)
        sq = sq + emb_swap(sq)
        rstd = lax.rsqrt(sq / (width * emb_count) + NORM_EPS)[:, :, None]

        qh, kh = 2 * q_blk, 2 * kv_blk
        near_offs = [core * q_blk, (1 - core) * q_blk, qh + core * kv_blk, qh + (1 - core) * kv_blk]
        low_own = down(hidden, rstd, g_row, 0, FIRST, base, [w_dq, near_q, w_dkv, near_kv, w_kr2], near_offs + [qh + kh])

        def rows_of(low, r):
            return low[r * seq:(r + 1) * seq]

        own_in = [emb_swap(rows_of(low_own, r)) for r in range(FIRST)]

        w_uq, sib_uq = after((w_uq, sib_uq), low_own)
        flat = lambda w: w.reshape(kv_lora, own_heads * 128)
        wq_all = jnp.concatenate([w_uq.transpose(1, 2, 0), sib_uq.transpose(1, 2, 0)], axis=0)
        wkv_all = jnp.concatenate([flat(w_uk), flat(sib_uk), flat(w_uv), flat(sib_uv)], axis=1)
        wo_own, wo_sib = w_o.reshape(own_heads * 128, width), sib_o.reshape(own_heads * 128, width)

        lows = {}
        for r in range(FIRST):
            arrived_r = own_in[r] if r == 0 else after(own_in[r], lat)
            lat = (rows_of(low_own, r).astype(F32) + arrived_r.astype(F32)).astype(BF16)
            far_lat = cross(lat[:, :qh + kh])
            lows[r] = ((lat[:, :qh + kh], far_lat, lat[:, qh + kh:]), (0, 0, 0))
        far_kv = cross(after(w_dkv, lat))

        far_gain, far_q = after((far_gain, far_q), wq_all, wkv_all)
        gains = jnp.concatenate([gain, swap(gain), far_gain, swap(far_gain)], axis=0).astype(F32)
        gains = jnp.concatenate([lax.dynamic_slice_in_dim(gains, lax.bitwise_xor(pos, r), 1, 0) for r in range(4)], axis=0)
        gq_all = gains[:, :q_blk].reshape(1, q_lora)
        gkv_all = gains[:, q_blk:].reshape(1, kv_lora)
        diag_q = swap(far_q)
        every_offs = [lax.bitwise_xor(pos, r) * q_blk for r in range(4)] + [q_lora + lax.bitwise_xor(pos, r) * kv_blk for r in range(4)] + [q_lora + kv_lora]

        side_flag = side.astype(jnp.int32)[None]
        parts, arrived, ckvs, kks = [], {}, [], []
        last = wq_all
        result = blank(hidden.shape, BF16)

        def finish(i, lo, hi, dep):
            at = after(base, *dep)
            h_i = lax.dynamic_slice(hidden, (at + i, 0 * at + lo, 0 * at), (1, hi - lo, width)).astype(F32)
            total = parts[i][lo:hi].astype(F32) + arrived[i, lo].astype(F32)
            return (h_i + total[None]).astype(BF16)

        for i in range(half):
            gq_i = after(gq_all, last)
            ins, at = lows[i]
            part, ckv, kk = head_block(ins, at, side_flag, gq_i, gkv_all, cos_p, sin_p, wq_all, wkv_all, wo_own, wo_sib, scale)
            ckvs.append(ckv)
            kks.append(kk)
            parts.append(part)
            for lo, hi in PIECES.get(i, ((0, seq),)):
                arrived[i, lo] = cross(part[lo:hi])
            last = part
            if i == 0:
                far_kv = after(far_kv, part)
                diag_kv = swap(far_kv)
                every = [w_dq, near_q, far_q, diag_q, w_dkv, near_kv, far_kv, diag_kv, w_kr2]
            for first, n in DOWNS.get(i, ()):
                low = down(hidden, after(rstd, last), g_row, first, n, base, every, every_offs)
                last = low
                for r in range(n):
                    lows[first + r] = ((low, emb_swap(rows_of(low, r))), (r, 0))

        def spread(own, other):
            full = blank((n_seq,) + own.shape[1:], own.dtype)
            full = lax.dynamic_update_slice_in_dim(full, own, base, 0)
            return lax.dynamic_update_slice_in_dim(full, other, half - base, 0)

        ckv_own = jnp.concatenate(ckvs, axis=0).reshape(half, seq, kv_lora)
        kk = jnp.concatenate(kks, axis=0)
        kk = jnp.concatenate([kk[:, :hr], kk[:, 2 * hr:3 * hr]], axis=1).reshape(half, seq, rope)
        mine = lax.dynamic_slice_in_dim(ckv_own, pos * kv_blk, kv_blk, 2)
        theirs = lax.dynamic_slice_in_dim(ckv_own, lax.bitwise_xor(pos, 1) * kv_blk, kv_blk, 2)
        ckv_out, kpe_out = spread(mine, swap(theirs)), spread(kk, swap(kk))

        waiting = []

        def place(result):
            i, lo, other = waiting.pop(0)
            return lax.dynamic_update_slice(result, other, (half - base + i, 0 * base + lo, 0 * base))

        for i in range(half):
            for lo, hi in PIECES.get(i, ((0, seq),)):
                out_i = finish(i, lo, hi, (last,))
                waiting.append((i, lo, swap(out_i)))
                result = lax.dynamic_update_slice(result, out_i, (base + i, 0 * base + lo, 0 * base))
                if len(waiting) > 1:
                    result = place(result)
        result = place(result)
        return result, ckv_out, kpe_out

    return jax.shard_map(block, mesh=mesh, in_specs=in_specs, out_specs=out_specs, check_vma=False)
```

time: 3290 us -> 1210 us (0.37)
  matrix products: 1350 us -> 0 us
  waiting for transfers between devices: 1380 us -> 450 us
  Pallas kernels: 0 us -> 519 us
  other arithmetic: 245 us -> 102 us
  local copies, waits for them, and re-layouts: 233 us -> 96.3 us
  loops' own time: 43.9 us -> 0 us
    dot_general x259 -> x0, matrix products: 1280 us -> none  [the longest x64 549 us: attend_block(): jnp.einsum('irl,ilw->irw', attn_prob, v_heads, preferred_element_type=jnp...]
    psum x3 -> x0, waiting for transfers between devices: 1200 us -> none  [the longest x1 957 us: local_block(): attn_sum = lax.psum(attn_part, 'head')]
    pallas_call x0 -> x14, Pallas kernels: none -> 519 us  [the longest x8 428 us: head_block(): pl.pallas_call(lambda *refs: block_kernel(scale, len(ins) == 3, *refs), g...]
    ppermute x0 -> x44, waiting for transfers between devices: none -> 450 us  [the longest x14 392 us: cross(): return lax.ppermute(v, 'head', ACROSS)]
    all_gather x2 -> x0, waiting for transfers between devices: 182 us -> none  [the longest x1 154 us: local_block(): cq_full = lax.all_gather(cq_loc, 'head', axis=2, tiled=True)]
    while x256 -> x0, local copies, waits for them, and re-layouts: 128 us -> none
    sub x64 -> x0, other arithmetic: 111 us -> none  [attend_block(): attn_prob = jax.nn.softmax(scores, axis=-1).astype(jnp.bfloat16)]
    convert_element_type x23 -> x3, other arithmetic: 71 us -> 0.63 us  [the longest x2 0.61 us: block(): lat = (rows_of(low_own, r).astype(F32) + arrived_r.astype(F32)).astype(BF16)]
  transfers between devices with their start and end apart: 5 -> 44, of which waited for: 5 -> 12; matrix products, arithmetic and copies ran while one was open for 1% -> 16% of each run, Pallas kernels for 0% -> 43%
where the time goes in v1:
time: 1210 us; the launch traced here: 1200 us
  Pallas kernels  519 us (43%)
  waiting for transfers between devices  450 us (37%)
  other arithmetic  102 us (8%)
  local copies, waits for them, and re-layouts  96.3 us (8%)
  starting transfers between devices  28.6 us (2%)
    pallas_call x8, Pallas kernels, head_block(): pl.pallas_call(lambda *refs: block_kernel(scale, len(ins) == 3, *refs), g...  428 us
    ppermute x14, waiting for transfers between devices, cross(): return lax.ppermute(v, 'head', ACROSS)  392 us
    pallas_call x3, Pallas kernels, down(): pl.pallas_call(down_kernel, grid_spec=pltpu.PrefetchScalarGridSpec(num_sc...  90.9 us
    dynamic_update_slice x9, other arithmetic, block(): lax.dynamic_update_slice(result, out_i, (base + i, 0 * base + lo, 0 * base))  67.2 us
    ppermute x9, waiting for transfers between devices, emb_swap(): return lax.ppermute(v, 'emb', EMB_SWAP)  41.8 us
    dynamic_update_slice x9, local copies, waits for them, and re-layouts, place(): lax.dynamic_update_slice(result, other, (half - base + i, 0 * base + lo,...  35.7 us
  transfers between devices with their start and end apart: 44, of which 12 were waited for; matrix products, arithmetic and copies ran while one was open for 16% of the time, Pallas kernels for 43%

profile of v1, /device:TPU:0, one launch (start us, length us, event | category | flops | bytes accessed | tf_op | source)
XLA Modules:
  0.0 1197.2 jit_solution(4967265883771854595)
XLA Ops:
  1.5 10.5 multiply_reduce_fusion
  12.0 3.0 collective-permute-start
  16.0 3.5 bitcast_dynamic-update-slice_fusion.3
  24.5 3.2 pad_maximum_fusion.2.rest_4_.rest_8_
  27.8 14.5 %collective-permute-done.2.rest_3_.rest_5_ = bf16[3584,128]{1,0:T(8,128)(2,1)S(1)} collective-permute-done((bf16[3584,128]{1,0:T(8,128)(2,1)S(1)}, bf16[3584,128]{1,0:T(8,128)(2,1)S(1)}, u32[]{:S(2)}, u32[]{:S(2)}) %collective-permute-start.2) | collective-permute-done | bytes 917536 | tf_op jit(solution)/shard_map/ppermute | solution.py:218
  47.2 16.9 %down.3 = bf16[1024,1152]{1,0:T(8,128)(2,1)} custom-call(s32[6]{0:T(128)} %stack.79.offs_ref, bf16[16,512,3584]{2,1,0:T(8,128)(2,1)} %h_ref.5, f32[8,512,1]{2,1,0:T(8,128)} %copy.28.rstd_ref, f32[1,3584]{1,0:T(1,128)} %reshape.51.g_ref, bf16[3584,384]{1,0:T(8,128)(2,1)} %rest_0_.5, bf16[3584,384]{1,0:T(8,128)(2,1)} %collective-permute-done.1.rest_1_, ...), custom_call_target="tpu_custom_call" | custom-call | flops 8455716864 | bytes 15597568 | tf_op jit(solution)/shard_map/down/pallas_call | solution.py:57
  67.5 3.4 bitcast_dynamic-update-slice_fusion.2
  71.4 3.6 bitcast_dynamic-update-slice_fusion.1
  76.9 17.9 %collective-permute-done.3 = bf16[512,1152]{1,0:T(8,128)(2,1)S(1)} collective-permute-done((bf16[512,1152]{1,0:T(8,128)(2,1)S(1)}, bf16[512,1152]{1,0:T(8,128)(2,1)S(1)}, u32[]{:S(2)}, u32[]{:S(2)}) %collective-permute-start.3) | collective-permute-done | bytes 1179680 | tf_op jit(solution)/shard_map/ppermute | solution.py:224
  95.3 23.9 %collective-permute-done.14 = bf16[512,1152]{1,0:T(8,128)(2,1)S(1)} collective-permute-done((bf16[512,1152]{1,0:T(8,128)(2,1)S(1)}, bf16[512,1152]{1,0:T(8,128)(2,1)S(1)}, u32[]{:S(2)}, u32[]{:S(2)}) %collective-permute-start.14) | collective-permute-done | bytes 1179680 | tf_op jit(solution)/shard_map/ppermute | solution.py:224
  119.5 16.6 %pad_maximum_fusion.refs_8_.refs_7_ = bf16[32,192,1536]{2,1,0:T(8,128)(2,1)} fusion(bf16[16,192,1536]{2,1,0:T(8,128)(2,1)} %bitcast.18, bf16[16,192,1536]{2,1,0:T(8,128)(2,1)} %bitcast.88), kind=kLoop, calls=%fused_computation.1 | loop fusion | flops 9437184 | bytes 37748736 | tf_op jit(solution)/shard_map/concatenate | solution.py:267
  140.4 4.9 collective-permute-done.4.refs_2_
  146.2 53.0 %block.8 = (bf16[512,3584]{1,0:T(8,128)(2,1)}, bf16[512,512]{1,0:T(8,128)(2,1)}, bf16[512,128]{1,0:T(8,128)(2,1)}) custom-call(s32[1]{0:T(128)} %bitcast.refs_0_, bf16[512,1024]{1,0:T(8,128)(2,1)} %copy-done.10, bf16[512,1024]{1,0:T(8,128)(2,1)} %copy-done.30, bf16[512,128]{1,0:T(8,128)(2,1)} %slice.93.refs_3_, f32[1,1536]{1,0:T(1,128)} %bitcast.91, ...), custom_call_target="tpu_custom_call" | custom-call | flops 44999999488 | bytes 64000000 | tf_op jit(solution)/shard_map/block/pallas_call | solution.py:181
  205.4 27.7 %down.4.refs_1_ = bf16[1024,2176]{1,0:T(8,128)(2,1)} custom-call(s32[10]{0:T(128)} %stack.73.offs_ref, bf16[16,512,3584]{2,1,0:T(8,128)(2,1)} %h_ref.5, f32[8,512,1]{2,1,0:T(8,128)} %copy.29.rstd_ref, f32[1,3584]{1,0:T(1,128)} %reshape.51.g_ref, bf16[3584,384]{1,0:T(8,128)(2,1)} %rest_0_.5, bf16[3584,384]{1,0:T(8,128)(2,1)} %collective-permute-done.1.rest_1_, ...), custom_call_target="tpu_custom_call" | custom-call | flops 15971909632 | bytes 22937600 | tf_op jit(solution)/shard_map/down/pallas_call | solution.py:57
  233.1 4.0 fusion.22
  238.6 53.0 %block.9 = (bf16[512,3584]{1,0:T(8,128)(2,1)}, bf16[512,512]{1,0:T(8,128)(2,1)}, bf16[512,128]{1,0:T(8,128)(2,1)}) custom-call(s32[1]{0:T(128)} %bitcast.refs_0_, bf16[512,1024]{1,0:T(8,128)(2,1)} %copy-done.11, bf16[512,1024]{1,0:T(8,128)(2,1)} %collective-permute-done.18.refs_2_, bf16[512,128]{1,0:T(8,128)(2,1)} %slice.98.refs_3_, f32[1,1536]{1,0:T(1,128)} %bitcast.92, ...), custom_call_target="tpu_custom_call" | custom-call | flops 44999999488 | bytes 64000000 | tf_op jit(solution)/shard_map/block/pallas_call | solution.py:181
  292.5 53.7 %block.10 = (bf16[512,3584]{1,0:T(8,128)(2,1)}, bf16[512,512]{1,0:T(8,128)(2,1)}, bf16[512,128]{1,0:T(8,128)(2,1)}) custom-call(s32[1]{0:T(128)} %bitcast.refs_0_, bf16[1024,2176]{1,0:T(8,128)(2,1)} %down.4.refs_1_, bf16[512,2176]{1,0:T(8,128)(2,1)} %collective-permute-done.17.refs_2_, f32[1,1536]{1,0:T(1,128)} %bitcast.93, f32[1,512]{1,0:T(1,128)} %bitcast.101, ...), custom_call_target="tpu_custom_call" | custom-call | flops 44999999488 | bytes 64000000 | tf_op jit(solution)/shard_map/block/pallas_call | solution.py:181
  348.1 46.3 %down.5.refs_1_ = bf16[2048,2176]{1,0:T(8,128)(2,1)} custom-call(s32[10]{0:T(128)} %stack.71.offs_ref, bf16[16,512,3584]{2,1,0:T(8,128)(2,1)} %h_ref.5, f32[8,512,1]{2,1,0:T(8,128)} %copy.30.rstd_ref, f32[1,3584]{1,0:T(1,128)} %reshape.51.g_ref, bf16[3584,384]{1,0:T(8,128)(2,1)} %rest_0_.5, bf16[3584,384]{1,0:T(8,128)(2,1)} %collective-permute-done.1.rest_1_, ...), custom_call_target="tpu_custom_call" | custom-call | flops 31943819264 | bytes 30277632 | tf_op jit(solution)/shard_map/down/pallas_call | solution.py:57
  394.4 6.1 fusion.21
  402.3 53.6 %block.11 = (bf16[512,3584]{1,0:T(8,128)(2,1)}, bf16[512,512]{1,0:T(8,128)(2,1)}, bf16[512,128]{1,0:T(8,128)(2,1)}) custom-call(s32[1]{0:T(128)} %bitcast.refs_0_, bf16[1024,2176]{1,0:T(8,128)(2,1)} %down.4.refs_1_, bf16[512,2176]{1,0:T(8,128)(2,1)} %collective-permute-done.23.refs_2_, f32[1,1536]{1,0:T(1,128)} %bitcast.94, f32[1,512]{1,0:T(1,128)} %bitcast.102, ...), custom_call_target="tpu_custom_call" | custom-call | flops 44999999488 | bytes 64000000 | tf_op jit(solution)/shard_map/block/pallas_call | solution.py:181
  458.2 53.8 %block.12 = (bf16[512,3584]{1,0:T(8,128)(2,1)}, bf16[512,512]{1,0:T(8,128)(2,1)}, bf16[512,128]{1,0:T(8,128)(2,1)}) custom-call(s32[1]{0:T(128)} %bitcast.refs_0_, bf16[2048,2176]{1,0:T(8,128)(2,1)} %down.5.refs_1_, bf16[512,2176]{1,0:T(8,128)(2,1)} %collective-permute-done.22.refs_2_, f32[1,1536]{1,0:T(1,128)} %bitcast.95, f32[1,512]{1,0:T(1,128)} %bitcast.103, ...), custom_call_target="tpu_custom_call" | custom-call | flops 44999999488 | bytes 64000000 | tf_op jit(solution)/shard_map/block/pallas_call | solution.py:181
  512.0 53.6 %block.13 = (bf16[512,3584]{1,0:T(8,128)(2,1)}, bf16[512,512]{1,0:T(8,128)(2,1)}, bf16[512,128]{1,0:T(8,128)(2,1)}) custom-call(s32[1]{0:T(128)} %bitcast.refs_0_, bf16[2048,2176]{1,0:T(8,128)(2,1)} %down.5.refs_1_, bf16[512,2176]{1,0:T(8,128)(2,1)} %collective-permute-done.21.refs_2_, f32[1,1536]{1,0:T(1,128)} %bitcast.96, f32[1,512]{1,0:T(1,128)} %bitcast.104, ...), custom_call_target="tpu_custom_call" | custom-call | flops 44999999488 | bytes 64000000 | tf_op jit(solution)/shard_map/block/pallas_call | solution.py:181
  565.6 53.8 %block.14 = (bf16[512,3584]{1,0:T(8,128)(2,1)}, bf16[512,512]{1,0:T(8,128)(2,1)}, bf16[512,128]{1,0:T(8,128)(2,1)}) custom-call(s32[1]{0:T(128)} %bitcast.refs_0_, bf16[2048,2176]{1,0:T(8,128)(2,1)} %down.5.refs_1_, bf16[512,2176]{1,0:T(8,128)(2,1)} %collective-permute-done.20.refs_2_, f32[1,1536]{1,0:T(1,128)} %bitcast.97, f32[1,512]{1,0:T(1,128)} %bitcast.105, ...), custom_call_target="tpu_custom_call" | custom-call | flops 44999999488 | bytes 64000000 | tf_op jit(solution)/shard_map/block/pallas_call | solution.py:181
  619.5 53.9 %block.15 = (bf16[512,3584]{1,0:T(8,128)(2,1)}, bf16[512,512]{1,0:T(8,128)(2,1)}, bf16[512,128]{1,0:T(8,128)(2,1)}) custom-call(s32[1]{0:T(128)} %bitcast.refs_0_, bf16[2048,2176]{1,0:T(8,128)(2,1)} %down.5.refs_1_, bf16[512,2176]{1,0:T(8,128)(2,1)} %collective-permute-done.19.refs_2_, f32[1,1536]{1,0:T(1,128)} %bitcast.98, f32[1,512]{1,0:T(1,128)} %bitcast.106, ...), custom_call_target="tpu_custom_call" | custom-call | flops 44999999488 | bytes 64000000 | tf_op jit(solution)/shard_map/block/pallas_call | solution.py:181
  673.3 8.6 constant_dynamic-update-slice_fusion.36
  684.0 8.6 constant_dynamic-update-slice_fusion.35
  692.7 4.1 constant_dynamic-update-slice_fusion.34
  696.8 67.7 %collective-permute-done.27 = bf16[512,3584]{1,0:T(8,128)(2,1)} collective-permute-done((bf16[512,3584]{1,0:T(8,128)(2,1)}, bf16[512,3584]{1,0:T(8,128)(2,1)}, u32[]{:S(2)}, u32[]{:S(2)}) %collective-permute-start.27) | collective-permute-done | bytes 3670048 | tf_op jit(solution)/shard_map/ppermute | solution.py:221
  764.5 8.6 constant_dynamic-update-slice_fusion.33
  775.2 4.3 constant_dynamic-update-slice_fusion.32
  779.5 63.7 %collective-permute-done.29 = bf16[512,3584]{1,0:T(8,128)(2,1)} collective-permute-done((bf16[512,3584]{1,0:T(8,128)(2,1)}, bf16[512,3584]{1,0:T(8,128)(2,1)}, u32[]{:S(2)}, u32[]{:S(2)}) %collective-permute-start.29) | collective-permute-done | bytes 3670048 | tf_op jit(solution)/shard_map/ppermute | solution.py:221
  843.2 7.6 constant_dynamic-update-slice_fusion.31
  850.8 4.1 constant_dynamic-update-slice_fusion.30
  854.9 66.9 %collective-permute-done.31 = bf16[512,3584]{1,0:T(8,128)(2,1)} collective-permute-done((bf16[512,3584]{1,0:T(8,128)(2,1)}, bf16[512,3584]{1,0:T(8,128)(2,1)}, u32[]{:S(2)}, u32[]{:S(2)}) %collective-permute-start.31) | collective-permute-done | bytes 3670048 | tf_op jit(solution)/shard_map/ppermute | solution.py:221
  921.8 8.6 constant_dynamic-update-slice_fusion.29
  936.6 4.3 constant_dynamic-update-slice_fusion.28
  940.8 59.6 %collective-permute-done.33 = bf16[512,3584]{1,0:T(8,128)(2,1)} collective-permute-done((bf16[512,3584]{1,0:T(8,128)(2,1)}, bf16[512,3584]{1,0:T(8,128)(2,1)}, u32[]{:S(2)}, u32[]{:S(2)}) %collective-permute-start.33) | collective-permute-done | bytes 3670048 | tf_op jit(solution)/shard_map/ppermute | solution.py:221
  1000.5 7.6 constant_dynamic-update-slice_fusion.27
  1008.1 4.1 constant_dynamic-update-slice_fusion.26
  1012.2 66.5 %collective-permute-done.35 = bf16[512,3584]{1,0:T(8,128)(2,1)} collective-permute-done((bf16[512,3584]{1,0:T(8,128)(2,1)}, bf16[512,3584]{1,0:T(8,128)(2,1)}, u32[]{:S(2)}, u32[]{:S(2)}) %collective-permute-start.35) | collective-permute-done | bytes 3670048 | tf_op jit(solution)/shard_map/ppermute | solution.py:221
  1078.6 9.0 constant_dynamic-update-slice_fusion.25
  1096.8 4.3 constant_dynamic-update-slice_fusion.24
  1101.1 31.8 %collective-permute-done.37 = bf16[256,3584]{1,0:T(8,128)(2,1)S(1)} collective-permute-done((bf16[256,3584]{1,0:T(8,128)(2,1)}, bf16[256,3584]{1,0:T(8,128)(2,1)S(1)}, u32[]{:S(2)}, u32[]{:S(2)}) %collective-permute-start.37) | collective-permute-done | bytes 1835040 | tf_op jit(solution)/shard_map/ppermute | solution.py:221
  1132.9 4.0 constant_dynamic-update-slice_fusion.23
  1136.9 4.1 constant_dynamic-update-slice_fusion.22
  1141.0 30.8 %collective-permute-done.39 = bf16[256,3584]{1,0:T(8,128)(2,1)} collective-permute-done((bf16[256,3584]{1,0:T(8,128)(2,1)}, bf16[256,3584]{1,0:T(8,128)(2,1)}, u32[]{:S(2)}, u32[]{:S(2)}) %collective-permute-start.39) | collective-permute-done | bytes 1835040 | tf_op jit(solution)/shard_map/ppermute | solution.py:221
  1171.9 4.5 constant_dynamic-update-slice_fusion.21
  1190.3 3.6 constant_dynamic-update-slice_fusion.20
  (197 shorter events, 73.9 us)
Async XLA Ops:
  0.6 145.6 %collective-permute-start.12 = (bf16[16,128,3584]{2,1,0:T(8,128)(2,1)}, bf16[16,128,3584]{2,1,0:T(8,128)(2,1)}, u32[]{:S(2)}, u32[]{:S(2)}) collective-permute-start(bf16[16,128,3584]{2,1,0:T(8,128)(2,1)} %param.21), channel_id=1, source_target_pairs={{0,1},{1,0},{2,3},{3,2},{4,5},{5,4},{6,7},{7,6}} | collective-permute-start | bytes 44040200 | tf_op jit(solution)/shard_map/ppermute | solution.py:218
  1.5 117.7 %collective-permute-start.8 = (bf16[1536,16,192]{0,2,1:T(8,128)(2,1)}, bf16[1536,16,192]{0,2,1:T(8,128)(2,1)}, u32[]{:S(2)}, u32[]{:S(2)}) collective-permute-start(bf16[1536,16,192]{0,2,1:T(8,128)(2,1)} %param.18), channel_id=1, source_target_pairs={{0,1},{1,0},{2,3},{3,2},{4,5},{5,4},{6,7},{7,6}} | collective-permute-start | bytes 28311560 | tf_op jit(solution)/shard_map/ppermute | solution.py:218
  12.0 12.5 %collective-permute-start = (f32[8,512]{1,0:T(8,128)S(1)}, f32[8,512]{1,0:T(8,128)S(1)}, u32[]{:S(2)}, u32[]{:S(2)}) collective-permute-start(f32[8,512]{1,0:T(8,128)S(1)} %multiply_reduce_fusion), channel_id=1, source_target_pairs={{0,4},{4,0},{1,5},{5,1},{2,6},{6,2},{3,7},{7,3}} | collective-permute-start | bytes 49160 | tf_op jit(solution)/shard_map/ppermute | solution.py:224
  15.0 29.6 %collective-permute-start.1 = (bf16[3584,384]{1,0:T(8,128)(2,1)}, bf16[3584,384]{1,0:T(8,128)(2,1)}, u32[]{:S(2)}, u32[]{:S(2)}) collective-permute-start(bf16[3584,384]{1,0:T(8,128)(2,1)} %rest_0_.5), channel_id=1, source_target_pairs={{0,1},{1,0},{2,3},{3,2},{4,5},{5,4},{6,7},{7,6}} | collective-permute-start | bytes 8257544 | tf_op jit(solution)/shard_map/ppermute | solution.py:218
  15.0 27.2 %collective-permute-start.2 = (bf16[3584,128]{1,0:T(8,128)(2,1)S(1)}, bf16[3584,128]{1,0:T(8,128)(2,1)S(1)}, u32[]{:S(2)}, u32[]{:S(2)}) collective-permute-start(bf16[3584,128]{1,0:T(8,128)(2,1)S(1)} %copy-done.3), channel_id=1, source_target_pairs={{0,1},{1,0},{2,3},{3,2},{4,5},{5,4},{6,7},{7,6}} | collective-permute-start | bytes 2752520 | tf_op jit(solution)/shard_map/ppermute | solution.py:218
  24.5 41.4 %collective-permute-start.9 = (bf16[512,16,128]{2,1,0:T(8,128)(2,1)}, bf16[512,16,128]{2,1,0:T(8,128)(2,1)}, u32[]{:S(2)}, u32[]{:S(2)}) collective-permute-start(bf16[512,16,128]{2,1,0:T(8,128)(2,1)} %param.19), channel_id=1, source_target_pairs={{0,1},{1,0},{2,3},{3,2},{4,5},{5,4},{6,7},{7,6}} | collective-permute-start | bytes 6291464 | tf_op jit(solution)/shard_map/ppermute | solution.py:218
  42.2 28.7 %collective-permute-start.10 = (bf16[512,16,128]{2,1,0:T(8,128)(2,1)}, bf16[512,16,128]{2,1,0:T(8,128)(2,1)S(1)}, u32[]{:S(2)}, u32[]{:S(2)}) collective-permute-start(bf16[512,16,128]{2,1,0:T(8,128)(2,1)} %param.20), channel_id=1, source_target_pairs={{0,1},{1,0},{2,3},{3,2},{4,5},{5,4},{6,7},{7,6}} | collective-permute-start | bytes 6291464 | tf_op jit(solution)/shard_map/ppermute | solution.py:218
  44.6 91.6 %collective-permute-start.7 = (bf16[3584,384]{1,0:T(8,128)(2,1)}, bf16[3584,384]{1,0:T(8,128)(2,1)}, u32[]{:S(2)}, u32[]{:S(2)}) collective-permute-start(bf16[3584,384]{1,0:T(8,128)(2,1)} %rest_0_.5), channel_id=1, source_target_pairs={{0,2},{2,0},{1,3},{3,1},{4,6},{6,4},{5,7},{7,5}} | collective-permute-start | bytes 8257544 | tf_op jit(solution)/shard_map/ppermute | solution.py:221
  65.9 28.9 %collective-permute-start.3 = (bf16[512,1152]{1,0:T(8,128)(2,1)S(1)}, bf16[512,1152]{1,0:T(8,128)(2,1)S(1)}, u32[]{:S(2)}, u32[]{:S(2)}) collective-permute-start(bf16[512,1152]{1,0:T(8,128)(2,1)S(1)} %get-tuple-element.125), channel_id=1, source_target_pairs={{0,4},{4,0},{1,5},{5,1},{2,6},{6,2},{3,7},{7,3}} | collective-permute-start | bytes 3538952 | tf_op jit(solution)/shard_map/ppermute | solution.py:224
  70.9 48.3 %collective-permute-start.14 = (bf16[512,1152]{1,0:T(8,128)(2,1)S(1)}, bf16[512,1152]{1,0:T(8,128)(2,1)S(1)}, u32[]{:S(2)}, u32[]{:S(2)}) collective-permute-start(bf16[512,1152]{1,0:T(8,128)(2,1)S(1)} %get-tuple-element.124), channel_id=1, source_target_pairs={{0,4},{4,0},{1,5},{5,1},{2,6},{6,2},{3,7},{7,3}} | collective-permute-start | bytes 3538952 | tf_op jit(solution)/shard_map/ppermute | solution.py:224
  94.8 41.4 %collective-permute-start.6 = (bf16[1,512]{1,0:T(2,128)(2,1)S(1)}, bf16[1,512]{1,0:T(2,128)(2,1)S(1)}, u32[]{:S(2)}, u32[]{:S(2)}) collective-permute-start(bf16[1,512]{1,0:T(2,128)(2,1)S(1)} %broadcast_in_dim.47), channel_id=1, source_target_pairs={{0,2},{2,0},{1,3},{3,1},{4,6},{6,4},{5,7},{7,5}} | collective-permute-start | bytes 3080 | tf_op jit(solution)/shard_map/ppermute | solution.py:221
  119.2 19.9 %collective-permute-start.5 = (bf16[1,512]{1,0:T(2,128)(2,1)S(1)}, bf16[1,512]{1,0:T(2,128)(2,1)S(1)}, u32[]{:S(2)}, u32[]{:S(2)}) collective-permute-start(bf16[1,512]{1,0:T(2,128)(2,1)S(1)} %broadcast_in_dim.47), channel_id=1, source_target_pairs={{0,1},{1,0},{2,3},{3,2},{4,5},{5,4},{6,7},{7,6}} | collective-permute-start | bytes 3080 | tf_op jit(solution)/shard_map/ppermute | solution.py:218
  119.2 26.0 %collective-permute-start.4 = (bf16[512,1024]{1,0:T(8,128)(2,1)S(1)}, bf16[512,1024]{1,0:T(8,128)(2,1)S(1)}, u32[]{:S(2)}, u32[]{:S(2)}) collective-permute-start(bf16[512,1024]{1,0:T(8,128)(2,1)S(1)} %slice.92.refs_1_), channel_id=1, source_target_pairs={{0,2},{2,0},{1,3},{3,1},{4,6},{6,4},{5,7},{7,5}} | collective-permute-start | bytes 3145736 | tf_op jit(solution)/shard_map/ppermute | solution.py:221
  136.2 2.9 collective-permute-start.11
  137.4 61.8 %collective-permute-start.15 = (bf16[3584,128]{1,0:T(8,128)(2,1)S(1)}, bf16[3584,128]{1,0:T(8,128)(2,1)}, u32[]{:S(2)}, u32[]{:S(2)}) collective-permute-start(bf16[3584,128]{1,0:T(8,128)(2,1)S(1)} %copy-done.4), channel_id=1, source_target_pairs={{0,2},{2,0},{1,3},{3,1},{4,6},{6,4},{5,7},{7,5}} | collective-permute-start | bytes 2752520 | tf_op jit(solution)/shard_map/ppermute | solution.py:221
  139.1 66.2 %collective-permute-start.13 = (bf16[3584,384]{1,0:T(8,128)(2,1)}, bf16[3584,384]{1,0:T(8,128)(2,1)}, u32[]{:S(2)}, u32[]{:S(2)}) collective-permute-start(bf16[3584,384]{1,0:T(8,128)(2,1)} %collective-permute-done.7.rest_2_), channel_id=1, source_target_pairs={{0,1},{1,0},{2,3},{3,2},{4,5},{5,4},{6,7},{7,6}} | collective-permute-start | bytes 8257544 | tf_op jit(solution)/shard_map/ppermute | solution.py:218
  199.3 6.1 collective-permute-start.16
  201.4 37.3 %collective-permute-start.18 = (bf16[512,1024]{1,0:T(8,128)(2,1)S(1)}, bf16[512,1024]{1,0:T(8,128)(2,1)}, u32[]{:S(2)}, u32[]{:S(2)}) collective-permute-start(bf16[512,1024]{1,0:T(8,128)(2,1)S(1)} %slice.97.refs_1_), channel_id=1, source_target_pairs={{0,2},{2,0},{1,3},{3,1},{4,6},{6,4},{5,7},{7,5}} | collective-permute-start | bytes 3145736 | tf_op jit(solution)/shard_map/ppermute | solution.py:221
  201.7 471.7 %collective-permute-start.24 = (bf16[512,3584]{1,0:T(8,128)(2,1)}, bf16[512,3584]{1,0:T(8,128)(2,1)}, u32[]{:S(2)}, u32[]{:S(2)}) collective-permute-start(bf16[512,3584]{1,0:T(8,128)(2,1)} %get-tuple-element.49), channel_id=1, source_target_pairs={{0,2},{2,0},{1,3},{3,1},{4,6},{6,4},{5,7},{7,5}} | collective-permute-start | bytes 11010056 | tf_op jit(solution)/shard_map/ppermute | solution.py:221
  237.1 55.4 %collective-permute-start.17 = (bf16[512,2176]{1,0:T(8,128)(2,1)S(1)}, bf16[512,2176]{1,0:T(8,128)(2,1)}, u32[]{:S(2)}, u32[]{:S(2)}) collective-permute-start(bf16[512,2176]{1,0:T(8,128)(2,1)S(1)} %get-tuple-element.119), channel_id=1, source_target_pairs={{0,4},{4,0},{1,5},{5,1},{2,6},{6,2},{3,7},{7,3}} | collective-permute-start | bytes 6684680 | tf_op jit(solution)/shard_map/ppermute | solution.py:224
  291.6 392.4 %collective-permute-start.25 = (bf16[512,3584]{1,0:T(8,128)(2,1)}, bf16[512,3584]{1,0:T(8,128)(2,1)}, u32[]{:S(2)}, u32[]{:S(2)}) collective-permute-start(bf16[512,3584]{1,0:T(8,128)(2,1)} %get-tuple-element.56), channel_id=1, source_target_pairs={{0,2},{2,0},{1,3},{3,1},{4,6},{6,4},{5,7},{7,5}} | collective-permute-start | bytes 11010056 | tf_op jit(solution)/shard_map/ppermute | solution.py:221
  292.2 110.1 %collective-permute-start.23 = (bf16[512,2176]{1,0:T(8,128)(2,1)}, bf16[512,2176]{1,0:T(8,128)(2,1)}, u32[]{:S(2)}, u32[]{:S(2)}) collective-permute-start(bf16[512,2176]{1,0:T(8,128)(2,1)} %get-tuple-element.118), channel_id=1, source_target_pairs={{0,4},{4,0},{1,5},{5,1},{2,6},{6,2},{3,7},{7,3}} | collective-permute-start | bytes 6684680 | tf_op jit(solution)/shard_map/ppermute | solution.py:224
  400.6 57.4 %collective-permute-start.22 = (bf16[512,2176]{1,0:T(8,128)(2,1)}, bf16[512,2176]{1,0:T(8,128)(2,1)}, u32[]{:S(2)}, u32[]{:S(2)}) collective-permute-start(bf16[512,2176]{1,0:T(8,128)(2,1)} %get-tuple-element.114), channel_id=1, source_target_pairs={{0,4},{4,0},{1,5},{5,1},{2,6},{6,2},{3,7},{7,3}} | collective-permute-start | bytes 6684680 | tf_op jit(solution)/shard_map/ppermute | solution.py:224
  455.9 56.2 %collective-permute-start.21 = (bf16[512,2176]{1,0:T(8,128)(2,1)}, bf16[512,2176]{1,0:T(8,128)(2,1)}, u32[]{:S(2)}, u32[]{:S(2)}) collective-permute-start(bf16[512,2176]{1,0:T(8,128)(2,1)} %get-tuple-element.115), channel_id=1, source_target_pairs={{0,4},{4,0},{1,5},{5,1},{2,6},{6,2},{3,7},{7,3}} | collective-permute-start | bytes 6684680 | tf_op jit(solution)/shard_map/ppermute | solution.py:224
  456.2 109.5 %collective-permute-start.20 = (bf16[512,2176]{1,0:T(8,128)(2,1)}, bf16[512,2176]{1,0:T(8,128)(2,1)}, u32[]{:S(2)}, u32[]{:S(2)}) collective-permute-start(bf16[512,2176]{1,0:T(8,128)(2,1)} %get-tuple-element.116), channel_id=1, source_target_pairs={{0,4},{4,0},{1,5},{5,1},{2,6},{6,2},{3,7},{7,3}} | collective-permute-start | bytes 6684680 | tf_op jit(solution)/shard_map/ppermute | solution.py:224
  457.9 161.5 %collective-permute-start.19 = (bf16[512,2176]{1,0:T(8,128)(2,1)S(1)}, bf16[512,2176]{1,0:T(8,128)(2,1)}, u32[]{:S(2)}, u32[]{:S(2)}) collective-permute-start(bf16[512,2176]{1,0:T(8,128)(2,1)S(1)} %get-tuple-element.117), channel_id=1, source_target_pairs={{0,4},{4,0},{1,5},{5,1},{2,6},{6,2},{3,7},{7,3}} | collective-permute-start | bytes 6684680 | tf_op jit(solution)/shard_map/ppermute | solution.py:224
  682.0 10.7 collective-permute-start.26
  682.0 82.5 %collective-permute-start.27 = (bf16[512,3584]{1,0:T(8,128)(2,1)}, bf16[512,3584]{1,0:T(8,128)(2,1)}, u32[]{:S(2)}, u32[]{:S(2)}) collective-permute-start(bf16[512,3584]{1,0:T(8,128)(2,1)} %get-tuple-element.58), channel_id=1, source_target_pairs={{0,2},{2,0},{1,3},{3,1},{4,6},{6,4},{5,7},{7,5}} | collective-permute-start | bytes 11010056 | tf_op jit(solution)/shard_map/ppermute | solution.py:221
  683.7 159.5 %collective-permute-start.29 = (bf16[512,3584]{1,0:T(8,128)(2,1)}, bf16[512,3584]{1,0:T(8,128)(2,1)}, u32[]{:S(2)}, u32[]{:S(2)}) collective-permute-start(bf16[512,3584]{1,0:T(8,128)(2,1)} %get-tuple-element.61), channel_id=1, source_target_pairs={{0,2},{2,0},{1,3},{3,1},{4,6},{6,4},{5,7},{7,5}} | collective-permute-start | bytes 11010056 | tf_op jit(solution)/shard_map/ppermute | solution.py:221
  692.7 82.5 %collective-permute-start.28 = (bf16[1,512,3584]{2,1,0:T(8,128)(2,1)}, bf16[1,512,3584]{2,1,0:T(8,128)(2,1)}, u32[]{:S(2)}, u32[]{:S(2)}) collective-permute-start(bf16[1,512,3584]{2,1,0:T(8,128)(2,1)} %get-tuple-element.111), channel_id=1, source_target_pairs={{0,1},{1,0},{2,3},{3,2},{4,5},{5,4},{6,7},{7,6}} | collective-permute-start | bytes 11010056 | tf_op jit(solution)/shard_map/ppermute | solution.py:218
  773.2 77.6 %collective-permute-start.30 = (bf16[1,512,3584]{2,1,0:T(8,128)(2,1)}, bf16[1,512,3584]{2,1,0:T(8,128)(2,1)}, u32[]{:S(2)}, u32[]{:S(2)}) collective-permute-start(bf16[1,512,3584]{2,1,0:T(8,128)(2,1)} %get-tuple-element.109), channel_id=1, source_target_pairs={{0,1},{1,0},{2,3},{3,2},{4,5},{5,4},{6,7},{7,6}} | collective-permute-start | bytes 11010056 | tf_op jit(solution)/shard_map/ppermute | solution.py:218
  773.2 148.7 %collective-permute-start.31 = (bf16[512,3584]{1,0:T(8,128)(2,1)}, bf16[512,3584]{1,0:T(8,128)(2,1)}, u32[]{:S(2)}, u32[]{:S(2)}) collective-permute-start(bf16[512,3584]{1,0:T(8,128)(2,1)} %get-tuple-element.63), channel_id=1, source_target_pairs={{0,2},{2,0},{1,3},{3,1},{4,6},{6,4},{5,7},{7,5}} | collective-permute-start | bytes 11010056 | tf_op jit(solution)/shard_map/ppermute | solution.py:221
  774.9 225.6 %collective-permute-start.33 = (bf16[512,3584]{1,0:T(8,128)(2,1)}, bf16[512,3584]{1,0:T(8,128)(2,1)}, u32[]{:S(2)}, u32[]{:S(2)}) collective-permute-start(bf16[512,3584]{1,0:T(8,128)(2,1)} %get-tuple-element.65), channel_id=1, source_target_pairs={{0,2},{2,0},{1,3},{3,1},{4,6},{6,4},{5,7},{7,5}} | collective-permute-start | bytes 11010056 | tf_op jit(solution)/shard_map/ppermute | solution.py:221
  850.8 85.8 %collective-permute-start.32 = (bf16[1,512,3584]{2,1,0:T(8,128)(2,1)}, bf16[1,512,3584]{2,1,0:T(8,128)(2,1)}, u32[]{:S(2)}, u32[]{:S(2)}) collective-permute-start(bf16[1,512,3584]{2,1,0:T(8,128)(2,1)} %get-tuple-element.107), channel_id=1, source_target_pairs={{0,1},{1,0},{2,3},{3,2},{4,5},{5,4},{6,7},{7,6}} | collective-permute-start | bytes 11010056 | tf_op jit(solution)/shard_map/ppermute | solution.py:218
  854.9 77.3 %copy-start.20 = (bf16[512,128]{1,0:T(8,128)(2,1)S(1)}, bf16[512,128]{1,0:T(8,128)(2,1)}, u32[]{:S(2)}) copy-start(bf16[512,128]{1,0:T(8,128)(2,1)} %get-tuple-element.79) | copy-start | bytes 393220
  854.9 77.4 %copy-start.12 = (bf16[512,512]{1,0:T(8,128)(2,1)S(1)}, bf16[512,512]{1,0:T(8,128)(2,1)}, u32[]{:S(2)}) copy-start(bf16[512,512]{1,0:T(8,128)(2,1)} %get-tuple-element.71) | copy-start | bytes 1572868
  854.9 78.2 %copy-start.25 = (bf16[512,128]{1,0:T(8,128)(2,1)S(1)}, bf16[512,128]{1,0:T(8,128)(2,1)}, u32[]{:S(2)}) copy-start(bf16[512,128]{1,0:T(8,128)(2,1)} %get-tuple-element.80) | copy-start | bytes 393220
  930.5 77.6 %collective-permute-start.34 = (bf16[1,512,3584]{2,1,0:T(8,128)(2,1)}, bf16[1,512,3584]{2,1,0:T(8,128)(2,1)}, u32[]{:S(2)}, u32[]{:S(2)}) collective-permute-start(bf16[1,512,3584]{2,1,0:T(8,128)(2,1)} %get-tuple-element.105), channel_id=1, source_target_pairs={{0,1},{1,0},{2,3},{3,2},{4,5},{5,4},{6,7},{7,6}} | collective-permute-start | bytes 11010056 | tf_op jit(solution)/shard_map/ppermute | solution.py:218
  930.5 148.2 %collective-permute-start.35 = (bf16[512,3584]{1,0:T(8,128)(2,1)}, bf16[512,3584]{1,0:T(8,128)(2,1)}, u32[]{:S(2)}, u32[]{:S(2)}) collective-permute-start(bf16[512,3584]{1,0:T(8,128)(2,1)} %get-tuple-element.67), channel_id=1, source_target_pairs={{0,2},{2,0},{1,3},{3,1},{4,6},{6,4},{5,7},{7,5}} | collective-permute-start | bytes 11010056 | tf_op jit(solution)/shard_map/ppermute | solution.py:221
  1008.1 88.7 %collective-permute-start.36 = (bf16[1,512,3584]{2,1,0:T(8,128)(2,1)}, bf16[1,512,3584]{2,1,0:T(8,128)(2,1)}, u32[]{:S(2)}, u32[]{:S(2)}) collective-permute-start(bf16[1,512,3584]{2,1,0:T(8,128)(2,1)} %get-tuple-element.103), channel_id=1, source_target_pairs={{0,1},{1,0},{2,3},{3,2},{4,5},{5,4},{6,7},{7,6}} | collective-permute-start | bytes 11010056 | tf_op jit(solution)/shard_map/ppermute | solution.py:218
  1012.2 75.5 %copy-start.1 = (bf16[512,3584]{1,0:T(8,128)(2,1)S(1)}, bf16[512,3584]{1,0:T(8,128)(2,1)}, u32[]{:S(2)}) copy-start(bf16[512,3584]{1,0:T(8,128)(2,1)} %get-tuple-element.69) | copy-start | bytes 11010052
  1087.7 49.2 %collective-permute-start.38 = (bf16[1,512,3584]{2,1,0:T(8,128)(2,1)}, bf16[1,512,3584]{2,1,0:T(8,128)(2,1)}, u32[]{:S(2)}, u32[]{:S(2)}) collective-permute-start(bf16[1,512,3584]{2,1,0:T(8,128)(2,1)} %get-tuple-element.101), channel_id=1, source_target_pairs={{0,1},{1,0},{2,3},{3,2},{4,5},{5,4},{6,7},{7,6}} | collective-permute-start | bytes 11010056 | tf_op jit(solution)/shard_map/ppermute | solution.py:218
  1089.8 43.1 %collective-permute-start.37 = (bf16[256,3584]{1,0:T(8,128)(2,1)}, bf16[256,3584]{1,0:T(8,128)(2,1)S(1)}, u32[]{:S(2)}, u32[]{:S(2)}) collective-permute-start(bf16[256,3584]{1,0:T(8,128)(2,1)} %get-tuple-element.123), channel_id=1, source_target_pairs={{0,2},{2,0},{1,3},{3,1},{4,6},{6,4},{5,7},{7,5}} | collective-permute-start | bytes 5505032 | tf_op jit(solution)/shard_map/ppermute | solution.py:221
  1091.5 80.3 %collective-permute-start.39 = (bf16[256,3584]{1,0:T(8,128)(2,1)}, bf16[256,3584]{1,0:T(8,128)(2,1)}, u32[]{:S(2)}, u32[]{:S(2)}) collective-permute-start(bf16[256,3584]{1,0:T(8,128)(2,1)} %get-tuple-element.122), channel_id=1, source_target_pairs={{0,2},{2,0},{1,3},{3,1},{4,6},{6,4},{5,7},{7,5}} | collective-permute-start | bytes 5505032 | tf_op jit(solution)/shard_map/ppermute | solution.py:221
  1136.9 53.4 %collective-permute-start.40 = (bf16[1,256,3584]{2,1,0:T(8,128)(2,1)}, bf16[1,256,3584]{2,1,0:T(8,128)(2,1)}, u32[]{:S(2)}, u32[]{:S(2)}) collective-permute-start(bf16[1,256,3584]{2,1,0:T(8,128)(2,1)} %get-tuple-element.99), channel_id=1, source_target_pairs={{0,1},{1,0},{2,3},{3,2},{4,5},{5,4},{6,7},{7,6}} | collective-permute-start | bytes 5505032 | tf_op jit(solution)/shard_map/ppermute | solution.py:218
  1176.4 17.5 %collective-permute-start.41 = (bf16[1,256,3584]{2,1,0:T(8,128)(2,1)}, bf16[1,256,3584]{2,1,0:T(8,128)(2,1)}, u32[]{:S(2)}, u32[]{:S(2)}) collective-permute-start(bf16[1,256,3584]{2,1,0:T(8,128)(2,1)} %get-tuple-element.97), channel_id=1, source_target_pairs={{0,1},{1,0},{2,3},{3,2},{4,5},{5,4},{6,7},{7,6}} | collective-permute-start | bytes 5505032 | tf_op jit(solution)/shard_map/ppermute | solution.py:218
  1179.2 9.7 collective-permute-start.42
  1181.4 2.3 collective-permute-start.43
  (27 other events, 402.6 us)

commit v2 on v1

--- a/solution.py
+++ b/solution.py
@@ -17,9 +17,9 @@
 ACROSS = [(0, 2), (2, 0), (1, 3), (3, 1)]
 EMB_SWAP = [(0, 1), (1, 0)]
 
-FIRST = 2
-DOWNS = {0: ((2, 2),), 2: ((4, 4),)}
-PIECES = {7: ((0, 256), (256, 512))}
+FIRST = 3
+DOWNS = {1: ((3, 1),), 2: ((4, 1),), 3: ((5, 3),)}
+PIECES = {0: ((0, 256), (256, 512)), 7: ((0, 384), (384, 512))}
 ROWS = 256
 
 
@@ -74,51 +74,63 @@
     )(offs, hidden, rstd, g_in, *pieces)
 
 
-def block_kernel(scale, split, side_ref, *refs):
-    n_in = 3 if split else 2
+def block_kernel(scale, mode, q_lo, side_ref, *refs):
+    n_in = {"full": 2, "pair": 4, "sum": 3, "sum2": 6}[mode]
     ins = refs[:n_in]
     gq_ref, gkv_ref, cos_ref, sin_ref, wq_ref, wk_ref, wv_ref, wo_a_ref, wo_b_ref = refs[n_in:n_in + 9]
     part_ref, ckv_ref, kk_ref, cq_ref, kpe_ref, ctx_ref = refs[n_in + 9:]
     step = pl.program_id(0)
-    seq, q_lora = cq_ref.shape
-    kv_lora = ckv_ref.shape[1]
+    q_rows, q_lora = cq_ref.shape
+    seq, kv_lora = ckv_ref.shape
     heads = wq_ref.shape[0]
     wide = heads * 128
     steps = ctx_ref.shape[1] // wide
     blk = 256
+    qh, kh = q_lora // 2, kv_lora // 2
 
     def norm(vals, gain):
         mean_sq = jnp.mean(vals * vals, axis=-1, keepdims=True)
         return (vals * lax.rsqrt(mean_sq + NORM_EPS) * gain).astype(BF16)
 
-    @pl.when(step == 0)
-    def _():
-        @pl.loop(0, seq // 128)
+    def fill(group, start, count):
+        @pl.loop(0, count // 128)
         def _(c):
-            rows = pl.ds(pl.multiple_of(c * 128, 128), 128)
+            src = pl.ds(pl.multiple_of(c * 128, 128), 128)
+            rows = pl.ds(pl.multiple_of(start + c * 128, 128), 128)
 
             def summed(a_ref, b_ref, lo, hi):
-                return (a_ref[rows, lo:hi].astype(F32) + b_ref[rows, lo:hi].astype(F32)).astype(BF16).astype(F32)
-
-            if split:
+                return (a_ref[src, lo:hi].astype(F32) + b_ref[src, lo:hi].astype(F32)).astype(BF16).astype(F32)
+
+            def halves(lo, hi):
+                if mode == "pair":
+                    own, far = summed(group[0], group[1], lo, hi), summed(group[2], group[3], lo, hi)
+                else:
+                    own, far = group[0][src, lo:hi].astype(F32), group[1][src, lo:hi].astype(F32)
                 first = side_ref[0] == 0
-                qh, kh = q_lora // 2, kv_lora // 2
-
-                def both(lo, hi):
-                    own, far = ins[0][rows, lo:hi].astype(F32), ins[1][rows, lo:hi].astype(F32)
-                    return jnp.concatenate([jnp.where(first, own, far), jnp.where(first, far, own)], axis=1)
-
-                cq, ckv, kr = both(0, qh), both(qh, qh + kh), ins[2][rows].astype(F32)
+                return jnp.concatenate([jnp.where(first, own, far), jnp.where(first, far, own)], axis=1)
+
+            if mode == "full":
+                ckv, kr = summed(group[0], group[1], q_lora, q_lora + kv_lora), summed(group[0], group[1], q_lora + kv_lora, q_lora + kv_lora + 128)
             else:
-                cq, ckv = summed(ins[0], ins[1], 0, q_lora), summed(ins[0], ins[1], q_lora, q_lora + kv_lora)
-                kr = summed(ins[0], ins[1], q_lora + kv_lora, q_lora + kv_lora + 128)
-            cq_ref[rows] = norm(cq, gq_ref[...])
+                ckv = halves(qh, qh + kh)
+                kr = summed(group[0], group[1], qh + kh, qh + kh + 128) if mode == "pair" else group[2][src].astype(F32)
+            if start >= q_lo:
+                cq = summed(group[0], group[1], 0, q_lora) if mode == "full" else halves(0, qh)
+                cq_ref[pl.ds(pl.multiple_of(start - q_lo + c * 128, 128), 128)] = norm(cq, gq_ref[...])
             ckv_ref[rows] = norm(ckv, gkv_ref[...])
             kk = kr * cos_ref[rows] + pltpu.roll(kr, 64, 1) * sin_ref[rows]
             odd = (lax.broadcasted_iota(jnp.int32, kk.shape, 1) // 32) % 2 == 1
             kk_ref[rows] = kk.astype(BF16)
             kpe_ref[0, rows] = jnp.where(odd, 0.0, kk).astype(BF16)
             kpe_ref[1, rows] = jnp.where(odd, kk, 0.0).astype(BF16)
+
+    @pl.when(step == 0)
+    def _():
+        if mode == "sum2":
+            fill(ins[:3], 0, seq // 2)
+            fill(ins[3:], seq // 2, seq // 2)
+        else:
+            fill(ins, 0, seq)
 
     def nt(a, b):
         return lax.dot_general(a, b, (((1,), (1,)), ((), ())), preferred_element_type=F32)
@@ -132,21 +144,24 @@
             a, b = 2 * pair, 2 * pair + 1
             wr = jnp.concatenate([wq_ref[a, 128:160], wq_ref[b, 128:160], wq_ref[a, 160:192], wq_ref[b, 160:192]], axis=0)
             qr = nt(cq, wr).astype(BF16).astype(F32)
-            qps.append((qr * cos_ref[...] + pltpu.roll(qr, 64, 1) * sin_ref[...]).astype(BF16))
+            qps.append((qr * cos_ref[q_lo:] + pltpu.roll(qr, 64, 1) * sin_ref[q_lo:]).astype(BF16))
         kn = jnp.dot(ckv, wk_ref[...], preferred_element_type=F32).astype(BF16)
         val = jnp.dot(ckv, wv_ref[...], preferred_element_type=F32).astype(BF16)
         row = lax.broadcasted_iota(jnp.int32, (blk, blk), 0)
         col = lax.broadcasted_iota(jnp.int32, (blk, blk), 1)
         allowed = col <= row
-        items = [(hh, qb) for hh in range(heads) for qb in range(seq // blk)]
+        items = [(hh, qb) for hh in range(heads) for qb in range(q_rows // blk)]
+
+        def span(qb):
+            return slice(qb * blk, (qb + 1) * blk), q_lo + (qb + 1) * blk
 
         def score(hh, qb):
-            cols, rows, end = slice(hh * 128, hh * 128 + 128), slice(qb * blk, (qb + 1) * blk), (qb + 1) * blk
+            cols, (rows, end) = slice(hh * 128, hh * 128 + 128), span(qb)
             key = jnp.concatenate([kn[:end, cols], kpe_ref[hh % 2, :end]], axis=1)
             q = jnp.concatenate([qn[rows, cols], qps[hh // 2][rows]], axis=1)
             s = nt(q, key)
             diag = jnp.where(allowed, s[:, end - blk:], -jnp.inf)
-            return diag if qb == 0 else jnp.concatenate([s[:, :end - blk], diag], axis=1)
+            return diag if end == blk else jnp.concatenate([s[:, :end - blk], diag], axis=1)
 
         def softmax(s):
             top = jnp.max(s, axis=1, keepdims=True)
@@ -156,7 +171,7 @@
         scores = [score(*it) for it in items]
         probs = [softmax(s) for s in scores]
         for p, (hh, qb) in zip(probs, items):
-            rows, end = slice(qb * blk, (qb + 1) * blk), (qb + 1) * blk
+            rows, end = span(qb)
             o = jnp.dot(p, val[:end, hh * 128:hh * 128 + 128], preferred_element_type=F32).astype(BF16)
             ctx_ref[rows, pl.ds(pl.multiple_of(step * wide + hh * 128, 128), 128)] = o
 
@@ -168,8 +183,9 @@
         part_ref[...] = out.astype(BF16)
 
 
-def head_block(ins, at, side, gq, gkv, cos_p, sin_p, wq, wkv, wo_a, wo_b, scale):
-    seq = cos_p.shape[0]
+def head_block(mode, ins, at, q_lo, seq, side, gq, gkv, cos_p, sin_p, wq, wkv, wo_a, wo_b, scale):
+    q_rows = seq - q_lo
+    in_rows = seq // 2 if mode == "sum2" else seq
     n_heads, qk, q_lora = wq.shape
     kv_lora, depth, width = wkv.shape[0], wo_a.shape[0], wo_a.shape[1]
     heads, wide = 4, 512
@@ -179,11 +195,11 @@
     oc = lambda j: jnp.maximum(j - steps, 0)
     const = lambda shape: pl.BlockSpec(shape, lambda j, o: (0,) * len(shape), pipeline_mode=once)
     return pl.pallas_call(
-        lambda *refs: block_kernel(scale, len(ins) == 3, *refs),
+        lambda *refs: block_kernel(scale, mode, q_lo, *refs),
         grid_spec=pltpu.PrefetchScalarGridSpec(
             num_scalar_prefetch=1,
             grid=(steps + out_steps,),
-            in_specs=[pl.BlockSpec((seq, a.shape[1]), lambda j, o, r=r: (r, 0), pipeline_mode=once) for a, r in zip(ins, at)] + [
+            in_specs=[pl.BlockSpec((in_rows, a.shape[1]), lambda j, o, r=r: (r, 0), pipeline_mode=once) for a, r in zip(ins, at)] + [
                 const((1, q_lora)), const((1, kv_lora)), const((seq, 128)), const((seq, 128)),
                 pl.BlockSpec((heads, qk, q_lora), lambda j, o: (hd(j), 0, 0)),
                 pl.BlockSpec((kv_lora, wide), lambda j, o: (0, hd(j))),
@@ -192,15 +208,15 @@
                 pl.BlockSpec((depth, wide), lambda j, o: (0, oc(j))),
             ],
             out_specs=[
-                pl.BlockSpec((seq, wide), lambda j, o: (0, oc(j))),
+                pl.BlockSpec((q_rows, wide), lambda j, o: (0, oc(j))),
                 pl.BlockSpec((seq, kv_lora), lambda j, o: (0, 0)),
                 pl.BlockSpec((seq, 128), lambda j, o: (0, 0)),
             ],
-            scratch_shapes=[pltpu.VMEM((seq, q_lora), BF16), pltpu.VMEM((2, seq, 128), BF16), pltpu.VMEM((seq, n_heads * 128), BF16)],
+            scratch_shapes=[pltpu.VMEM((q_rows, q_lora), BF16), pltpu.VMEM((2, seq, 128), BF16), pltpu.VMEM((q_rows, n_heads * 128), BF16)],
         ),
-        out_shape=[jax.ShapeDtypeStruct((seq, width), BF16), jax.ShapeDtypeStruct((seq, kv_lora), BF16), jax.ShapeDtypeStruct((seq, 128), BF16)],
+        out_shape=[jax.ShapeDtypeStruct((q_rows, width), BF16), jax.ShapeDtypeStruct((seq, kv_lora), BF16), jax.ShapeDtypeStruct((seq, 128), BF16)],
         compiler_params=pltpu.CompilerParams(dimension_semantics=("arbitrary",), vmem_limit_bytes=60 * 2**20),
-        cost_estimate=pl.CostEstimate(flops=45 * 10**9, bytes_accessed=64 * 10**6, transcendentals=n_heads * seq * seq),
+        cost_estimate=pl.CostEstimate(flops=45 * 10**9 * q_rows // 512, bytes_accessed=64 * 10**6, transcendentals=n_heads * seq * seq),
         name="block",
     )(side, *ins, gq, gkv, cos_p, sin_p, wq, wkv, wkv, wo_a, wo_b)
 
@@ -238,6 +254,7 @@
         base = core * half
 
         far_q = cross(w_dq)
+        far_kv = cross(w_dkv)
         near_q, near_kv = swap(w_dq), swap(w_dkv)
         sib_uq, sib_uk, sib_uv = swap(w_uq), swap(w_uk), swap(w_uv)
         sib_o = swap(w_o)
@@ -260,22 +277,22 @@
         def rows_of(low, r):
             return low[r * seq:(r + 1) * seq]
 
-        own_in = [emb_swap(rows_of(low_own, r)) for r in range(FIRST)]
-
-        w_uq, sib_uq = after((w_uq, sib_uq), low_own)
+        cuts = [(0, seq // 2), (seq // 2, seq)] + [(r * seq, r * seq + seq) for r in range(1, FIRST)]
+        own_in = [emb_swap(low_own[lo:hi]) for lo, hi in cuts]
+
+        w_uq, sib_uq, w_uk, w_uv, sib_uk, sib_uv = after((w_uq, sib_uq, w_uk, w_uv, sib_uk, sib_uv), low_own)
         flat = lambda w: w.reshape(kv_lora, own_heads * 128)
-        wq_all = jnp.concatenate([w_uq.transpose(1, 2, 0), sib_uq.transpose(1, 2, 0)], axis=0)
         wkv_all = jnp.concatenate([flat(w_uk), flat(sib_uk), flat(w_uv), flat(sib_uv)], axis=1)
+        wq_all = jnp.concatenate([w_uq.transpose(1, 2, 0), after(sib_uq, wkv_all).transpose(1, 2, 0)], axis=0)
         wo_own, wo_sib = w_o.reshape(own_heads * 128, width), sib_o.reshape(own_heads * 128, width)
 
-        lows = {}
-        for r in range(FIRST):
-            arrived_r = own_in[r] if r == 0 else after(own_in[r], lat)
-            lat = (rows_of(low_own, r).astype(F32) + arrived_r.astype(F32)).astype(BF16)
+        lats = []
+        for k, (lo, hi) in enumerate(cuts[:2]):
+            got = own_in[k] if k == 0 else after(own_in[k], lat)
+            lat = (low_own[lo:hi].astype(F32) + got.astype(F32)).astype(BF16)
             far_lat = cross(lat[:, :qh + kh])
-            lows[r] = ((lat[:, :qh + kh], far_lat, lat[:, qh + kh:]), (0, 0, 0))
-        far_kv = cross(after(w_dkv, lat))
-
+            lats.append((lat[:, :qh + kh], far_lat, lat[:, qh + kh:]))
+        low_x = cross(low_own[seq:2 * seq, :qh + kh])
         far_gain, far_q = after((far_gain, far_q), wq_all, wkv_all)
         gains = jnp.concatenate([gain, swap(gain), far_gain, swap(far_gain)], axis=0).astype(F32)
         gains = jnp.concatenate([lax.dynamic_slice_in_dim(gains, lax.bitwise_xor(pos, r), 1, 0) for r in range(4)], axis=0)
@@ -285,35 +302,52 @@
         every_offs = [lax.bitwise_xor(pos, r) * q_blk for r in range(4)] + [q_lora + lax.bitwise_xor(pos, r) * kv_blk for r in range(4)] + [q_lora + kv_lora]
 
         side_flag = side.astype(jnp.int32)[None]
-        parts, arrived, ckvs, kks = [], {}, [], []
+        parts, arrived, ckvs, kks = {}, {}, [], []
         last = wq_all
         result = blank(hidden.shape, BF16)
 
         def finish(i, lo, hi, dep):
             at = after(base, *dep)
             h_i = lax.dynamic_slice(hidden, (at + i, 0 * at + lo, 0 * at), (1, hi - lo, width)).astype(F32)
-            total = parts[i][lo:hi].astype(F32) + arrived[i, lo].astype(F32)
+            total = parts[i, lo].astype(F32) + arrived[i, lo].astype(F32)
             return (h_i + total[None]).astype(BF16)
 
-        for i in range(half):
-            gq_i = after(gq_all, last)
-            ins, at = lows[i]
-            part, ckv, kk = head_block(ins, at, side_flag, gq_i, gkv_all, cos_p, sin_p, wq_all, wkv_all, wo_own, wo_sib, scale)
+        def run(mode, ins, at, q_lo, rows, dep):
+            return head_block(mode, ins, at, q_lo, rows, side_flag, after(gq_all, dep), gkv_all, cos_p, sin_p, wq_all, wkv_all, wo_own, wo_sib, scale)
+
+        def send(i, lo, part):
+            parts[i, lo] = part
+            arrived[i, lo] = cross(part)
+
+        hs = seq // 2
+        part_a, _, _ = run("sum", lats[0], (0,) * 3, 0, hs, last)
+        send(0, 0, part_a)
+        low_xy = emb_swap(after(low_x, part_a))
+        part, ckv, kk = run("sum2", lats[0] + lats[1], (0,) * 6, hs, seq, part_a)
+        send(0, hs, part)
+        ckvs.append(ckv)
+        kks.append(kk)
+        far_kv = after(far_kv, part)
+        diag_kv = swap(far_kv)
+        every = [w_dq, near_q, far_q, diag_q, w_dkv, near_kv, far_kv, diag_kv, w_kr2]
+        lows = {1: ("pair", (low_own, own_in[2], low_x, low_xy), (1, 0, 0, 0))}
+        last = part
+        for i in range(1, half):
+            mode, ins, at = lows[i]
+            part, ckv, kk = run(mode, ins, at, 0, seq, last)
             ckvs.append(ckv)
             kks.append(kk)
-            parts.append(part)
+            last = part
             for lo, hi in PIECES.get(i, ((0, seq),)):
-                arrived[i, lo] = cross(part[lo:hi])
-            last = part
-            if i == 0:
-                far_kv = after(far_kv, part)
-                diag_kv = swap(far_kv)
-                every = [w_dq, near_q, far_q, diag_q, w_dkv, near_kv, far_kv, diag_kv, w_kr2]
+                send(i, lo, part[lo:hi])
+            if i == 1:
+                last = down(hidden, after(rstd, last), g_row, 2, 1, base, [far_q, diag_q, far_kv, diag_kv], near_offs)
+                lows[2] = ("pair", (low_own, own_in[3], last, emb_swap(last)), (2, 0, 0, 0))
             for first, n in DOWNS.get(i, ()):
                 low = down(hidden, after(rstd, last), g_row, first, n, base, every, every_offs)
                 last = low
                 for r in range(n):
-                    lows[first + r] = ((low, emb_swap(rows_of(low, r))), (r, 0))
+                    lows[first + r] = ("full", (low, emb_swap(rows_of(low, r))), (r, 0))
 
         def spread(own, other):
             full = blank((n_seq,) + own.shape[1:], own.dtype)

time: 1210 us -> 1290 us (1.066)
  Pallas kernels: 519 us -> 557 us
  waiting for transfers between devices: 450 us -> 485 us
    ppermute x14 -> x16, waiting for transfers between devices: 392 us -> 448 us  [cross(): return lax.ppermute(v, 'head', ACROSS)]
    ppermute x9 -> x12, waiting for transfers between devices: 41.8 us -> 19 us  [emb_swap(): return lax.ppermute(v, 'emb', EMB_SWAP)]
    pallas_call x8 -> x9, Pallas kernels: 428 us -> 450 us  [head_block(): pl.pallas_call(lambda *refs: block_kernel(scale, mode, q_lo, *refs), grid...]
    pallas_call x3 -> x5, Pallas kernels: 90.9 us -> 107 us  [down(): pl.pallas_call(down_kernel, grid_spec=pltpu.PrefetchScalarGridSpec(num_sc...]
    dynamic_update_slice x9 -> x10, local copies, waits for them, and re-layouts: 35.7 us -> 36.6 us  [place(): lax.dynamic_update_slice(result, other, (half - base + i, 0 * base + lo,...]
    dynamic_update_slice x9 -> x10, other arithmetic: 67.2 us -> 67.6 us  [block(): lax.dynamic_update_slice(result, out_i, (base + i, 0 * base + lo, 0 * base))]
  transfers between devices with their start and end apart: 44 -> 50, of which waited for: 12 -> 12; matrix products, arithmetic and copies ran while one was open for 16% -> 15% of each run, Pallas kernels for 43% -> 43%
where the time goes in v2:
time: 1290 us
  Pallas kernels  557 us (43%)
  waiting for transfers between devices  485 us (38%)
  local copies, waits for them, and re-layouts  106 us (8%)
  other arithmetic  99.1 us (8%)
  starting transfers between devices  37.5 us (3%)
    pallas_call x9, Pallas kernels, head_block(): pl.pallas_call(lambda *refs: block_kernel(scale, mode, q_lo, *refs), grid...  450 us
    ppermute x16, waiting for transfers between devices, cross(): return lax.ppermute(v, 'head', ACROSS)  448 us
    pallas_call x5, Pallas kernels, down(): pl.pallas_call(down_kernel, grid_spec=pltpu.PrefetchScalarGridSpec(num_sc...  107 us
    dynamic_update_slice x10, other arithmetic, block(): lax.dynamic_update_slice(result, out_i, (base + i, 0 * base + lo, 0 * base))  67.6 us
    dynamic_update_slice x10, local copies, waits for them, and re-layouts, place(): lax.dynamic_update_slice(result, other, (half - base + i, 0 * base + lo,...  36.6 us
  transfers between devices with their start and end apart: 50, of which 12 were waited for; matrix products, arithmetic and copies ran while one was open for 15% of the time, Pallas kernels for 43%

profile of v2, /device:TPU:0, one launch (start us, length us, event | category | flops | bytes accessed | tf_op | source)
XLA Modules:
  0.0 1285.9 jit_solution(6461045007873660509)
XLA Ops:
  2.0 10.4 multiply_reduce_fusion
  23.6 18.7 %collective-permute-done.2.rest_3_.rest_5_ = bf16[3584,128]{1,0:T(8,128)(2,1)} collective-permute-done((bf16[3584,128]{1,0:T(8,128)(2,1)}, bf16[3584,128]{1,0:T(8,128)(2,1)}, u32[]{:S(2)}, u32[]{:S(2)}) %collective-permute-start.2) | collective-permute-done | bytes 917536 | tf_op jit(solution)/shard_map/ppermute | solution.py:234
  44.3 22.2 %down.5.refs_1_ = bf16[1536,1152]{1,0:T(8,128)(2,1)} custom-call(s32[6]{0:T(128)} %stack.105.offs_ref, bf16[16,512,3584]{2,1,0:T(8,128)(2,1)} %h_ref.9, f32[8,512,1]{2,1,0:T(8,128)} %copy.30.rstd_ref, f32[1,3584]{1,0:T(1,128)} %reshape.51.g_ref, bf16[3584,384]{1,0:T(8,128)(2,1)} %rest_0_.7, bf16[3584,384]{1,0:T(8,128)(2,1)} %copy-done.1, ...), custom_call_target="tpu_custom_call" | custom-call | flops 12683575296 | bytes 19267584 | tf_op jit(solution)/shard_map/down/pallas_call | solution.py:57
  75.8 9.9 collective-permute-done.5
  92.0 9.1 collective-permute-done.16
  110.0 13.3 %pad_maximum_fusion.refs_8_.refs_11_.refs_9_.refs_7_ = bf16[32,192,1536]{2,1,0:T(8,128)(2,1)} fusion(bf16[16,192,1536]{2,1,0:T(8,128)(2,1)} %bitcast.19, bf16[16,192,1536]{2,1,0:T(8,128)(2,1)S(1)} %bitcast.97), kind=kLoop, calls=%fused_computation.1 | loop fusion | flops 9437184 | bytes 37748736 | tf_op jit(solution)/shard_map/concatenate | solution.py:286
  123.3 40.3 %collective-permute-done.8 = bf16[1,512]{1,0:T(2,128)(2,1)S(1)} collective-permute-done((bf16[1,512]{1,0:T(2,128)(2,1)S(1)}, bf16[1,512]{1,0:T(2,128)(2,1)S(1)}, u32[]{:S(2)}, u32[]{:S(2)}) %collective-permute-start.8) | collective-permute-done | bytes 1056 | tf_op jit(solution)/shard_map/ppermute | solution.py:237
  171.6 43.4 %collective-permute-done.6.refs_2_ = bf16[256,1024]{1,0:T(8,128)(2,1)S(1)} collective-permute-done((bf16[256,1024]{1,0:T(8,128)(2,1)S(1)}, bf16[256,1024]{1,0:T(8,128)(2,1)S(1)}, u32[]{:S(2)}, u32[]{:S(2)}) %collective-permute-start.6) | collective-permute-done | bytes 524320 | tf_op jit(solution)/shard_map/ppermute | solution.py:237
  217.7 33.2 %block.9 = (bf16[256,3584]{1,0:T(8,128)(2,1)}, bf16[256,512]{1,0:T(8,128)(2,1)}, bf16[256,128]{1,0:T(8,128)(2,1)}) custom-call(s32[1]{0:T(128)} %bitcast.refs_0_, bf16[256,1024]{1,0:T(8,128)(2,1)} %copy-done.21, bf16[256,1024]{1,0:T(8,128)(2,1)} %copy-done.36, bf16[256,128]{1,0:T(8,128)(2,1)} %slice.93.refs_3_, f32[1,1536]{1,0:T(1,128)} %bitcast.100, ...), custom_call_target="tpu_custom_call" | custom-call | flops 22499999744 | bytes 64000000 | tf_op jit(solution)/shard_map/block/pallas_call | solution.py:197
  251.4 38.5 %block.10 = (bf16[256,3584]{1,0:T(8,128)(2,1)}, bf16[512,512]{1,0:T(8,128)(2,1)}, bf16[512,128]{1,0:T(8,128)(2,1)}) custom-call(s32[1]{0:T(128)} %bitcast.refs_0_, bf16[256,1024]{1,0:T(8,128)(2,1)} %copy-done.21, bf16[256,1024]{1,0:T(8,128)(2,1)} %copy-done.36, bf16[256,128]{1,0:T(8,128)(2,1)} %slice.93.refs_3_, bf16[256,1024]{1,0:T(8,128)(2,1)} %copy-done.22, ...), custom_call_target="tpu_custom_call" | custom-call | flops 22499999744 | bytes 64000000 | tf_op jit(solution)/shard_map/block/pallas_call | solution.py:197
  290.1 54.2 %block.11 = (bf16[512,3584]{1,0:T(8,128)(2,1)}, bf16[512,512]{1,0:T(8,128)(2,1)}, bf16[512,128]{1,0:T(8,128)(2,1)}) custom-call(s32[1]{0:T(128)} %bitcast.refs_0_, bf16[1536,1152]{1,0:T(8,128)(2,1)} %down.5.refs_1_, bf16[512,1152]{1,0:T(8,128)(2,1)} %collective-permute-done.3.refs_2_, bf16[512,1024]{1,0:T(8,128)(2,1)} %collective-permute-done.4.refs_3_, ...), custom_call_target="tpu_custom_call" | custom-call | flops 44999999488 | bytes 64000000 | tf_op jit(solution)/shard_map/block/pallas_call | solution.py:197
  346.3 11.1 down.6.refs_3_
  364.8 18.6 %down.7.refs_1_ = bf16[512,2176]{1,0:T(8,128)(2,1)} custom-call(s32[10]{0:T(128)} %stack.97.offs_ref, bf16[16,512,3584]{2,1,0:T(8,128)(2,1)} %h_ref.9, f32[8,512,1]{2,1,0:T(8,128)} %copy.32.rstd_ref, f32[1,3584]{1,0:T(1,128)} %reshape.51.g_ref, bf16[3584,384]{1,0:T(8,128)(2,1)} %rest_0_.7, bf16[3584,384]{1,0:T(8,128)(2,1)} %copy-done.1, ...), custom_call_target="tpu_custom_call" | custom-call | flops 7985954816 | bytes 19267584 | tf_op jit(solution)/shard_map/down/pallas_call | solution.py:57
  385.7 54.2 %block.12 = (bf16[512,3584]{1,0:T(8,128)(2,1)}, bf16[512,512]{1,0:T(8,128)(2,1)}, bf16[512,128]{1,0:T(8,128)(2,1)}) custom-call(s32[1]{0:T(128)} %bitcast.refs_0_, bf16[1536,1152]{1,0:T(8,128)(2,1)} %down.5.refs_1_, bf16[512,1152]{1,0:T(8,128)(2,1)} %collective-permute-done.22.refs_2_, bf16[512,1024]{1,0:T(8,128)(2,1)} %down.6.refs_3_, ...), custom_call_target="tpu_custom_call" | custom-call | flops 44999999488 | bytes 64000000 | tf_op jit(solution)/shard_map/block/pallas_call | solution.py:197
  441.9 18.5 %down.8.refs_1_ = bf16[512,2176]{1,0:T(8,128)(2,1)} custom-call(s32[10]{0:T(128)} %stack.107.offs_ref, bf16[16,512,3584]{2,1,0:T(8,128)(2,1)} %h_ref.9, f32[8,512,1]{2,1,0:T(8,128)} %copy.33.rstd_ref, f32[1,3584]{1,0:T(1,128)} %reshape.51.g_ref, bf16[3584,384]{1,0:T(8,128)(2,1)} %rest_0_.7, bf16[3584,384]{1,0:T(8,128)(2,1)} %copy-done.1, ...), custom_call_target="tpu_custom_call" | custom-call | flops 7985954816 | bytes 19267584 | tf_op jit(solution)/shard_map/down/pallas_call | solution.py:57
  462.9 54.2 %block.13 = (bf16[512,3584]{1,0:T(8,128)(2,1)}, bf16[512,512]{1,0:T(8,128)(2,1)}, bf16[512,128]{1,0:T(8,128)(2,1)}) custom-call(s32[1]{0:T(128)} %bitcast.refs_0_, bf16[512,2176]{1,0:T(8,128)(2,1)} %down.7.refs_1_, bf16[512,2176]{1,0:T(8,128)(2,1)} %copy-done.34, f32[1,1536]{1,0:T(1,128)} %bitcast.104, f32[1,512]{1,0:T(1,128)} %bitcast.113, ...), custom_call_target="tpu_custom_call" | custom-call | flops 44999999488 | bytes 64000000 | tf_op jit(solution)/shard_map/block/pallas_call | solution.py:197
  519.1 36.8 %down.9.refs_1_ = bf16[1536,2176]{1,0:T(8,128)(2,1)} custom-call(s32[10]{0:T(128)} %stack.95.offs_ref, bf16[16,512,3584]{2,1,0:T(8,128)(2,1)} %h_ref.9, f32[8,512,1]{2,1,0:T(8,128)} %copy.34.rstd_ref, f32[1,3584]{1,0:T(1,128)} %reshape.51.g_ref, bf16[3584,384]{1,0:T(8,128)(2,1)} %rest_0_.7, bf16[3584,384]{1,0:T(8,128)(2,1)} %copy-done.1, ...), custom_call_target="tpu_custom_call" | custom-call | flops 23957864448 | bytes 26607616 | tf_op jit(solution)/shard_map/down/pallas_call | solution.py:57
  555.8 5.5 fusion.23
  563.3 54.1 %block.14 = (bf16[512,3584]{1,0:T(8,128)(2,1)}, bf16[512,512]{1,0:T(8,128)(2,1)}, bf16[512,128]{1,0:T(8,128)(2,1)}) custom-call(s32[1]{0:T(128)} %bitcast.refs_0_, bf16[512,2176]{1,0:T(8,128)(2,1)} %down.8.refs_1_, bf16[512,2176]{1,0:T(8,128)(2,1)} %collective-permute-done.27.refs_2_, f32[1,1536]{1,0:T(1,128)} %bitcast.105, f32[1,512]{1,0:T(1,128)} %bitcast.114, ...), custom_call_target="tpu_custom_call" | custom-call | flops 44999999488 | bytes 64000000 | tf_op jit(solution)/shard_map/block/pallas_call | solution.py:197
  618.3 53.6 %block.15 = (bf16[512,3584]{1,0:T(8,128)(2,1)}, bf16[512,512]{1,0:T(8,128)(2,1)}, bf16[512,128]{1,0:T(8,128)(2,1)}) custom-call(s32[1]{0:T(128)} %bitcast.refs_0_, bf16[1536,2176]{1,0:T(8,128)(2,1)} %down.9.refs_1_, bf16[512,2176]{1,0:T(8,128)(2,1)} %collective-permute-done.26.refs_2_, f32[1,1536]{1,0:T(1,128)} %bitcast.106, f32[1,512]{1,0:T(1,128)} %bitcast.115, ...), custom_call_target="tpu_custom_call" | custom-call | flops 44999999488 | bytes 64000000 | tf_op jit(solution)/shard_map/block/pallas_call | solution.py:197
  671.9 53.8 %block.16 = (bf16[512,3584]{1,0:T(8,128)(2,1)}, bf16[512,512]{1,0:T(8,128)(2,1)}, bf16[512,128]{1,0:T(8,128)(2,1)}) custom-call(s32[1]{0:T(128)} %bitcast.refs_0_, bf16[1536,2176]{1,0:T(8,128)(2,1)} %down.9.refs_1_, bf16[512,2176]{1,0:T(8,128)(2,1)} %collective-permute-done.25.refs_2_, f32[1,1536]{1,0:T(1,128)} %bitcast.107, f32[1,512]{1,0:T(1,128)} %bitcast.116, ...), custom_call_target="tpu_custom_call" | custom-call | flops 44999999488 | bytes 64000000 | tf_op jit(solution)/shard_map/block/pallas_call | solution.py:197
  725.8 53.8 %block.17 = (bf16[512,3584]{1,0:T(8,128)(2,1)}, bf16[512,512]{1,0:T(8,128)(2,1)}, bf16[512,128]{1,0:T(8,128)(2,1)}) custom-call(s32[1]{0:T(128)} %bitcast.refs_0_, bf16[1536,2176]{1,0:T(8,128)(2,1)} %down.9.refs_1_, bf16[512,2176]{1,0:T(8,128)(2,1)} %collective-permute-done.24.refs_2_, f32[1,1536]{1,0:T(1,128)} %bitcast.108, f32[1,512]{1,0:T(1,128)} %bitcast.117, ...), custom_call_target="tpu_custom_call" | custom-call | flops 44999999488 | bytes 64000000 | tf_op jit(solution)/shard_map/block/pallas_call | solution.py:197
  779.6 5.1 constant_dynamic-update-slice_fusion.38
  785.8 4.5 constant_dynamic-update-slice_fusion.37
  790.6 3.0 constant_dynamic-update-slice_fusion.36
  793.6 7.6 constant_dynamic-update-slice_fusion.35
  805.3 61.9 %collective-permute-done.33 = bf16[512,3584]{1,0:T(8,128)(2,1)} collective-permute-done((bf16[512,3584]{1,0:T(8,128)(2,1)}, bf16[512,3584]{1,0:T(8,128)(2,1)}, u32[]{:S(2)}, u32[]{:S(2)}) %collective-permute-start.33) | collective-permute-done | bytes 3670048 | tf_op jit(solution)/shard_map/ppermute | solution.py:237
  867.2 7.6 constant_dynamic-update-slice_fusion.33
  876.0 4.1 constant_dynamic-update-slice_fusion.32
  880.1 65.8 %collective-permute-done.35 = bf16[512,3584]{1,0:T(8,128)(2,1)} collective-permute-done((bf16[512,3584]{1,0:T(8,128)(2,1)}, bf16[512,3584]{1,0:T(8,128)(2,1)}, u32[]{:S(2)}, u32[]{:S(2)}) %collective-permute-start.35) | collective-permute-done | bytes 3670048 | tf_op jit(solution)/shard_map/ppermute | solution.py:237
  945.8 8.6 constant_dynamic-update-slice_fusion.31
  955.6 4.1 constant_dynamic-update-slice_fusion.30
  959.8 64.7 %collective-permute-done.37 = bf16[512,3584]{1,0:T(8,128)(2,1)} collective-permute-done((bf16[512,3584]{1,0:T(8,128)(2,1)}, bf16[512,3584]{1,0:T(8,128)(2,1)}, u32[]{:S(2)}, u32[]{:S(2)}) %collective-permute-start.37) | collective-permute-done | bytes 3670048 | tf_op jit(solution)/shard_map/ppermute | solution.py:237
  1024.5 8.7 constant_dynamic-update-slice_fusion.29
  1038.0 4.1 constant_dynamic-update-slice_fusion.28
  1042.2 61.0 %collective-permute-done.39 = bf16[512,3584]{1,0:T(8,128)(2,1)} collective-permute-done((bf16[512,3584]{1,0:T(8,128)(2,1)}, bf16[512,3584]{1,0:T(8,128)(2,1)}, u32[]{:S(2)}, u32[]{:S(2)}) %collective-permute-start.39) | collective-permute-done | bytes 3670048 | tf_op jit(solution)/shard_map/ppermute | solution.py:237
  1103.1 8.6 constant_dynamic-update-slice_fusion.27
  1113.5 3.6 slice.83
  1120.5 4.3 constant_dynamic-update-slice_fusion.26
  1124.8 57.0 %collective-permute-done.41 = bf16[512,3584]{1,0:T(8,128)(2,1)} collective-permute-done((bf16[512,3584]{1,0:T(8,128)(2,1)}, bf16[512,3584]{1,0:T(8,128)(2,1)}, u32[]{:S(2)}, u32[]{:S(2)}) %collective-permute-start.41) | collective-permute-done | bytes 3670048 | tf_op jit(solution)/shard_map/ppermute | solution.py:237
  1181.8 7.8 constant_dynamic-update-slice_fusion.25
  1190.0 4.3 constant_dynamic-update-slice_fusion.24
  1194.3 46.0 %collective-permute-done.43 = bf16[384,3584]{1,0:T(8,128)(2,1)} collective-permute-done((bf16[384,3584]{1,0:T(8,128)(2,1)}, bf16[384,3584]{1,0:T(8,128)(2,1)}, u32[]{:S(2)}, u32[]{:S(2)}) %collective-permute-start.43) | collective-permute-done | bytes 2752544 | tf_op jit(solution)/shard_map/ppermute | solution.py:237
  1240.3 6.0 constant_dynamic-update-slice_fusion.23
  1259.4 4.1 constant_dynamic-update-slice_fusion.22
  1263.6 7.5 collective-permute-done.45
  1271.1 3.0 constant_dynamic-update-slice_fusion.21
  1279.8 3.5 constant_dynamic-update-slice_fusion.20
  (239 shorter events, 110.4 us)
Async XLA Ops:
  0.6 215.5 %collective-permute-start.14 = (bf16[16,128,3584]{2,1,0:T(8,128)(2,1)}, bf16[16,128,3584]{2,1,0:T(8,128)(2,1)}, u32[]{:S(2)}, u32[]{:S(2)}) collective-permute-start(bf16[16,128,3584]{2,1,0:T(8,128)(2,1)} %param.21), channel_id=1, source_target_pairs={{0,1},{1,0},{2,3},{3,2},{4,5},{5,4},{6,7},{7,6}} | collective-permute-start | bytes 44040200 | tf_op jit(solution)/shard_map/ppermute | solution.py:234
  1.5 101.6 %collective-permute-start.10 = (bf16[1536,16,192]{0,2,1:T(8,128)(2,1)}, bf16[1536,16,192]{0,2,1:T(8,128)(2,1)}, u32[]{:S(2)}, u32[]{:S(2)}) collective-permute-start(bf16[1536,16,192]{0,2,1:T(8,128)(2,1)} %param.18), channel_id=1, source_target_pairs={{0,1},{1,0},{2,3},{3,2},{4,5},{5,4},{6,7},{7,6}} | collective-permute-start | bytes 28311560 | tf_op jit(solution)/shard_map/ppermute | solution.py:234
  1.5 41.2 %collective-permute-start.1 = (bf16[3584,384]{1,0:T(8,128)(2,1)}, bf16[3584,384]{1,0:T(8,128)(2,1)S(1)}, u32[]{:S(2)}, u32[]{:S(2)}) collective-permute-start(bf16[3584,384]{1,0:T(8,128)(2,1)} %rest_0_.7), channel_id=1, source_target_pairs={{0,1},{1,0},{2,3},{3,2},{4,5},{5,4},{6,7},{7,6}} | collective-permute-start | bytes 8257544 | tf_op jit(solution)/shard_map/ppermute | solution.py:234
  12.4 8.9 collective-permute-start
  15.0 27.4 %collective-permute-start.2 = (bf16[3584,128]{1,0:T(8,128)(2,1)}, bf16[3584,128]{1,0:T(8,128)(2,1)}, u32[]{:S(2)}, u32[]{:S(2)}) collective-permute-start(bf16[3584,128]{1,0:T(8,128)(2,1)} %rest_4_.5), channel_id=1, source_target_pairs={{0,1},{1,0},{2,3},{3,2},{4,5},{5,4},{6,7},{7,6}} | collective-permute-start | bytes 2752520 | tf_op jit(solution)/shard_map/ppermute | solution.py:234
  21.3 81.2 %collective-permute-start.11 = (bf16[512,16,128]{2,1,0:T(8,128)(2,1)}, bf16[512,16,128]{2,1,0:T(8,128)(2,1)}, u32[]{:S(2)}, u32[]{:S(2)}) collective-permute-start(bf16[512,16,128]{2,1,0:T(8,128)(2,1)} %param.19), channel_id=1, source_target_pairs={{0,1},{1,0},{2,3},{3,2},{4,5},{5,4},{6,7},{7,6}} | collective-permute-start | bytes 6291464 | tf_op jit(solution)/shard_map/ppermute | solution.py:234
  42.4 60.7 %collective-permute-start.12 = (bf16[512,16,128]{2,1,0:T(8,128)(2,1)}, bf16[512,16,128]{2,1,0:T(8,128)(2,1)}, u32[]{:S(2)}, u32[]{:S(2)}) collective-permute-start(bf16[512,16,128]{2,1,0:T(8,128)(2,1)} %param.20), channel_id=1, source_target_pairs={{0,1},{1,0},{2,3},{3,2},{4,5},{5,4},{6,7},{7,6}} | collective-permute-start | bytes 6291464 | tf_op jit(solution)/shard_map/ppermute | solution.py:234
  69.0 16.8 %collective-permute-start.5 = (bf16[256,1152]{1,0:T(8,128)(2,1)}, bf16[256,1152]{1,0:T(8,128)(2,1)}, u32[]{:S(2)}, u32[]{:S(2)}) collective-permute-start(bf16[256,1152]{1,0:T(8,128)(2,1)} %get-tuple-element.142), channel_id=1, source_target_pairs={{0,4},{4,0},{1,5},{5,1},{2,6},{6,2},{3,7},{7,3}} | collective-permute-start | bytes 1769480 | tf_op jit(solution)/shard_map/ppermute | solution.py:240
  85.8 15.2 %collective-permute-start.16 = (bf16[256,1152]{1,0:T(8,128)(2,1)}, bf16[256,1152]{1,0:T(8,128)(2,1)S(1)}, u32[]{:S(2)}, u32[]{:S(2)}) collective-permute-start(bf16[256,1152]{1,0:T(8,128)(2,1)} %get-tuple-element.141), channel_id=1, source_target_pairs={{0,4},{4,0},{1,5},{5,1},{2,6},{6,2},{3,7},{7,3}} | collective-permute-start | bytes 1769480 | tf_op jit(solution)/shard_map/ppermute | solution.py:240
  101.0 64.0 %collective-permute-start.9 = (bf16[3584,384]{1,0:T(8,128)(2,1)S(1)}, bf16[3584,384]{1,0:T(8,128)(2,1)S(1)}, u32[]{:S(2)}, u32[]{:S(2)}) collective-permute-start(bf16[3584,384]{1,0:T(8,128)(2,1)S(1)} %copy-done), channel_id=1, source_target_pairs={{0,2},{2,0},{1,3},{3,1},{4,6},{6,4},{5,7},{7,5}} | collective-permute-start | bytes 8257544 | tf_op jit(solution)/shard_map/ppermute | solution.py:237
  102.5 61.1 %collective-permute-start.8 = (bf16[1,512]{1,0:T(2,128)(2,1)S(1)}, bf16[1,512]{1,0:T(2,128)(2,1)S(1)}, u32[]{:S(2)}, u32[]{:S(2)}) collective-permute-start(bf16[1,512]{1,0:T(2,128)(2,1)S(1)} %copy-done.33), channel_id=1, source_target_pairs={{0,2},{2,0},{1,3},{3,1},{4,6},{6,4},{5,7},{7,5}} | collective-permute-start | bytes 3080 | tf_op jit(solution)/shard_map/ppermute | solution.py:237
  103.1 65.2 %collective-permute-start.7 = (bf16[1,512]{1,0:T(2,128)(2,1)S(1)}, bf16[1,512]{1,0:T(2,128)(2,1)S(1)}, u32[]{:S(2)}, u32[]{:S(2)}) collective-permute-start(bf16[1,512]{1,0:T(2,128)(2,1)S(1)} %copy-done.33), channel_id=1, source_target_pairs={{0,1},{1,0},{2,3},{3,2},{4,5},{5,4},{6,7},{7,6}} | collective-permute-start | bytes 3080 | tf_op jit(solution)/shard_map/ppermute | solution.py:234
  103.1 186.8 %collective-permute-start.19 = (bf16[3584,128]{1,0:T(8,128)(2,1)}, bf16[3584,128]{1,0:T(8,128)(2,1)}, u32[]{:S(2)}, u32[]{:S(2)}) collective-permute-start(bf16[3584,128]{1,0:T(8,128)(2,1)} %rest_4_.5), channel_id=1, source_target_pairs={{0,2},{2,0},{1,3},{3,1},{4,6},{6,4},{5,7},{7,5}} | collective-permute-start | bytes 2752520 | tf_op jit(solution)/shard_map/ppermute | solution.py:237
  163.6 87.2 %collective-permute-start.4 = (bf16[512,1024]{1,0:T(8,128)(2,1)}, bf16[512,1024]{1,0:T(8,128)(2,1)}, u32[]{:S(2)}, u32[]{:S(2)}) collective-permute-start(bf16[512,1024]{1,0:T(8,128)(2,1)} %slice.90), channel_id=1, source_target_pairs={{0,2},{2,0},{1,3},{3,1},{4,6},{6,4},{5,7},{7,5}} | collective-permute-start | bytes 3145736 | tf_op jit(solution)/shard_map/ppermute | solution.py:237
  168.3 121.8 %collective-permute-start.3 = (bf16[512,1152]{1,0:T(8,128)(2,1)}, bf16[512,1152]{1,0:T(8,128)(2,1)}, u32[]{:S(2)}, u32[]{:S(2)}) collective-permute-start(bf16[512,1152]{1,0:T(8,128)(2,1)} %get-tuple-element.140), channel_id=1, source_target_pairs={{0,4},{4,0},{1,5},{5,1},{2,6},{6,2},{3,7},{7,3}} | collective-permute-start | bytes 3538952 | tf_op jit(solution)/shard_map/ppermute | solution.py:240
  169.8 45.1 %collective-permute-start.6 = (bf16[256,1024]{1,0:T(8,128)(2,1)S(1)}, bf16[256,1024]{1,0:T(8,128)(2,1)S(1)}, u32[]{:S(2)}, u32[]{:S(2)}) collective-permute-start(bf16[256,1024]{1,0:T(8,128)(2,1)S(1)} %slice.92.refs_1_), channel_id=1, source_target_pairs={{0,2},{2,0},{1,3},{3,1},{4,6},{6,4},{5,7},{7,5}} | collective-permute-start | bytes 1572872 | tf_op jit(solution)/shard_map/ppermute | solution.py:237
  215.0 168.9 %collective-permute-start.22 = (bf16[512,1152]{1,0:T(8,128)(2,1)}, bf16[512,1152]{1,0:T(8,128)(2,1)}, u32[]{:S(2)}, u32[]{:S(2)}) collective-permute-start(bf16[512,1152]{1,0:T(8,128)(2,1)} %get-tuple-element.139), channel_id=1, source_target_pairs={{0,4},{4,0},{1,5},{5,1},{2,6},{6,2},{3,7},{7,3}} | collective-permute-start | bytes 3538952 | tf_op jit(solution)/shard_map/ppermute | solution.py:240
  216.2 34.7 %collective-permute-start.17 = (bf16[256,1024]{1,0:T(8,128)(2,1)S(1)}, bf16[256,1024]{1,0:T(8,128)(2,1)}, u32[]{:S(2)}, u32[]{:S(2)}) collective-permute-start(bf16[256,1024]{1,0:T(8,128)(2,1)S(1)} %slice.96.refs_4_), channel_id=1, source_target_pairs={{0,2},{2,0},{1,3},{3,1},{4,6},{6,4},{5,7},{7,5}} | collective-permute-start | bytes 1572872 | tf_op jit(solution)/shard_map/ppermute | solution.py:237
  250.8 95.5 %collective-permute-start.18 = (bf16[3584,384]{1,0:T(8,128)(2,1)S(1)}, bf16[3584,384]{1,0:T(8,128)(2,1)}, u32[]{:S(2)}, u32[]{:S(2)}) collective-permute-start(bf16[3584,384]{1,0:T(8,128)(2,1)S(1)} %copy-done.3), channel_id=1, source_target_pairs={{0,1},{1,0},{2,3},{3,2},{4,5},{5,4},{6,7},{7,6}} | collective-permute-start | bytes 8257544 | tf_op jit(solution)/shard_map/ppermute | solution.py:234
  250.9 39.2 %collective-permute-start.15 = (bf16[512,1024]{1,0:T(8,128)(2,1)}, bf16[512,1024]{1,0:T(8,128)(2,1)}, u32[]{:S(2)}, u32[]{:S(2)}) collective-permute-start(bf16[512,1024]{1,0:T(8,128)(2,1)} %collective-permute-done.4.refs_3_), channel_id=1, source_target_pairs={{0,4},{4,0},{1,5},{5,1},{2,6},{6,2},{3,7},{7,3}} | collective-permute-start | bytes 3145736 | tf_op jit(solution)/shard_map/ppermute | solution.py:240
  289.9 56.4 %collective-permute-start.20 = (bf16[3584,128]{1,0:T(8,128)(2,1)}, bf16[3584,128]{1,0:T(8,128)(2,1)}, u32[]{:S(2)}, u32[]{:S(2)}) collective-permute-start(bf16[3584,128]{1,0:T(8,128)(2,1)} %collective-permute-done.19.rest_2_.rest_6_), channel_id=1, source_target_pairs={{0,1},{1,0},{2,3},{3,2},{4,5},{5,4},{6,7},{7,6}} | collective-permute-start | bytes 2752520 | tf_op jit(solution)/shard_map/ppermute | solution.py:234
  357.4 27.4 %collective-permute-start.23 = (bf16[512,1024]{1,0:T(8,128)(2,1)}, bf16[512,1024]{1,0:T(8,128)(2,1)S(1)}, u32[]{:S(2)}, u32[]{:S(2)}) collective-permute-start(bf16[512,1024]{1,0:T(8,128)(2,1)} %down.6.refs_3_), channel_id=1, source_target_pairs={{0,4},{4,0},{1,5},{5,1},{2,6},{6,2},{3,7},{7,3}} | collective-permute-start | bytes 3145736 | tf_op jit(solution)/shard_map/ppermute | solution.py:240
  360.8 418.7 %collective-permute-start.28 = (bf16[256,3584]{1,0:T(8,128)(2,1)}, bf16[256,3584]{1,0:T(8,128)(2,1)}, u32[]{:S(2)}, u32[]{:S(2)}) collective-permute-start(bf16[256,3584]{1,0:T(8,128)(2,1)} %get-tuple-element.63), channel_id=1, source_target_pairs={{0,2},{2,0},{1,3},{3,1},{4,6},{6,4},{5,7},{7,5}} | collective-permute-start | bytes 5505032 | tf_op jit(solution)/shard_map/ppermute | solution.py:237
  361.4 424.5 %collective-permute-start.29 = (bf16[256,3584]{1,0:T(8,128)(2,1)}, bf16[256,3584]{1,0:T(8,128)(2,1)}, u32[]{:S(2)}, u32[]{:S(2)}) collective-permute-start(bf16[256,3584]{1,0:T(8,128)(2,1)} %get-tuple-element.67), channel_id=1, source_target_pairs={{0,2},{2,0},{1,3},{3,1},{4,6},{6,4},{5,7},{7,5}} | collective-permute-start | bytes 5505032 | tf_op jit(solution)/shard_map/ppermute | solution.py:237
  383.4 78.2 %collective-permute-start.21 = (bf16[512,2176]{1,0:T(8,128)(2,1)}, bf16[512,2176]{1,0:T(8,128)(2,1)S(1)}, u32[]{:S(2)}, u32[]{:S(2)}) collective-permute-start(bf16[512,2176]{1,0:T(8,128)(2,1)} %down.7.refs_1_), channel_id=1, source_target_pairs={{0,4},{4,0},{1,5},{5,1},{2,6},{6,2},{3,7},{7,3}} | collective-permute-start | bytes 6684680 | tf_op jit(solution)/shard_map/ppermute | solution.py:240
  383.9 409.7 %collective-permute-start.31 = (bf16[512,3584]{1,0:T(8,128)(2,1)}, bf16[512,3584]{1,0:T(8,128)(2,1)}, u32[]{:S(2)}, u32[]{:S(2)}) collective-permute-start(bf16[512,3584]{1,0:T(8,128)(2,1)} %get-tuple-element.69), channel_id=1, source_target_pairs={{0,2},{2,0},{1,3},{3,1},{4,6},{6,4},{5,7},{7,5}} | collective-permute-start | bytes 11010056 | tf_op jit(solution)/shard_map/ppermute | solution.py:237
  460.3 101.8 %collective-permute-start.27 = (bf16[512,2176]{1,0:T(8,128)(2,1)}, bf16[512,2176]{1,0:T(8,128)(2,1)}, u32[]{:S(2)}, u32[]{:S(2)}) collective-permute-start(bf16[512,2176]{1,0:T(8,128)(2,1)} %down.8.refs_1_), channel_id=1, source_target_pairs={{0,4},{4,0},{1,5},{5,1},{2,6},{6,2},{3,7},{7,3}} | collective-permute-start | bytes 6684680 | tf_op jit(solution)/shard_map/ppermute | solution.py:240
  561.3 56.1 %collective-permute-start.26 = (bf16[512,2176]{1,0:T(8,128)(2,1)}, bf16[512,2176]{1,0:T(8,128)(2,1)}, u32[]{:S(2)}, u32[]{:S(2)}) collective-permute-start(bf16[512,2176]{1,0:T(8,128)(2,1)} %get-tuple-element.134), channel_id=1, source_target_pairs={{0,4},{4,0},{1,5},{5,1},{2,6},{6,2},{3,7},{7,3}} | collective-permute-start | bytes 6684680 | tf_op jit(solution)/shard_map/ppermute | solution.py:240
  562.1 109.8 %collective-permute-start.25 = (bf16[512,2176]{1,0:T(8,128)(2,1)}, bf16[512,2176]{1,0:T(8,128)(2,1)}, u32[]{:S(2)}, u32[]{:S(2)}) collective-permute-start(bf16[512,2176]{1,0:T(8,128)(2,1)} %get-tuple-element.135), channel_id=1, source_target_pairs={{0,4},{4,0},{1,5},{5,1},{2,6},{6,2},{3,7},{7,3}} | collective-permute-start | bytes 6684680 | tf_op jit(solution)/shard_map/ppermute | solution.py:240
  617.4 108.3 %collective-permute-start.24 = (bf16[512,2176]{1,0:T(8,128)(2,1)S(1)}, bf16[512,2176]{1,0:T(8,128)(2,1)}, u32[]{:S(2)}, u32[]{:S(2)}) collective-permute-start(bf16[512,2176]{1,0:T(8,128)(2,1)S(1)} %get-tuple-element.136), channel_id=1, source_target_pairs={{0,4},{4,0},{1,5},{5,1},{2,6},{6,2},{3,7},{7,3}} | collective-permute-start | bytes 6684680 | tf_op jit(solution)/shard_map/ppermute | solution.py:240
  784.7 82.5 %collective-permute-start.33 = (bf16[512,3584]{1,0:T(8,128)(2,1)}, bf16[512,3584]{1,0:T(8,128)(2,1)}, u32[]{:S(2)}, u32[]{:S(2)}) collective-permute-start(bf16[512,3584]{1,0:T(8,128)(2,1)} %get-tuple-element.75), channel_id=1, source_target_pairs={{0,2},{2,0},{1,3},{3,1},{4,6},{6,4},{5,7},{7,5}} | collective-permute-start | bytes 11010056 | tf_op jit(solution)/shard_map/ppermute | solution.py:237
  790.3 12.0 collective-permute-start.32
  801.1 74.8 %collective-permute-start.34 = (bf16[1,512,3584]{2,1,0:T(8,128)(2,1)}, bf16[1,512,3584]{2,1,0:T(8,128)(2,1)}, u32[]{:S(2)}, u32[]{:S(2)}) collective-permute-start(bf16[1,512,3584]{2,1,0:T(8,128)(2,1)} %get-tuple-element.129), channel_id=1, source_target_pairs={{0,1},{1,0},{2,3},{3,2},{4,5},{5,4},{6,7},{7,6}} | collective-permute-start | bytes 11010056 | tf_op jit(solution)/shard_map/ppermute | solution.py:234
  801.4 144.4 %collective-permute-start.35 = (bf16[512,3584]{1,0:T(8,128)(2,1)}, bf16[512,3584]{1,0:T(8,128)(2,1)}, u32[]{:S(2)}, u32[]{:S(2)}) collective-permute-start(bf16[512,3584]{1,0:T(8,128)(2,1)} %get-tuple-element.78), channel_id=1, source_target_pairs={{0,2},{2,0},{1,3},{3,1},{4,6},{6,4},{5,7},{7,5}} | collective-permute-start | bytes 11010056 | tf_op jit(solution)/shard_map/ppermute | solution.py:237
  874.8 80.9 %collective-permute-start.36 = (bf16[1,512,3584]{2,1,0:T(8,128)(2,1)}, bf16[1,512,3584]{2,1,0:T(8,128)(2,1)}, u32[]{:S(2)}, u32[]{:S(2)}) collective-permute-start(bf16[1,512,3584]{2,1,0:T(8,128)(2,1)} %get-tuple-element.127), channel_id=1, source_target_pairs={{0,1},{1,0},{2,3},{3,2},{4,5},{5,4},{6,7},{7,6}} | collective-permute-start | bytes 11010056 | tf_op jit(solution)/shard_map/ppermute | solution.py:234
  874.8 149.7 %collective-permute-start.37 = (bf16[512,3584]{1,0:T(8,128)(2,1)}, bf16[512,3584]{1,0:T(8,128)(2,1)}, u32[]{:S(2)}, u32[]{:S(2)}) collective-permute-start(bf16[512,3584]{1,0:T(8,128)(2,1)} %get-tuple-element.81), channel_id=1, source_target_pairs={{0,2},{2,0},{1,3},{3,1},{4,6},{6,4},{5,7},{7,5}} | collective-permute-start | bytes 11010056 | tf_op jit(solution)/shard_map/ppermute | solution.py:237
  954.5 83.6 %collective-permute-start.38 = (bf16[1,512,3584]{2,1,0:T(8,128)(2,1)}, bf16[1,512,3584]{2,1,0:T(8,128)(2,1)}, u32[]{:S(2)}, u32[]{:S(2)}) collective-permute-start(bf16[1,512,3584]{2,1,0:T(8,128)(2,1)} %get-tuple-element.125), channel_id=1, source_target_pairs={{0,1},{1,0},{2,3},{3,2},{4,5},{5,4},{6,7},{7,6}} | collective-permute-start | bytes 11010056 | tf_op jit(solution)/shard_map/ppermute | solution.py:234
  954.5 148.7 %collective-permute-start.39 = (bf16[512,3584]{1,0:T(8,128)(2,1)}, bf16[512,3584]{1,0:T(8,128)(2,1)}, u32[]{:S(2)}, u32[]{:S(2)}) collective-permute-start(bf16[512,3584]{1,0:T(8,128)(2,1)} %get-tuple-element.83), channel_id=1, source_target_pairs={{0,2},{2,0},{1,3},{3,1},{4,6},{6,4},{5,7},{7,5}} | collective-permute-start | bytes 11010056 | tf_op jit(solution)/shard_map/ppermute | solution.py:237
  1033.2 87.3 %collective-permute-start.40 = (bf16[1,512,3584]{2,1,0:T(8,128)(2,1)}, bf16[1,512,3584]{2,1,0:T(8,128)(2,1)}, u32[]{:S(2)}, u32[]{:S(2)}) collective-permute-start(bf16[1,512,3584]{2,1,0:T(8,128)(2,1)} %get-tuple-element.123), channel_id=1, source_target_pairs={{0,1},{1,0},{2,3},{3,2},{4,5},{5,4},{6,7},{7,6}} | collective-permute-start | bytes 11010056 | tf_op jit(solution)/shard_map/ppermute | solution.py:234
  1035.1 146.6 %collective-permute-start.41 = (bf16[512,3584]{1,0:T(8,128)(2,1)}, bf16[512,3584]{1,0:T(8,128)(2,1)}, u32[]{:S(2)}, u32[]{:S(2)}) collective-permute-start(bf16[512,3584]{1,0:T(8,128)(2,1)} %get-tuple-element.85), channel_id=1, source_target_pairs={{0,2},{2,0},{1,3},{3,1},{4,6},{6,4},{5,7},{7,5}} | collective-permute-start | bytes 11010056 | tf_op jit(solution)/shard_map/ppermute | solution.py:237
  1111.8 78.2 %collective-permute-start.42 = (bf16[1,512,3584]{2,1,0:T(8,128)(2,1)}, bf16[1,512,3584]{2,1,0:T(8,128)(2,1)}, u32[]{:S(2)}, u32[]{:S(2)}) collective-permute-start(bf16[1,512,3584]{2,1,0:T(8,128)(2,1)} %get-tuple-element.121), channel_id=1, source_target_pairs={{0,1},{1,0},{2,3},{3,2},{4,5},{5,4},{6,7},{7,6}} | collective-permute-start | bytes 11010056 | tf_op jit(solution)/shard_map/ppermute | solution.py:234
  1119.2 121.1 %collective-permute-start.43 = (bf16[384,3584]{1,0:T(8,128)(2,1)}, bf16[384,3584]{1,0:T(8,128)(2,1)}, u32[]{:S(2)}, u32[]{:S(2)}) collective-permute-start(bf16[384,3584]{1,0:T(8,128)(2,1)} %slice.83), channel_id=1, source_target_pairs={{0,2},{2,0},{1,3},{3,1},{4,6},{6,4},{5,7},{7,5}} | collective-permute-start | bytes 8257544 | tf_op jit(solution)/shard_map/ppermute | solution.py:237
  1189.6 68.5 %collective-permute-start.44 = (bf16[1,512,3584]{2,1,0:T(8,128)(2,1)}, bf16[1,512,3584]{2,1,0:T(8,128)(2,1)}, u32[]{:S(2)}, u32[]{:S(2)}) collective-permute-start(bf16[1,512,3584]{2,1,0:T(8,128)(2,1)} %get-tuple-element.119), channel_id=1, source_target_pairs={{0,1},{1,0},{2,3},{3,2},{4,5},{5,4},{6,7},{7,6}} | collective-permute-start | bytes 11010056 | tf_op jit(solution)/shard_map/ppermute | solution.py:234
  1246.4 33.5 %collective-permute-start.46 = (bf16[1,384,3584]{2,1,0:T(8,128)(2,1)}, bf16[1,384,3584]{2,1,0:T(8,128)(2,1)}, u32[]{:S(2)}, u32[]{:S(2)}) collective-permute-start(bf16[1,384,3584]{2,1,0:T(8,128)(2,1)} %get-tuple-element.117), channel_id=1, source_target_pairs={{0,1},{1,0},{2,3},{3,2},{4,5},{5,4},{6,7},{7,6}} | collective-permute-start | bytes 8257544 | tf_op jit(solution)/shard_map/ppermute | solution.py:234
  1248.1 26.1 %collective-permute-start.49 = (bf16[8,512,64]{1,2,0:T(8,128)(2,1)}, bf16[8,512,64]{1,2,0:T(8,128)(2,1)}, u32[]{:S(2)}, u32[]{:S(2)}) collective-permute-start(bf16[8,512,64]{1,2,0:T(8,128)(2,1)} %copy.35), channel_id=1, source_target_pairs={{0,1},{1,0},{2,3},{3,2},{4,5},{5,4},{6,7},{7,6}} | collective-permute-start | bytes 1572872 | tf_op jit(solution)/shard_map/ppermute | solution.py:234
  1248.6 22.5 %collective-permute-start.45 = (bf16[128,3584]{1,0:T(8,128)(2,1)}, bf16[128,3584]{1,0:T(8,128)(2,1)S(1)}, u32[]{:S(2)}, u32[]{:S(2)}) collective-permute-start(bf16[128,3584]{1,0:T(8,128)(2,1)} %slice.84), channel_id=1, source_target_pairs={{0,2},{2,0},{1,3},{3,1},{4,6},{6,4},{5,7},{7,5}} | collective-permute-start | bytes 2752520 | tf_op jit(solution)/shard_map/ppermute | solution.py:237
  1258.1 19.4 %collective-permute-start.48 = (bf16[8,512,128]{2,1,0:T(8,128)(2,1)}, bf16[8,512,128]{2,1,0:T(8,128)(2,1)}, u32[]{:S(2)}, u32[]{:S(2)}) collective-permute-start(bf16[8,512,128]{2,1,0:T(8,128)(2,1)} %get-tuple-element.137), channel_id=1, source_target_pairs={{0,1},{1,0},{2,3},{3,2},{4,5},{5,4},{6,7},{7,6}} | collective-permute-start | bytes 3145736 | tf_op jit(solution)/shard_map/ppermute | solution.py:234
  1274.1 9.2 collective-permute-start.47
  (42 other events, 837.7 us)

commit v3 on v2

--- a/solution.py
+++ b/solution.py
@@ -188,8 +188,8 @@
     in_rows = seq // 2 if mode == "sum2" else seq
     n_heads, qk, q_lora = wq.shape
     kv_lora, depth, width = wkv.shape[0], wo_a.shape[0], wo_a.shape[1]
-    heads, wide = 4, 512
-    steps, out_steps = n_heads // heads, width // wide
+    heads, wide, cols = 8, 1024, 512
+    steps, out_steps = n_heads // heads, width // cols
     once = pl.Buffered(1)
     hd = lambda j: jnp.minimum(j, steps - 1)
     oc = lambda j: jnp.maximum(j - steps, 0)
@@ -204,11 +204,11 @@
                 pl.BlockSpec((heads, qk, q_lora), lambda j, o: (hd(j), 0, 0)),
                 pl.BlockSpec((kv_lora, wide), lambda j, o: (0, hd(j))),
                 pl.BlockSpec((kv_lora, wide), lambda j, o: (0, steps + hd(j))),
-                pl.BlockSpec((depth, wide), lambda j, o: (0, oc(j))),
-                pl.BlockSpec((depth, wide), lambda j, o: (0, oc(j))),
+                pl.BlockSpec((depth, cols), lambda j, o: (0, oc(j))),
+                pl.BlockSpec((depth, cols), lambda j, o: (0, oc(j))),
             ],
             out_specs=[
-                pl.BlockSpec((q_rows, wide), lambda j, o: (0, oc(j))),
+                pl.BlockSpec((q_rows, cols), lambda j, o: (0, oc(j))),
                 pl.BlockSpec((seq, kv_lora), lambda j, o: (0, 0)),
                 pl.BlockSpec((seq, 128), lambda j, o: (0, 0)),
             ],
@@ -327,11 +327,13 @@
         send(0, hs, part)
         ckvs.append(ckv)
         kks.append(kk)
-        far_kv = after(far_kv, part)
+        far_kv = after(far_kv, part_a)
         diag_kv = swap(far_kv)
         every = [w_dq, near_q, far_q, diag_q, w_dkv, near_kv, far_kv, diag_kv, w_kr2]
         lows = {1: ("pair", (low_own, own_in[2], low_x, low_xy), (1, 0, 0, 0))}
         last = part
+        last = down(hidden, rstd, g_row, 2, 1, after(base, last), [far_q, diag_q, far_kv, diag_kv], near_offs)
+        lows[2] = ("pair", (low_own, own_in[3], last, emb_swap(last)), (2, 0, 0, 0))
         for i in range(1, half):
             mode, ins, at = lows[i]
             part, ckv, kk = run(mode, ins, at, 0, seq, last)
@@ -340,11 +342,8 @@
             last = part
             for lo, hi in PIECES.get(i, ((0, seq),)):
                 send(i, lo, part[lo:hi])
-            if i == 1:
-                last = down(hidden, after(rstd, last), g_row, 2, 1, base, [far_q, diag_q, far_kv, diag_kv], near_offs)
-                lows[2] = ("pair", (low_own, own_in[3], last, emb_swap(last)), (2, 0, 0, 0))
             for first, n in DOWNS.get(i, ()):
-                low = down(hidden, after(rstd, last), g_row, first, n, base, every, every_offs)
+                low = down(hidden, rstd, g_row, first, n, after(base, last), every, every_offs)
                 last = low
                 for r in range(n):
                     lows[first + r] = ("full", (low, emb_swap(rows_of(low, r))), (r, 0))

time: 1290 us -> 1290 us (level)
  transfers between devices with their start and end apart: 50 -> 50, of which waited for: 12 -> 12; matrix products, arithmetic and copies ran while one was open for 15% -> 14% of each run, Pallas kernels for 43% -> 44%
where the time goes in v3:
time: 1290 us; the launch traced here: 1280 us
  Pallas kernels  556 us (43%)
  waiting for transfers between devices  490 us (38%)
  other arithmetic  98.6 us (8%)
  local copies, waits for them, and re-layouts  94.7 us (7%)
  starting transfers between devices  37.4 us (3%)
    ppermute x16, waiting for transfers between devices, cross(): return lax.ppermute(v, 'head', ACROSS)  451 us
    pallas_call x9, Pallas kernels, head_block(): pl.pallas_call(lambda *refs: block_kernel(scale, mode, q_lo, *refs), grid...  448 us
    pallas_call x5, Pallas kernels, down(): pl.pallas_call(down_kernel, grid_spec=pltpu.PrefetchScalarGridSpec(num_sc...  109 us
    dynamic_update_slice x10, other arithmetic, block(): lax.dynamic_update_slice(result, out_i, (base + i, 0 * base + lo, 0 * base))  67.7 us
    dynamic_update_slice x10, local copies, waits for them, and re-layouts, place(): lax.dynamic_update_slice(result, other, (half - base + i, 0 * base + lo,...  35 us
  transfers between devices with their start and end apart: 50, of which 12 were waited for; matrix products, arithmetic and copies ran while one was open for 14% of the time, Pallas kernels for 44%

profile of v3, /device:TPU:0, one launch (start us, length us, event | category | flops | bytes accessed | tf_op | source)
XLA Modules:
  0.0 1278.3 jit_solution(1004336909148303068)
XLA Ops:
  2.0 10.4 multiply_reduce_fusion
  24.3 18.0 %collective-permute-done.2.rest_3_.rest_5_ = bf16[3584,128]{1,0:T(8,128)(2,1)} collective-permute-done((bf16[3584,128]{1,0:T(8,128)(2,1)}, bf16[3584,128]{1,0:T(8,128)(2,1)}, u32[]{:S(2)}, u32[]{:S(2)}) %collective-permute-start.2) | collective-permute-done | bytes 917536 | tf_op jit(solution)/shard_map/ppermute | solution.py:234
  44.3 22.3 %down.5.refs_1_ = bf16[1536,1152]{1,0:T(8,128)(2,1)} custom-call(s32[6]{0:T(128)} %stack.91.offs_ref, bf16[16,512,3584]{2,1,0:T(8,128)(2,1)} %h_ref.9, f32[8,512,1]{2,1,0:T(8,128)} %copy.30.rstd_ref, f32[1,3584]{1,0:T(1,128)} %reshape.51.g_ref, bf16[3584,384]{1,0:T(8,128)(2,1)} %rest_0_.7, bf16[3584,384]{1,0:T(8,128)(2,1)} %copy-done.1, ...), custom_call_target="tpu_custom_call" | custom-call | flops 12683575296 | bytes 19267584 | tf_op jit(solution)/shard_map/down/pallas_call | solution.py:57
  74.1 11.8 collective-permute-done.5
  92.0 9.0 collective-permute-done.16
  110.1 13.3 %pad_maximum_fusion.refs_8_.refs_11_.refs_9_.refs_7_ = bf16[32,192,1536]{2,1,0:T(8,128)(2,1)} fusion(bf16[16,192,1536]{2,1,0:T(8,128)(2,1)} %bitcast.8, bf16[16,192,1536]{2,1,0:T(8,128)(2,1)S(1)} %bitcast.97), kind=kLoop, calls=%fused_computation.1 | loop fusion | flops 9437184 | bytes 37748736 | tf_op jit(solution)/shard_map/concatenate | solution.py:286
  123.4 40.4 %collective-permute-done.8 = bf16[1,512]{1,0:T(2,128)(2,1)S(1)} collective-permute-done((bf16[1,512]{1,0:T(2,128)(2,1)S(1)}, bf16[1,512]{1,0:T(2,128)(2,1)S(1)}, u32[]{:S(2)}, u32[]{:S(2)}) %collective-permute-start.8) | collective-permute-done | bytes 1056 | tf_op jit(solution)/shard_map/ppermute | solution.py:237
  170.1 44.8 %collective-permute-done.6.refs_2_ = bf16[256,1024]{1,0:T(8,128)(2,1)S(1)} collective-permute-done((bf16[256,1024]{1,0:T(8,128)(2,1)S(1)}, bf16[256,1024]{1,0:T(8,128)(2,1)S(1)}, u32[]{:S(2)}, u32[]{:S(2)}) %collective-permute-start.6) | collective-permute-done | bytes 524320 | tf_op jit(solution)/shard_map/ppermute | solution.py:237
  216.1 32.7 %block.9 = (bf16[256,3584]{1,0:T(8,128)(2,1)}, bf16[256,512]{1,0:T(8,128)(2,1)}, bf16[256,128]{1,0:T(8,128)(2,1)}) custom-call(s32[1]{0:T(128)} %bitcast.refs_0_, bf16[256,1024]{1,0:T(8,128)(2,1)} %copy-done.21, bf16[256,1024]{1,0:T(8,128)(2,1)} %copy-done.37, bf16[256,128]{1,0:T(8,128)(2,1)} %slice.93.refs_3_, f32[1,1536]{1,0:T(1,128)} %bitcast.100, ...), custom_call_target="tpu_custom_call" | custom-call | flops 22499999744 | bytes 64000000 | tf_op jit(solution)/shard_map/block/pallas_call | solution.py:197
  251.2 38.4 %block.10 = (bf16[256,3584]{1,0:T(8,128)(2,1)}, bf16[512,512]{1,0:T(8,128)(2,1)}, bf16[512,128]{1,0:T(8,128)(2,1)}) custom-call(s32[1]{0:T(128)} %bitcast.refs_0_, bf16[256,1024]{1,0:T(8,128)(2,1)} %copy-done.21, bf16[256,1024]{1,0:T(8,128)(2,1)} %copy-done.37, bf16[256,128]{1,0:T(8,128)(2,1)} %slice.93.refs_3_, bf16[256,1024]{1,0:T(8,128)(2,1)} %copy-done.22, ...), custom_call_target="tpu_custom_call" | custom-call | flops 22499999744 | bytes 64000000 | tf_op jit(solution)/shard_map/block/pallas_call | solution.py:197
  292.3 10.6 down.6.refs_3_
  304.5 54.1 %block.11 = (bf16[512,3584]{1,0:T(8,128)(2,1)}, bf16[512,512]{1,0:T(8,128)(2,1)}, bf16[512,128]{1,0:T(8,128)(2,1)}) custom-call(s32[1]{0:T(128)} %bitcast.refs_0_, bf16[1536,1152]{1,0:T(8,128)(2,1)} %down.5.refs_1_, bf16[512,1152]{1,0:T(8,128)(2,1)} %collective-permute-done.3.refs_2_, bf16[512,1024]{1,0:T(8,128)(2,1)} %collective-permute-done.4.refs_3_, ...), custom_call_target="tpu_custom_call" | custom-call | flops 44999999488 | bytes 64000000 | tf_op jit(solution)/shard_map/block/pallas_call | solution.py:197
  359.2 19.1 %down.7.refs_1_ = bf16[512,2176]{1,0:T(8,128)(2,1)} custom-call(s32[10]{0:T(128)} %stack.103.offs_ref, bf16[16,512,3584]{2,1,0:T(8,128)(2,1)} %h_ref.9, f32[8,512,1]{2,1,0:T(8,128)} %copy.30.rstd_ref, f32[1,3584]{1,0:T(1,128)} %reshape.51.g_ref, bf16[3584,384]{1,0:T(8,128)(2,1)} %rest_0_.7, bf16[3584,384]{1,0:T(8,128)(2,1)} %copy-done.1, ...), custom_call_target="tpu_custom_call" | custom-call | flops 7985954816 | bytes 19267584 | tf_op jit(solution)/shard_map/down/pallas_call | solution.py:57
  380.7 53.9 %block.12 = (bf16[512,3584]{1,0:T(8,128)(2,1)}, bf16[512,512]{1,0:T(8,128)(2,1)}, bf16[512,128]{1,0:T(8,128)(2,1)}) custom-call(s32[1]{0:T(128)} %bitcast.refs_0_, bf16[1536,1152]{1,0:T(8,128)(2,1)} %down.5.refs_1_, bf16[512,1152]{1,0:T(8,128)(2,1)} %collective-permute-done.22.refs_2_, bf16[512,1024]{1,0:T(8,128)(2,1)} %down.6.refs_3_, ...), custom_call_target="tpu_custom_call" | custom-call | flops 44999999488 | bytes 64000000 | tf_op jit(solution)/shard_map/block/pallas_call | solution.py:197
  435.2 19.2 %down.8.refs_1_ = bf16[512,2176]{1,0:T(8,128)(2,1)} custom-call(s32[10]{0:T(128)} %stack.105.offs_ref, bf16[16,512,3584]{2,1,0:T(8,128)(2,1)} %h_ref.9, f32[8,512,1]{2,1,0:T(8,128)} %copy.30.rstd_ref, f32[1,3584]{1,0:T(1,128)} %reshape.51.g_ref, bf16[3584,384]{1,0:T(8,128)(2,1)} %rest_0_.7, bf16[3584,384]{1,0:T(8,128)(2,1)} %copy-done.1, ...), custom_call_target="tpu_custom_call" | custom-call | flops 7985954816 | bytes 19267584 | tf_op jit(solution)/shard_map/down/pallas_call | solution.py:57
  457.3 53.5 %block.13 = (bf16[512,3584]{1,0:T(8,128)(2,1)}, bf16[512,512]{1,0:T(8,128)(2,1)}, bf16[512,128]{1,0:T(8,128)(2,1)}) custom-call(s32[1]{0:T(128)} %bitcast.refs_0_, bf16[512,2176]{1,0:T(8,128)(2,1)} %down.7.refs_1_, bf16[512,2176]{1,0:T(8,128)(2,1)} %copy-done.35, f32[1,1536]{1,0:T(1,128)} %bitcast.104, f32[1,512]{1,0:T(1,128)} %bitcast.113, ...), custom_call_target="tpu_custom_call" | custom-call | flops 44999999488 | bytes 64000000 | tf_op jit(solution)/shard_map/block/pallas_call | solution.py:197
  511.4 37.3 %down.9.refs_1_ = bf16[1536,2176]{1,0:T(8,128)(2,1)} custom-call(s32[10]{0:T(128)} %stack.107.offs_ref, bf16[16,512,3584]{2,1,0:T(8,128)(2,1)} %h_ref.9, f32[8,512,1]{2,1,0:T(8,128)} %copy.30.rstd_ref, f32[1,3584]{1,0:T(1,128)} %reshape.51.g_ref, bf16[3584,384]{1,0:T(8,128)(2,1)} %rest_0_.7, bf16[3584,384]{1,0:T(8,128)(2,1)} %copy-done.1, ...), custom_call_target="tpu_custom_call" | custom-call | flops 23957864448 | bytes 26607616 | tf_op jit(solution)/shard_map/down/pallas_call | solution.py:57
  548.7 5.6 fusion.23
  556.3 53.4 %block.14 = (bf16[512,3584]{1,0:T(8,128)(2,1)}, bf16[512,512]{1,0:T(8,128)(2,1)}, bf16[512,128]{1,0:T(8,128)(2,1)}) custom-call(s32[1]{0:T(128)} %bitcast.refs_0_, bf16[512,2176]{1,0:T(8,128)(2,1)} %down.8.refs_1_, bf16[512,2176]{1,0:T(8,128)(2,1)} %collective-permute-done.27.refs_2_, f32[1,1536]{1,0:T(1,128)} %bitcast.105, f32[1,512]{1,0:T(1,128)} %bitcast.114, ...), custom_call_target="tpu_custom_call" | custom-call | flops 44999999488 | bytes 64000000 | tf_op jit(solution)/shard_map/block/pallas_call | solution.py:197
  610.4 53.8 %block.15 = (bf16[512,3584]{1,0:T(8,128)(2,1)}, bf16[512,512]{1,0:T(8,128)(2,1)}, bf16[512,128]{1,0:T(8,128)(2,1)}) custom-call(s32[1]{0:T(128)} %bitcast.refs_0_, bf16[1536,2176]{1,0:T(8,128)(2,1)} %down.9.refs_1_, bf16[512,2176]{1,0:T(8,128)(2,1)} %collective-permute-done.26.refs_2_, f32[1,1536]{1,0:T(1,128)} %bitcast.106, f32[1,512]{1,0:T(1,128)} %bitcast.115, ...), custom_call_target="tpu_custom_call" | custom-call | flops 44999999488 | bytes 64000000 | tf_op jit(solution)/shard_map/block/pallas_call | solution.py:197
  664.1 53.8 %block.16 = (bf16[512,3584]{1,0:T(8,128)(2,1)}, bf16[512,512]{1,0:T(8,128)(2,1)}, bf16[512,128]{1,0:T(8,128)(2,1)}) custom-call(s32[1]{0:T(128)} %bitcast.refs_0_, bf16[1536,2176]{1,0:T(8,128)(2,1)} %down.9.refs_1_, bf16[512,2176]{1,0:T(8,128)(2,1)} %collective-permute-done.25.refs_2_, f32[1,1536]{1,0:T(1,128)} %bitcast.107, f32[1,512]{1,0:T(1,128)} %bitcast.116, ...), custom_call_target="tpu_custom_call" | custom-call | flops 44999999488 | bytes 64000000 | tf_op jit(solution)/shard_map/block/pallas_call | solution.py:197
  717.9 54.1 %block.17 = (bf16[512,3584]{1,0:T(8,128)(2,1)}, bf16[512,512]{1,0:T(8,128)(2,1)}, bf16[512,128]{1,0:T(8,128)(2,1)}) custom-call(s32[1]{0:T(128)} %bitcast.refs_0_, bf16[1536,2176]{1,0:T(8,128)(2,1)} %down.9.refs_1_, bf16[512,2176]{1,0:T(8,128)(2,1)} %collective-permute-done.24.refs_2_, f32[1,1536]{1,0:T(1,128)} %bitcast.108, f32[1,512]{1,0:T(1,128)} %bitcast.117, ...), custom_call_target="tpu_custom_call" | custom-call | flops 44999999488 | bytes 64000000 | tf_op jit(solution)/shard_map/block/pallas_call | solution.py:197
  772.1 5.2 constant_dynamic-update-slice_fusion.38
  778.4 4.5 constant_dynamic-update-slice_fusion.37
  783.2 3.0 constant_dynamic-update-slice_fusion.36
  786.2 7.6 constant_dynamic-update-slice_fusion.35
  796.3 63.5 %collective-permute-done.33 = bf16[512,3584]{1,0:T(8,128)(2,1)} collective-permute-done((bf16[512,3584]{1,0:T(8,128)(2,1)}, bf16[512,3584]{1,0:T(8,128)(2,1)}, u32[]{:S(2)}, u32[]{:S(2)}) %collective-permute-start.33) | collective-permute-done | bytes 3670048 | tf_op jit(solution)/shard_map/ppermute | solution.py:237
  859.8 7.6 constant_dynamic-update-slice_fusion.33
  868.6 4.1 constant_dynamic-update-slice_fusion.32
  872.7 65.8 %collective-permute-done.35 = bf16[512,3584]{1,0:T(8,128)(2,1)} collective-permute-done((bf16[512,3584]{1,0:T(8,128)(2,1)}, bf16[512,3584]{1,0:T(8,128)(2,1)}, u32[]{:S(2)}, u32[]{:S(2)}) %collective-permute-start.35) | collective-permute-done | bytes 3670048 | tf_op jit(solution)/shard_map/ppermute | solution.py:237
  938.5 8.6 constant_dynamic-update-slice_fusion.31
  948.3 4.1 constant_dynamic-update-slice_fusion.30
  952.4 64.7 %collective-permute-done.37 = bf16[512,3584]{1,0:T(8,128)(2,1)} collective-permute-done((bf16[512,3584]{1,0:T(8,128)(2,1)}, bf16[512,3584]{1,0:T(8,128)(2,1)}, u32[]{:S(2)}, u32[]{:S(2)}) %collective-permute-start.37) | collective-permute-done | bytes 3670048 | tf_op jit(solution)/shard_map/ppermute | solution.py:237
  1017.1 8.6 constant_dynamic-update-slice_fusion.29
  1030.6 4.1 constant_dynamic-update-slice_fusion.28
  1034.7 61.0 %collective-permute-done.39 = bf16[512,3584]{1,0:T(8,128)(2,1)} collective-permute-done((bf16[512,3584]{1,0:T(8,128)(2,1)}, bf16[512,3584]{1,0:T(8,128)(2,1)}, u32[]{:S(2)}, u32[]{:S(2)}) %collective-permute-start.39) | collective-permute-done | bytes 3670048 | tf_op jit(solution)/shard_map/ppermute | solution.py:237
  1095.8 8.6 constant_dynamic-update-slice_fusion.27
  1106.2 3.5 slice.83
  1113.1 4.3 constant_dynamic-update-slice_fusion.26
  1117.4 57.0 %collective-permute-done.41 = bf16[512,3584]{1,0:T(8,128)(2,1)} collective-permute-done((bf16[512,3584]{1,0:T(8,128)(2,1)}, bf16[512,3584]{1,0:T(8,128)(2,1)}, u32[]{:S(2)}, u32[]{:S(2)}) %collective-permute-start.41) | collective-permute-done | bytes 3670048 | tf_op jit(solution)/shard_map/ppermute | solution.py:237
  1174.4 7.8 constant_dynamic-update-slice_fusion.25
  1182.6 4.3 constant_dynamic-update-slice_fusion.24
  1186.9 46.0 %collective-permute-done.43 = bf16[384,3584]{1,0:T(8,128)(2,1)} collective-permute-done((bf16[384,3584]{1,0:T(8,128)(2,1)}, bf16[384,3584]{1,0:T(8,128)(2,1)}, u32[]{:S(2)}, u32[]{:S(2)}) %collective-permute-start.43) | collective-permute-done | bytes 2752544 | tf_op jit(solution)/shard_map/ppermute | solution.py:237
  1232.9 6.0 constant_dynamic-update-slice_fusion.23
  1252.1 4.1 constant_dynamic-update-slice_fusion.22
  1256.2 7.5 collective-permute-done.45
  1263.7 3.0 constant_dynamic-update-slice_fusion.21
  1272.4 3.5 constant_dynamic-update-slice_fusion.20
  (237 shorter events, 98.8 us)
Async XLA Ops:
  0.6 215.5 %collective-permute-start.14 = (bf16[16,128,3584]{2,1,0:T(8,128)(2,1)}, bf16[16,128,3584]{2,1,0:T(8,128)(2,1)}, u32[]{:S(2)}, u32[]{:S(2)}) collective-permute-start(bf16[16,128,3584]{2,1,0:T(8,128)(2,1)} %param.21), channel_id=1, source_target_pairs={{0,1},{1,0},{2,3},{3,2},{4,5},{5,4},{6,7},{7,6}} | collective-permute-start | bytes 44040200 | tf_op jit(solution)/shard_map/ppermute | solution.py:234
  1.5 101.6 %collective-permute-start.10 = (bf16[1536,16,192]{0,2,1:T(8,128)(2,1)}, bf16[1536,16,192]{0,2,1:T(8,128)(2,1)}, u32[]{:S(2)}, u32[]{:S(2)}) collective-permute-start(bf16[1536,16,192]{0,2,1:T(8,128)(2,1)} %param.18), channel_id=1, source_target_pairs={{0,1},{1,0},{2,3},{3,2},{4,5},{5,4},{6,7},{7,6}} | collective-permute-start | bytes 28311560 | tf_op jit(solution)/shard_map/ppermute | solution.py:234
  1.5 41.2 %collective-permute-start.1 = (bf16[3584,384]{1,0:T(8,128)(2,1)}, bf16[3584,384]{1,0:T(8,128)(2,1)S(1)}, u32[]{:S(2)}, u32[]{:S(2)}) collective-permute-start(bf16[3584,384]{1,0:T(8,128)(2,1)} %rest_0_.7), channel_id=1, source_target_pairs={{0,1},{1,0},{2,3},{3,2},{4,5},{5,4},{6,7},{7,6}} | collective-permute-start | bytes 8257544 | tf_op jit(solution)/shard_map/ppermute | solution.py:234
  12.4 9.6 collective-permute-start
  15.0 27.4 %collective-permute-start.2 = (bf16[3584,128]{1,0:T(8,128)(2,1)}, bf16[3584,128]{1,0:T(8,128)(2,1)}, u32[]{:S(2)}, u32[]{:S(2)}) collective-permute-start(bf16[3584,128]{1,0:T(8,128)(2,1)} %rest_4_.5), channel_id=1, source_target_pairs={{0,1},{1,0},{2,3},{3,2},{4,5},{5,4},{6,7},{7,6}} | collective-permute-start | bytes 2752520 | tf_op jit(solution)/shard_map/ppermute | solution.py:234
  22.0 80.5 %collective-permute-start.11 = (bf16[512,16,128]{2,1,0:T(8,128)(2,1)}, bf16[512,16,128]{2,1,0:T(8,128)(2,1)}, u32[]{:S(2)}, u32[]{:S(2)}) collective-permute-start(bf16[512,16,128]{2,1,0:T(8,128)(2,1)} %param.19), channel_id=1, source_target_pairs={{0,1},{1,0},{2,3},{3,2},{4,5},{5,4},{6,7},{7,6}} | collective-permute-start | bytes 6291464 | tf_op jit(solution)/shard_map/ppermute | solution.py:234
  42.4 60.8 %collective-permute-start.12 = (bf16[512,16,128]{2,1,0:T(8,128)(2,1)}, bf16[512,16,128]{2,1,0:T(8,128)(2,1)}, u32[]{:S(2)}, u32[]{:S(2)}) collective-permute-start(bf16[512,16,128]{2,1,0:T(8,128)(2,1)} %param.20), channel_id=1, source_target_pairs={{0,1},{1,0},{2,3},{3,2},{4,5},{5,4},{6,7},{7,6}} | collective-permute-start | bytes 6291464 | tf_op jit(solution)/shard_map/ppermute | solution.py:234
  69.1 16.8 %collective-permute-start.5 = (bf16[256,1152]{1,0:T(8,128)(2,1)}, bf16[256,1152]{1,0:T(8,128)(2,1)}, u32[]{:S(2)}, u32[]{:S(2)}) collective-permute-start(bf16[256,1152]{1,0:T(8,128)(2,1)} %get-tuple-element.142), channel_id=1, source_target_pairs={{0,4},{4,0},{1,5},{5,1},{2,6},{6,2},{3,7},{7,3}} | collective-permute-start | bytes 1769480 | tf_op jit(solution)/shard_map/ppermute | solution.py:240
  85.9 15.2 %collective-permute-start.16 = (bf16[256,1152]{1,0:T(8,128)(2,1)}, bf16[256,1152]{1,0:T(8,128)(2,1)S(1)}, u32[]{:S(2)}, u32[]{:S(2)}) collective-permute-start(bf16[256,1152]{1,0:T(8,128)(2,1)} %get-tuple-element.141), channel_id=1, source_target_pairs={{0,4},{4,0},{1,5},{5,1},{2,6},{6,2},{3,7},{7,3}} | collective-permute-start | bytes 1769480 | tf_op jit(solution)/shard_map/ppermute | solution.py:240
  101.1 64.1 %collective-permute-start.9 = (bf16[3584,384]{1,0:T(8,128)(2,1)S(1)}, bf16[3584,384]{1,0:T(8,128)(2,1)}, u32[]{:S(2)}, u32[]{:S(2)}) collective-permute-start(bf16[3584,384]{1,0:T(8,128)(2,1)S(1)} %copy-done), channel_id=1, source_target_pairs={{0,2},{2,0},{1,3},{3,1},{4,6},{6,4},{5,7},{7,5}} | collective-permute-start | bytes 8257544 | tf_op jit(solution)/shard_map/ppermute | solution.py:237
  102.5 61.2 %collective-permute-start.8 = (bf16[1,512]{1,0:T(2,128)(2,1)S(1)}, bf16[1,512]{1,0:T(2,128)(2,1)S(1)}, u32[]{:S(2)}, u32[]{:S(2)}) collective-permute-start(bf16[1,512]{1,0:T(2,128)(2,1)S(1)} %broadcast_in_dim.50), channel_id=1, source_target_pairs={{0,2},{2,0},{1,3},{3,1},{4,6},{6,4},{5,7},{7,5}} | collective-permute-start | bytes 3080 | tf_op jit(solution)/shard_map/ppermute | solution.py:237
  103.1 63.7 %collective-permute-start.7 = (bf16[1,512]{1,0:T(2,128)(2,1)S(1)}, bf16[1,512]{1,0:T(2,128)(2,1)S(1)}, u32[]{:S(2)}, u32[]{:S(2)}) collective-permute-start(bf16[1,512]{1,0:T(2,128)(2,1)S(1)} %broadcast_in_dim.50), channel_id=1, source_target_pairs={{0,1},{1,0},{2,3},{3,2},{4,5},{5,4},{6,7},{7,6}} | collective-permute-start | bytes 3080 | tf_op jit(solution)/shard_map/ppermute | solution.py:234
  103.1 145.8 %collective-permute-start.19 = (bf16[3584,128]{1,0:T(8,128)(2,1)}, bf16[3584,128]{1,0:T(8,128)(2,1)}, u32[]{:S(2)}, u32[]{:S(2)}) collective-permute-start(bf16[3584,128]{1,0:T(8,128)(2,1)} %rest_4_.5), channel_id=1, source_target_pairs={{0,2},{2,0},{1,3},{3,1},{4,6},{6,4},{5,7},{7,5}} | collective-permute-start | bytes 2752520 | tf_op jit(solution)/shard_map/ppermute | solution.py:237
  163.7 86.7 %collective-permute-start.4 = (bf16[512,1024]{1,0:T(8,128)(2,1)}, bf16[512,1024]{1,0:T(8,128)(2,1)}, u32[]{:S(2)}, u32[]{:S(2)}) collective-permute-start(bf16[512,1024]{1,0:T(8,128)(2,1)} %slice.90), channel_id=1, source_target_pairs={{0,2},{2,0},{1,3},{3,1},{4,6},{6,4},{5,7},{7,5}} | collective-permute-start | bytes 3145736 | tf_op jit(solution)/shard_map/ppermute | solution.py:237
  166.8 136.1 %collective-permute-start.3 = (bf16[512,1152]{1,0:T(8,128)(2,1)}, bf16[512,1152]{1,0:T(8,128)(2,1)}, u32[]{:S(2)}, u32[]{:S(2)}) collective-permute-start(bf16[512,1152]{1,0:T(8,128)(2,1)} %get-tuple-element.140), channel_id=1, source_target_pairs={{0,4},{4,0},{1,5},{5,1},{2,6},{6,2},{3,7},{7,3}} | collective-permute-start | bytes 3538952 | tf_op jit(solution)/shard_map/ppermute | solution.py:240
  168.3 46.6 %collective-permute-start.6 = (bf16[256,1024]{1,0:T(8,128)(2,1)S(1)}, bf16[256,1024]{1,0:T(8,128)(2,1)S(1)}, u32[]{:S(2)}, u32[]{:S(2)}) collective-permute-start(bf16[256,1024]{1,0:T(8,128)(2,1)S(1)} %slice.92.refs_1_), channel_id=1, source_target_pairs={{0,2},{2,0},{1,3},{3,1},{4,6},{6,4},{5,7},{7,5}} | collective-permute-start | bytes 1572872 | tf_op jit(solution)/shard_map/ppermute | solution.py:237
  215.0 35.7 %collective-permute-start.17 = (bf16[256,1024]{1,0:T(8,128)(2,1)S(1)}, bf16[256,1024]{1,0:T(8,128)(2,1)}, u32[]{:S(2)}, u32[]{:S(2)}) collective-permute-start(bf16[256,1024]{1,0:T(8,128)(2,1)S(1)} %slice.96.refs_4_), channel_id=1, source_target_pairs={{0,2},{2,0},{1,3},{3,1},{4,6},{6,4},{5,7},{7,5}} | collective-permute-start | bytes 1572872 | tf_op jit(solution)/shard_map/ppermute | solution.py:237
  216.1 74.1 %collective-permute-start.18 = (bf16[3584,384]{1,0:T(8,128)(2,1)}, bf16[3584,384]{1,0:T(8,128)(2,1)S(1)}, u32[]{:S(2)}, u32[]{:S(2)}) collective-permute-start(bf16[3584,384]{1,0:T(8,128)(2,1)} %collective-permute-done.9.rest_0_.rest_2_), channel_id=1, source_target_pairs={{0,1},{1,0},{2,3},{3,2},{4,5},{5,4},{6,7},{7,6}} | collective-permute-start | bytes 8257544 | tf_op jit(solution)/shard_map/ppermute | solution.py:234
  248.9 129.9 %collective-permute-start.22 = (bf16[512,1152]{1,0:T(8,128)(2,1)}, bf16[512,1152]{1,0:T(8,128)(2,1)}, u32[]{:S(2)}, u32[]{:S(2)}) collective-permute-start(bf16[512,1152]{1,0:T(8,128)(2,1)} %get-tuple-element.139), channel_id=1, source_target_pairs={{0,4},{4,0},{1,5},{5,1},{2,6},{6,2},{3,7},{7,3}} | collective-permute-start | bytes 3538952 | tf_op jit(solution)/shard_map/ppermute | solution.py:240
  250.4 40.7 %collective-permute-start.20 = (bf16[3584,128]{1,0:T(8,128)(2,1)}, bf16[3584,128]{1,0:T(8,128)(2,1)}, u32[]{:S(2)}, u32[]{:S(2)}) collective-permute-start(bf16[3584,128]{1,0:T(8,128)(2,1)} %collective-permute-done.19.rest_2_.rest_6_), channel_id=1, source_target_pairs={{0,1},{1,0},{2,3},{3,2},{4,5},{5,4},{6,7},{7,6}} | collective-permute-start | bytes 2752520 | tf_op jit(solution)/shard_map/ppermute | solution.py:234
  250.7 53.8 %collective-permute-start.15 = (bf16[512,1024]{1,0:T(8,128)(2,1)}, bf16[512,1024]{1,0:T(8,128)(2,1)}, u32[]{:S(2)}, u32[]{:S(2)}) collective-permute-start(bf16[512,1024]{1,0:T(8,128)(2,1)} %collective-permute-done.4.refs_3_), channel_id=1, source_target_pairs={{0,4},{4,0},{1,5},{5,1},{2,6},{6,2},{3,7},{7,3}} | collective-permute-start | bytes 3145736 | tf_op jit(solution)/shard_map/ppermute | solution.py:240
  290.3 481.8 %collective-permute-start.28 = (bf16[256,3584]{1,0:T(8,128)(2,1)}, bf16[256,3584]{1,0:T(8,128)(2,1)}, u32[]{:S(2)}, u32[]{:S(2)}) collective-permute-start(bf16[256,3584]{1,0:T(8,128)(2,1)} %get-tuple-element.63), channel_id=1, source_target_pairs={{0,2},{2,0},{1,3},{3,1},{4,6},{6,4},{5,7},{7,5}} | collective-permute-start | bytes 5505032 | tf_op jit(solution)/shard_map/ppermute | solution.py:237
  291.1 487.3 %collective-permute-start.29 = (bf16[256,3584]{1,0:T(8,128)(2,1)}, bf16[256,3584]{1,0:T(8,128)(2,1)}, u32[]{:S(2)}, u32[]{:S(2)}) collective-permute-start(bf16[256,3584]{1,0:T(8,128)(2,1)} %get-tuple-element.67), channel_id=1, source_target_pairs={{0,2},{2,0},{1,3},{3,1},{4,6},{6,4},{5,7},{7,5}} | collective-permute-start | bytes 5505032 | tf_op jit(solution)/shard_map/ppermute | solution.py:237
  302.9 76.8 %collective-permute-start.23 = (bf16[512,1024]{1,0:T(8,128)(2,1)}, bf16[512,1024]{1,0:T(8,128)(2,1)S(1)}, u32[]{:S(2)}, u32[]{:S(2)}) collective-permute-start(bf16[512,1024]{1,0:T(8,128)(2,1)} %down.6.refs_3_), channel_id=1, source_target_pairs={{0,4},{4,0},{1,5},{5,1},{2,6},{6,2},{3,7},{7,3}} | collective-permute-start | bytes 3145736 | tf_op jit(solution)/shard_map/ppermute | solution.py:240
  378.3 77.6 %collective-permute-start.21 = (bf16[512,2176]{1,0:T(8,128)(2,1)}, bf16[512,2176]{1,0:T(8,128)(2,1)S(1)}, u32[]{:S(2)}, u32[]{:S(2)}) collective-permute-start(bf16[512,2176]{1,0:T(8,128)(2,1)} %down.7.refs_1_), channel_id=1, source_target_pairs={{0,4},{4,0},{1,5},{5,1},{2,6},{6,2},{3,7},{7,3}} | collective-permute-start | bytes 6684680 | tf_op jit(solution)/shard_map/ppermute | solution.py:240
  378.8 407.4 %collective-permute-start.31 = (bf16[512,3584]{1,0:T(8,128)(2,1)}, bf16[512,3584]{1,0:T(8,128)(2,1)}, u32[]{:S(2)}, u32[]{:S(2)}) collective-permute-start(bf16[512,3584]{1,0:T(8,128)(2,1)} %get-tuple-element.72), channel_id=1, source_target_pairs={{0,2},{2,0},{1,3},{3,1},{4,6},{6,4},{5,7},{7,5}} | collective-permute-start | bytes 11010056 | tf_op jit(solution)/shard_map/ppermute | solution.py:237
  454.5 100.4 %collective-permute-start.27 = (bf16[512,2176]{1,0:T(8,128)(2,1)}, bf16[512,2176]{1,0:T(8,128)(2,1)}, u32[]{:S(2)}, u32[]{:S(2)}) collective-permute-start(bf16[512,2176]{1,0:T(8,128)(2,1)} %down.8.refs_1_), channel_id=1, source_target_pairs={{0,4},{4,0},{1,5},{5,1},{2,6},{6,2},{3,7},{7,3}} | collective-permute-start | bytes 6684680 | tf_op jit(solution)/shard_map/ppermute | solution.py:240
  554.3 55.5 %collective-permute-start.26 = (bf16[512,2176]{1,0:T(8,128)(2,1)}, bf16[512,2176]{1,0:T(8,128)(2,1)}, u32[]{:S(2)}, u32[]{:S(2)}) collective-permute-start(bf16[512,2176]{1,0:T(8,128)(2,1)} %get-tuple-element.134), channel_id=1, source_target_pairs={{0,4},{4,0},{1,5},{5,1},{2,6},{6,2},{3,7},{7,3}} | collective-permute-start | bytes 6684680 | tf_op jit(solution)/shard_map/ppermute | solution.py:240
  554.9 109.3 %collective-permute-start.25 = (bf16[512,2176]{1,0:T(8,128)(2,1)}, bf16[512,2176]{1,0:T(8,128)(2,1)}, u32[]{:S(2)}, u32[]{:S(2)}) collective-permute-start(bf16[512,2176]{1,0:T(8,128)(2,1)} %get-tuple-element.135), channel_id=1, source_target_pairs={{0,4},{4,0},{1,5},{5,1},{2,6},{6,2},{3,7},{7,3}} | collective-permute-start | bytes 6684680 | tf_op jit(solution)/shard_map/ppermute | solution.py:240
  609.8 108.2 %collective-permute-start.24 = (bf16[512,2176]{1,0:T(8,128)(2,1)S(1)}, bf16[512,2176]{1,0:T(8,128)(2,1)}, u32[]{:S(2)}, u32[]{:S(2)}) collective-permute-start(bf16[512,2176]{1,0:T(8,128)(2,1)S(1)} %get-tuple-element.136), channel_id=1, source_target_pairs={{0,4},{4,0},{1,5},{5,1},{2,6},{6,2},{3,7},{7,3}} | collective-permute-start | bytes 6684680 | tf_op jit(solution)/shard_map/ppermute | solution.py:240
  777.3 82.5 %collective-permute-start.33 = (bf16[512,3584]{1,0:T(8,128)(2,1)}, bf16[512,3584]{1,0:T(8,128)(2,1)}, u32[]{:S(2)}, u32[]{:S(2)}) collective-permute-start(bf16[512,3584]{1,0:T(8,128)(2,1)} %get-tuple-element.75), channel_id=1, source_target_pairs={{0,2},{2,0},{1,3},{3,1},{4,6},{6,4},{5,7},{7,5}} | collective-permute-start | bytes 11010056 | tf_op jit(solution)/shard_map/ppermute | solution.py:237
  783.0 12.0 collective-permute-start.32
  793.8 74.8 %collective-permute-start.34 = (bf16[1,512,3584]{2,1,0:T(8,128)(2,1)}, bf16[1,512,3584]{2,1,0:T(8,128)(2,1)}, u32[]{:S(2)}, u32[]{:S(2)}) collective-permute-start(bf16[1,512,3584]{2,1,0:T(8,128)(2,1)} %get-tuple-element.129), channel_id=1, source_target_pairs={{0,1},{1,0},{2,3},{3,2},{4,5},{5,4},{6,7},{7,6}} | collective-permute-start | bytes 11010056 | tf_op jit(solution)/shard_map/ppermute | solution.py:234
  794.1 144.4 %collective-permute-start.35 = (bf16[512,3584]{1,0:T(8,128)(2,1)}, bf16[512,3584]{1,0:T(8,128)(2,1)}, u32[]{:S(2)}, u32[]{:S(2)}) collective-permute-start(bf16[512,3584]{1,0:T(8,128)(2,1)} %get-tuple-element.78), channel_id=1, source_target_pairs={{0,2},{2,0},{1,3},{3,1},{4,6},{6,4},{5,7},{7,5}} | collective-permute-start | bytes 11010056 | tf_op jit(solution)/shard_map/ppermute | solution.py:237
  867.4 80.8 %collective-permute-start.36 = (bf16[1,512,3584]{2,1,0:T(8,128)(2,1)}, bf16[1,512,3584]{2,1,0:T(8,128)(2,1)}, u32[]{:S(2)}, u32[]{:S(2)}) collective-permute-start(bf16[1,512,3584]{2,1,0:T(8,128)(2,1)} %get-tuple-element.127), channel_id=1, source_target_pairs={{0,1},{1,0},{2,3},{3,2},{4,5},{5,4},{6,7},{7,6}} | collective-permute-start | bytes 11010056 | tf_op jit(solution)/shard_map/ppermute | solution.py:234
  867.4 149.7 %collective-permute-start.37 = (bf16[512,3584]{1,0:T(8,128)(2,1)}, bf16[512,3584]{1,0:T(8,128)(2,1)}, u32[]{:S(2)}, u32[]{:S(2)}) collective-permute-start(bf16[512,3584]{1,0:T(8,128)(2,1)} %get-tuple-element.81), channel_id=1, source_target_pairs={{0,2},{2,0},{1,3},{3,1},{4,6},{6,4},{5,7},{7,5}} | collective-permute-start | bytes 11010056 | tf_op jit(solution)/shard_map/ppermute | solution.py:237
  947.1 83.5 %collective-permute-start.38 = (bf16[1,512,3584]{2,1,0:T(8,128)(2,1)}, bf16[1,512,3584]{2,1,0:T(8,128)(2,1)}, u32[]{:S(2)}, u32[]{:S(2)}) collective-permute-start(bf16[1,512,3584]{2,1,0:T(8,128)(2,1)} %get-tuple-element.125), channel_id=1, source_target_pairs={{0,1},{1,0},{2,3},{3,2},{4,5},{5,4},{6,7},{7,6}} | collective-permute-start | bytes 11010056 | tf_op jit(solution)/shard_map/ppermute | solution.py:234
  947.1 148.7 %collective-permute-start.39 = (bf16[512,3584]{1,0:T(8,128)(2,1)}, bf16[512,3584]{1,0:T(8,128)(2,1)}, u32[]{:S(2)}, u32[]{:S(2)}) collective-permute-start(bf16[512,3584]{1,0:T(8,128)(2,1)} %get-tuple-element.83), channel_id=1, source_target_pairs={{0,2},{2,0},{1,3},{3,1},{4,6},{6,4},{5,7},{7,5}} | collective-permute-start | bytes 11010056 | tf_op jit(solution)/shard_map/ppermute | solution.py:237
  1025.8 87.3 %collective-permute-start.40 = (bf16[1,512,3584]{2,1,0:T(8,128)(2,1)}, bf16[1,512,3584]{2,1,0:T(8,128)(2,1)}, u32[]{:S(2)}, u32[]{:S(2)}) collective-permute-start(bf16[1,512,3584]{2,1,0:T(8,128)(2,1)} %get-tuple-element.123), channel_id=1, source_target_pairs={{0,1},{1,0},{2,3},{3,2},{4,5},{5,4},{6,7},{7,6}} | collective-permute-start | bytes 11010056 | tf_op jit(solution)/shard_map/ppermute | solution.py:234
  1027.7 146.7 %collective-permute-start.41 = (bf16[512,3584]{1,0:T(8,128)(2,1)}, bf16[512,3584]{1,0:T(8,128)(2,1)}, u32[]{:S(2)}, u32[]{:S(2)}) collective-permute-start(bf16[512,3584]{1,0:T(8,128)(2,1)} %get-tuple-element.85), channel_id=1, source_target_pairs={{0,2},{2,0},{1,3},{3,1},{4,6},{6,4},{5,7},{7,5}} | collective-permute-start | bytes 11010056 | tf_op jit(solution)/shard_map/ppermute | solution.py:237
  1104.4 78.2 %collective-permute-start.42 = (bf16[1,512,3584]{2,1,0:T(8,128)(2,1)}, bf16[1,512,3584]{2,1,0:T(8,128)(2,1)}, u32[]{:S(2)}, u32[]{:S(2)}) collective-permute-start(bf16[1,512,3584]{2,1,0:T(8,128)(2,1)} %get-tuple-element.121), channel_id=1, source_target_pairs={{0,1},{1,0},{2,3},{3,2},{4,5},{5,4},{6,7},{7,6}} | collective-permute-start | bytes 11010056 | tf_op jit(solution)/shard_map/ppermute | solution.py:234
  1111.8 121.1 %collective-permute-start.43 = (bf16[384,3584]{1,0:T(8,128)(2,1)}, bf16[384,3584]{1,0:T(8,128)(2,1)}, u32[]{:S(2)}, u32[]{:S(2)}) collective-permute-start(bf16[384,3584]{1,0:T(8,128)(2,1)} %slice.83), channel_id=1, source_target_pairs={{0,2},{2,0},{1,3},{3,1},{4,6},{6,4},{5,7},{7,5}} | collective-permute-start | bytes 8257544 | tf_op jit(solution)/shard_map/ppermute | solution.py:237
  1182.2 68.5 %collective-permute-start.44 = (bf16[1,512,3584]{2,1,0:T(8,128)(2,1)}, bf16[1,512,3584]{2,1,0:T(8,128)(2,1)}, u32[]{:S(2)}, u32[]{:S(2)}) collective-permute-start(bf16[1,512,3584]{2,1,0:T(8,128)(2,1)} %get-tuple-element.119), channel_id=1, source_target_pairs={{0,1},{1,0},{2,3},{3,2},{4,5},{5,4},{6,7},{7,6}} | collective-permute-start | bytes 11010056 | tf_op jit(solution)/shard_map/ppermute | solution.py:234
  1239.0 33.4 %collective-permute-start.46 = (bf16[1,384,3584]{2,1,0:T(8,128)(2,1)}, bf16[1,384,3584]{2,1,0:T(8,128)(2,1)}, u32[]{:S(2)}, u32[]{:S(2)}) collective-permute-start(bf16[1,384,3584]{2,1,0:T(8,128)(2,1)} %get-tuple-element.117), channel_id=1, source_target_pairs={{0,1},{1,0},{2,3},{3,2},{4,5},{5,4},{6,7},{7,6}} | collective-permute-start | bytes 8257544 | tf_op jit(solution)/shard_map/ppermute | solution.py:234
  1240.7 26.1 %collective-permute-start.49 = (bf16[8,512,64]{1,2,0:T(8,128)(2,1)}, bf16[8,512,64]{1,2,0:T(8,128)(2,1)}, u32[]{:S(2)}, u32[]{:S(2)}) collective-permute-start(bf16[8,512,64]{1,2,0:T(8,128)(2,1)} %copy.35), channel_id=1, source_target_pairs={{0,1},{1,0},{2,3},{3,2},{4,5},{5,4},{6,7},{7,6}} | collective-permute-start | bytes 1572872 | tf_op jit(solution)/shard_map/ppermute | solution.py:234
  1241.2 22.5 %collective-permute-start.45 = (bf16[128,3584]{1,0:T(8,128)(2,1)}, bf16[128,3584]{1,0:T(8,128)(2,1)S(1)}, u32[]{:S(2)}, u32[]{:S(2)}) collective-permute-start(bf16[128,3584]{1,0:T(8,128)(2,1)} %slice.84), channel_id=1, source_target_pairs={{0,2},{2,0},{1,3},{3,1},{4,6},{6,4},{5,7},{7,5}} | collective-permute-start | bytes 2752520 | tf_op jit(solution)/shard_map/ppermute | solution.py:237
  1250.7 19.4 %collective-permute-start.48 = (bf16[8,512,128]{2,1,0:T(8,128)(2,1)}, bf16[8,512,128]{2,1,0:T(8,128)(2,1)}, u32[]{:S(2)}, u32[]{:S(2)}) collective-permute-start(bf16[8,512,128]{2,1,0:T(8,128)(2,1)} %get-tuple-element.137), channel_id=1, source_target_pairs={{0,1},{1,0},{2,3},{3,2},{4,5},{5,4},{6,7},{7,6}} | collective-permute-start | bytes 3145736 | tf_op jit(solution)/shard_map/ppermute | solution.py:234
  1266.7 9.2 collective-permute-start.47
  (43 other events, 884.6 us)
